TPU v7x, 256 devices: a whole 4x4x8 slice. The times are simulated.
256 devices in a mesh: dp: 4 (over x), vocab: 64 (over y, z, core).
Axes of the slice: x: 4, y: 4, z: 8, core: 2. Of those that a mesh axis runs over, the one named last changes fastest.
Arguments:
- final_activation: bfloat16 [512, 8192], P('dp', 'vocab'), may hold values from -2000 to 2000
- output_projection_weights: bfloat16 [8192, 128256], P('dp', 'vocab'), may hold values from -0.0625 to 0.0625
- context_word_tallies: int32 [512, 128256], P('dp', 'vocab'), may hold values from 0 to 2
- emitted_word_tallies: int32 [512, 128256], P('dp', 'vocab'), may hold values from 0 to 2
- freshest_word: int32 [512], P('dp'), may hold values from 0 to 128255
- recurrence_divisor: float32 [512], P('dp'), may hold values from 1.1 to 2.5
- recurrence_fine: float32 [512], P('dp'), may hold values from 0 to 1.5
- appearance_fine: float32 [512], P('dp'), may hold values from 0 to 1.5
- softness_level: float32 [512], P('dp'), may hold values from 0.5 to 2
- random_draws: float32 [512], P('dp'), may hold values from 0.02 to 0.98
Outputs:
- new_counts: int32 [512, 128256], P('dp', 'vocab')
- log_likelihoods: float32 [512, 128256], P('dp', 'vocab')
- sample_quantile: float32 [512], P('dp')
All inputs are finite; a program needn't handle non-finite values.
Results may differ from a plain program's by a relative error of at most 0.0012.
Values may be sent and summed in bfloat16 or wider, within the bound.
No kernel may reach another device: no remote copies, remote signals or barrier semaphores. Data moves between devices by JAX's collectives and lax.ppermute only.
A program may use at most 128 MiB of HBM per device.

v0:
```python
import jax
import jax.numpy as jnp
from jax import lax
from jax.sharding import PartitionSpec as P

VOCAB = 128256


def copy_for_each(value, axis):
    copies = jnp.broadcast_to(value, (lax.axis_size(axis), *value.shape))
    return lax.all_to_all(copies, axis, split_axis=0, concat_axis=0, tiled=True)


def laid_out(pieces, dim):
    pieces = jnp.moveaxis(pieces, 0, dim)
    lengths = pieces.shape
    return pieces.reshape(*lengths[:dim], lengths[dim] * lengths[dim + 1], *lengths[dim + 2 :])


def gathered_copies(value, axis, dim):
    pieces = copy_for_each(value, axis)
    return laid_out(pieces, dim)


def split_up(value, dim, peers):
    lengths = value.shape
    pieces = value.reshape(*lengths[:dim], peers, lengths[dim] // peers, *lengths[dim + 1 :])
    return jnp.moveaxis(pieces, dim, 0)


def sum_at_owner(value, axis, dim):
    pieces = split_up(value, dim, lax.axis_size(axis))
    arrived = lax.all_to_all(pieces, axis, split_axis=0, concat_axis=0, tiled=True)
    return arrived.sum(axis=0)


def taken_together(value, axis):
    everything = copy_for_each(value, axis)
    return jnp.max(everything, axis=0)


def taken_together_2(value, axis):
    everything = copy_for_each(value, axis)
    return jnp.sum(everything, axis=0)


def joined_by_halves(pieces, combine):
    while len(jax.tree.leaves(pieces)[0]) > 1:
        pieces = jax.vmap(combine)(*(pieces[side::2] for side in (0, 1)))
    return pieces[0]


def prefix(value, axis, combine, identity):
    peers, index = (lax.axis_size(axis), lax.axis_index(axis))
    passed = jnp.arange(peers) < index

    def kept(part, zero, own):
        part = jnp.where(
            passed.reshape(-1, *(1 for _ in own.shape)), part, jnp.asarray(zero, own.dtype)
        )
        return part

    pieces = copy_for_each(value, axis)
    return joined_by_halves(kept(pieces, identity, value), combine)


def on_device(
    final_activation,
    output_projection_weights,
    context_word_tallies,
    emitted_word_tallies,
    freshest_word,
    recurrence_divisor,
    recurrence_fine,
    appearance_fine,
    softness_level,
    random_draws,
):
    full_rows = gathered_copies(final_activation, "vocab", 1)
    shard_width = output_projection_weights.shape[1]
    first_id = lax.axis_index("vocab") * shard_width
    token_ids = first_id + lax.broadcasted_iota(jnp.int32, (1, shard_width), 1)
    new_counts = emitted_word_tallies + (token_ids == freshest_word[:, None]).astype(jnp.int32)
    seen = context_word_tallies + new_counts > 0
    quarter_rows = lax.all_to_all(full_rows, "dp", split_axis=1, concat_axis=0, tiled=True)
    logits = sum_at_owner(
        jnp.dot(quarter_rows, output_projection_weights, preferred_element_type=jnp.float32),
        "dp",
        0,
    )
    factor = recurrence_divisor[:, None]
    adjusted_scores = jnp.where(
        seen, jnp.where(logits > 0, logits / factor, logits * factor), logits
    )
    adjusted_scores = adjusted_scores - recurrence_fine[:, None] * new_counts.astype(jnp.float32)
    adjusted_scores = adjusted_scores - appearance_fine[:, None] * (new_counts > 0).astype(
        jnp.float32
    )
    softened_scores = adjusted_scores / softness_level[:, None]
    highest_score = taken_together(jnp.max(softened_scores, axis=1), "vocab")
    exponentiated_mass = jnp.exp(softened_scores - highest_score[:, None])
    local_sum = jnp.sum(exponentiated_mass, axis=1)
    normalizer_mass = taken_together_2(local_sum, "vocab")

    def plus(earlier, later):
        return earlier + later

    lower_mass = prefix(local_sum, "vocab", plus, jnp.zeros_like(local_sum))
    log_likelihoods = softened_scores - highest_score[:, None] - jnp.log(normalizer_mass)[:, None]
    probs = exponentiated_mass / normalizer_mass[:, None]
    cdf = (lower_mass / normalizer_mass)[:, None] + jnp.cumsum(probs, axis=1)
    below = cdf - probs
    taken = jnp.minimum(jnp.maximum(random_draws[:, None] - below, 0.0), probs)
    position = (token_ids.astype(jnp.float32) + 0.5) / VOCAB
    partial_quantile = jnp.sum(taken * position, axis=1)
    sample_quantile = taken_together_2(partial_quantile, "vocab")
    return (new_counts, log_likelihoods, sample_quantile)


def solution(mesh):
    return jax.shard_map(
        on_device,
        mesh=mesh,
        in_specs=(
            P("dp", "vocab"),
            P("dp", "vocab"),
            P("dp", "vocab"),
            P("dp", "vocab"),
            P("dp"),
            P("dp"),
            P("dp"),
            P("dp"),
            P("dp"),
            P("dp"),
        ),
        out_specs=(P("dp", "vocab"), P("dp", "vocab"), P("dp")),
        check_vma=False,
    )
```

profile of v0, /device:TPU:1, one launch (start us, length us, event | category | flops | bytes accessed | tf_op | source)
XLA Modules:
  0.0 214.0 jit_solution(15038913976641535471)
XLA Ops:
  0.6 0.9 copy.26
  1.5 0.5 broadcast_in_dim.20
  2.0 64.1 %all_to_all.48 = bf16[64,128,128]{1,2,0:T(8,128)(2,1)S(1)} all-to-all(bf16[64,128,128]{1,2,0:T(8,128)(2,1)S(1)} %broadcast_in_dim.20), channel_id=1, replica_groups=mesh['dp'=4,'vocab'=64] {'vocab'}, dimensions={0} | all-to-all | bytes 4194304 | tf_op jit(solution)/shard_map/all_to_all | solution.py:11
  66.2 2.7 %copy.27 = bf16[128,4,2048]{2,0,1:T(8,128)(2,1)} copy(bf16[128,4,2048]{0,2,1:T(8,128)(2,1)S(1)} %bitcast.18) | data formatting | bytes 4194304 | tf_op jit(solution)/shard_map/all_to_all | solution.py:85
  68.8 29.5 %all_to_all.49 = bf16[128,4,2048]{2,0,1:T(8,128)(2,1)S(1)} all-to-all(bf16[128,4,2048]{2,0,1:T(8,128)(2,1)} %copy.27), channel_id=1, replica_groups=mesh['dp'=4,'vocab'=64] {'dp'}, dimensions={1} | all-to-all | bytes 4194304 | tf_op jit(solution)/shard_map/all_to_all | solution.py:85
  98.3 8.1 %fusion = f32[4,128,2004]{1,2,0:T(8,128)} fusion(bf16[2048,2004]{0,1:T(8,128)(2,1)} %param.11, bf16[128,4,2048]{2,0,1:T(8,128)(2,1)S(1)} %all_to_all.49), kind=kOutput, calls=%fused_computation | convolution fusion | flops 4202692608 | bytes 14409728 | tf_op jit(solution)/shard_map/dot_general | solution.py:87
  106.5 4.8 %all-to-all-start.2 = ((f32[4,128,2004]{1,2,0:T(8,128)}), f32[4,128,2004]{1,2,0:T(8,128)}, u32[]{:S(2)}, u32[]{:S(2)}) async-start(f32[4,128,2004]{1,2,0:T(8,128)} %fusion), calls=%async_computation.2 | async-start | bytes 8224768 | tf_op jit(solution)/shard_map/all_to_all | solution.py:33
  111.4 46.2 %all-to-all-done.2 = f32[4,128,2004]{1,2,0:T(8,128)} async-done(((f32[4,128,2004]{1,2,0:T(8,128)}), f32[4,128,2004]{1,2,0:T(8,128)}, u32[]{:S(2)}, u32[]{:S(2)}) %all-to-all-start.2) | async-done | bytes 4104224 | tf_op jit(solution)/shard_map/all_to_all | solution.py:33
  157.5 2.5 %reduce_sum.45 = f32[128,2004]{0,1:T(8,128)S(1)} reduce(f32[4,128,2004]{1,2,0:T(8,128)} %all-to-all-done.2, f32[]{:T(128)} %constant.10.clone.1), dimensions={0}, to_apply=%region_0.0 | reduce | flops 769536 | bytes 5130244 | tf_op jit(solution)/shard_map/reduce_sum | solution.py:34
  160.1 2.9 %fusion.11 = (f32[128]{0:T(128)S(1)}, f32[128,2004]{0,1:T(8,128)S(1)}, s32[128,2004]{0,1:T(8,128)}) fusion(f32[128]{0:T(128)S(1)} %copy-done.1, f32[128]{0:T(128)S(1)} %copy-done.2, f32[128]{0:T(128)S(1)} %copy-done.3, f32[128,2004]{0,1:T(8,128)S(1)} %reduce_sum.45, f32[128]{0:T(128)S(1)} %copy-done.4, s32[128,2004]{0,1:T(8,128)S(1)} %copy-done, ...), kind=kLoop, calls=%fused_computation.25 | loop fusion | flops 4617088 | bytes 5141328 | tf_op jit(solution)/shard_map/reduce_max | solution.py:100
  163.0 0.6 broadcast_in_dim.21
  163.6 9.1 %all-to-all-start.3 = ((f32[64,1,128]{2,1,0:T(1,128)}), f32[64,1,128]{2,1,0:T(1,128)S(1)}, u32[]{:S(2)}, u32[]{:S(2)}) async-start(f32[64,1,128]{2,1,0:T(1,128)} %broadcast_in_dim.21), calls=%async_computation.3 | async-start | bytes 65536 | tf_op jit(solution)/shard_map/all_to_all | solution.py:11
  172.8 9.2 %all-to-all-done.3 = f32[64,1,128]{2,1,0:T(1,128)S(1)} async-done(((f32[64,1,128]{2,1,0:T(1,128)}), f32[64,1,128]{2,1,0:T(1,128)S(1)}, u32[]{:S(2)}, u32[]{:S(2)}) %all-to-all-start.3) | async-done | bytes 32800 | tf_op jit(solution)/shard_map/all_to_all | solution.py:11
  182.0 0.3 exponential_reduce_fusion
  182.3 0.6 broadcast_in_dim.22
  183.0 4.7 %all-to-all-start.4 = ((f32[64,1,128]{2,1,0:T(1,128)}), f32[64,1,128]{2,1,0:T(1,128)S(1)}, u32[]{:S(2)}, u32[]{:S(2)}) async-start(f32[64,1,128]{2,1,0:T(1,128)} %broadcast_in_dim.22), calls=%async_computation.4 | async-start | bytes 65536 | tf_op jit(solution)/shard_map/all_to_all | solution.py:11
  187.7 9.3 %all-to-all-done.4 = f32[64,1,128]{2,1,0:T(1,128)S(1)} async-done(((f32[64,1,128]{2,1,0:T(1,128)}), f32[64,1,128]{2,1,0:T(1,128)S(1)}, u32[]{:S(2)}, u32[]{:S(2)}) %all-to-all-start.4) | async-done | bytes 32800 | tf_op jit(solution)/shard_map/all_to_all | solution.py:11
  197.3 0.1 reduce_sum.47
  197.4 1.1 exponential_divide_fusion
  198.6 0.6 fusion.3
  199.3 0.3 copy.30
  199.7 0.4 fusion.10
  200.1 13.3 %all_to_all.50 = f32[64,1,128]{2,1,0:T(1,128)S(1)} all-to-all(f32[64,1,128]{2,1,0:T(1,128)S(1)} %broadcast_in_dim.42), channel_id=1, replica_groups=mesh['dp'=4,'vocab'=64] {'vocab'}, dimensions={0} | all-to-all | bytes 65536 | tf_op jit(solution)/shard_map/all_to_all | solution.py:11
  213.5 0.5 reduce_sum.49
  (41 shorter events, 0.6 us)
Async XLA Ops:
  106.5 51.1 %all-to-all-start.2 = ((f32[4,128,2004]{1,2,0:T(8,128)}), f32[4,128,2004]{1,2,0:T(8,128)}, u32[]{:S(2)}, u32[]{:S(2)}) async-start(f32[4,128,2004]{1,2,0:T(8,128)} %fusion), calls=%async_computation.2 | async-start | bytes 8224768 | tf_op jit(solution)/shard_map/all_to_all | solution.py:33
  111.3 48.8 %copy-start = (s32[128,2004]{0,1:T(8,128)S(1)}, s32[128,2004]{0,1:T(8,128)}, u32[]{:S(2)}) copy-start(s32[128,2004]{0,1:T(8,128)} %param.12) | copy-start | bytes 3078148
  111.3 48.8 %copy-start.1 = (f32[128]{0:T(128)S(1)}, f32[128]{0:T(128)}, u32[]{:S(2)}) copy-start(f32[128]{0:T(128)} %param.18) | copy-start | bytes 1540
  111.3 48.8 %copy-start.2 = (f32[128]{0:T(128)S(1)}, f32[128]{0:T(128)}, u32[]{:S(2)}) copy-start(f32[128]{0:T(128)} %param.17) | copy-start | bytes 1540
  111.3 48.8 %copy-start.3 = (f32[128]{0:T(128)S(1)}, f32[128]{0:T(128)}, u32[]{:S(2)}) copy-start(f32[128]{0:T(128)} %param.16) | copy-start | bytes 1540
  111.3 48.8 %copy-start.4 = (f32[128]{0:T(128)S(1)}, f32[128]{0:T(128)}, u32[]{:S(2)}) copy-start(f32[128]{0:T(128)} %param.15) | copy-start | bytes 1540
  111.4 48.8 %copy-start.5 = (s32[128]{0:T(128)S(1)}, s32[128]{0:T(128)}, u32[]{:S(2)}) copy-start(s32[128]{0:T(128)} %param.14) | copy-start | bytes 1540
  163.6 18.4 %all-to-all-start.3 = ((f32[64,1,128]{2,1,0:T(1,128)}), f32[64,1,128]{2,1,0:T(1,128)S(1)}, u32[]{:S(2)}, u32[]{:S(2)}) async-start(f32[64,1,128]{2,1,0:T(1,128)} %broadcast_in_dim.21), calls=%async_computation.3 | async-start | bytes 65536 | tf_op jit(solution)/shard_map/all_to_all | solution.py:11
  183.0 14.1 %all-to-all-start.4 = ((f32[64,1,128]{2,1,0:T(1,128)}), f32[64,1,128]{2,1,0:T(1,128)S(1)}, u32[]{:S(2)}, u32[]{:S(2)}) async-start(f32[64,1,128]{2,1,0:T(1,128)} %broadcast_in_dim.22), calls=%async_computation.4 | async-start | bytes 65536 | tf_op jit(solution)/shard_map/all_to_all | solution.py:11
  198.5 1.2 copy-start.6
where the time goes:
time: 215 us; the launch traced here: 214 us
  blocking collectives  107 us (50%)
  waiting for transfers between devices  64.7 us (30%)
  starting transfers between devices  18.6 us (9%)
  other arithmetic  8.71 us (4%)
  matrix products  8.14 us (4%)
  local copies, waits for them, and re-layouts  5.95 us (3%)
    all_to_all x2, blocking collectives, copy_for_each(): return lax.all_to_all(copies, axis, split_axis=0, concat_axis=0, tiled=True)  77.5 us
    all_to_all x1, waiting for transfers between devices, sum_at_owner(): lax.all_to_all(pieces, axis, split_axis=0, concat_axis=0, tiled=True)  46.2 us
    all_to_all x1, blocking collectives, on_device(): lax.all_to_all(full_rows, 'dp', split_axis=1, concat_axis=0, tiled=True)  29.5 us
    all_to_all x2, waiting for transfers between devices, copy_for_each(): return lax.all_to_all(copies, axis, split_axis=0, concat_axis=0, tiled=True)  18.6 us
    all_to_all x2, starting transfers between devices, copy_for_each(): return lax.all_to_all(copies, axis, split_axis=0, concat_axis=0, tiled=True)  13.8 us
    dot_general x1, matrix products, on_device(): jnp.dot(quarter_rows, output_projection_weights, preferred_element_type=j...  8.14 us
    all_to_all x1, starting transfers between devices, sum_at_owner(): lax.all_to_all(pieces, axis, split_axis=0, concat_axis=0, tiled=True)  4.83 us
  transfers between devices with their start and end apart: 3, of which 3 were waited for; matrix products, arithmetic and copies ran while one was open for 0% of the time, Pallas kernels for 0%

commit v1 on v0

v1 whole, which is shorter than its diff:
```python
import jax
import jax.numpy as jnp
from jax import lax
from jax.sharding import Mesh
from jax.sharding import PartitionSpec as P

VOCAB = 128256
NX, NY, NZ, NC = 4, 4, 8, 2
PLANE = ("y", "z", "c")
EVERY = ("x", "y", "z", "c")
HALF = 1000


def moved(value, to):
    pairs = []
    for x in range(NX):
        for y in range(NY):
            for z in range(NZ):
                for c in range(NC):
                    tx, ty, tz, tc = to(x, y, z, c)
                    source = ((x * NY + y) * NZ + z) * NC + c
                    target = ((tx % NX * NY + ty % NY) * NZ + tz % NZ) * NC + tc % NC
                    pairs.append((source, target))
    return lax.ppermute(value, EVERY, pairs)


def copies_from(value, axis):
    size = lax.axis_size(axis)
    copies = jnp.broadcast_to(value, (size, *value.shape))
    return lax.all_to_all(copies, axis, split_axis=0, concat_axis=0, tiled=True)


def gathered_quarter(rows):
    mine = moved(rows, lambda x, y, z, c: (y, x, z, c))
    mine = copies_from(mine, "z")
    mine = copies_from(mine, "y")
    other = moved(mine, lambda x, y, z, c: (x, y, z, 1 - c))
    first = lax.axis_index("c") == 0
    both = jnp.stack(
        [jnp.where(first, mine, other), jnp.where(first, other, mine)], axis=2
    )
    return jnp.transpose(both, (0, 3, 1, 2, 4)).reshape(NX, 128, 2048)


def summed_at_owner(part):
    def up(value):
        return moved(value, lambda x, y, z, c: (x + 1, y, z, c))

    def down(value):
        return moved(value, lambda x, y, z, c: (x - 1, y, z, c))

    own, after, far, before = part
    far_a = up(far[:HALF])
    far_b = down(far[HALF:])
    after_b = up(after[HALF:])
    before_a = down(before[:HALF])
    after_a = up(after[:HALF] + far_a)
    before_b = down(before[HALF:] + far_b)
    return jnp.concatenate(
        [own[:HALF] + before_a + after_a, own[HALF:] + after_b + before_b], axis=0
    )


def on_device(
    final_activation,
    output_projection_weights,
    context_word_tallies,
    emitted_word_tallies,
    freshest_word,
    recurrence_divisor,
    recurrence_fine,
    appearance_fine,
    softness_level,
    random_draws,
):
    shard_width = output_projection_weights.shape[1]
    shard = lax.axis_index(PLANE)
    token_ids = shard * shard_width + lax.broadcasted_iota(jnp.int32, (1, shard_width), 1)
    new_counts = emitted_word_tallies + (token_ids == freshest_word[:, None]).astype(jnp.int32)
    seen = context_word_tallies + new_counts > 0

    groups = gathered_quarter(final_activation)
    groups = jnp.roll(groups, -lax.axis_index("x"), axis=0)
    weights = output_projection_weights.T
    part = lax.dot_general(
        weights, groups, (((1,), (2,)), ((), ())), preferred_element_type=jnp.float32
    )
    part = [part[:, k] for k in range(NX)]
    logits = summed_at_owner(part).T

    factor = recurrence_divisor[:, None]
    adjusted = jnp.where(seen, jnp.where(logits > 0, logits / factor, logits * factor), logits)
    adjusted = adjusted - recurrence_fine[:, None] * new_counts.astype(jnp.float32)
    adjusted = adjusted - appearance_fine[:, None] * (new_counts > 0).astype(jnp.float32)
    softened = adjusted / softness_level[:, None]

    local_top = jnp.max(softened, axis=1)
    mass = jnp.exp(softened - local_top[:, None])
    local_sum = jnp.sum(mass, axis=1)
    stats = copies_from(jnp.stack([local_top, local_sum]), PLANE)
    stats = stats.reshape(64, 2, 128)
    top = jnp.max(stats[:, 0], axis=0)
    sums = stats[:, 1] * jnp.exp(stats[:, 0] - top)
    total = jnp.sum(sums, axis=0)
    passed = lax.broadcasted_iota(jnp.int32, (64, 1), 0) < shard
    lower = jnp.sum(jnp.where(passed, sums, 0.0), axis=0) / total

    log_likelihoods = softened - top[:, None] - jnp.log(total)[:, None]
    probs = jnp.exp(softened - top[:, None]) / total[:, None]
    below = lower[:, None] + jnp.cumsum(probs, axis=1) - probs
    taken = jnp.minimum(jnp.maximum(random_draws[:, None] - below, 0.0), probs)
    position = (token_ids.astype(jnp.float32) + 0.5) / VOCAB
    partial_quantile = jnp.sum(taken * position, axis=1)
    sample_quantile = jnp.sum(copies_from(partial_quantile[None], PLANE), axis=0)[0]
    return new_counts, log_likelihoods, sample_quantile


def solution(mesh):
    split = Mesh(mesh.devices.reshape(NX, NY, NZ, NC), EVERY)
    whole = P("x", PLANE)
    row = P("x")
    return jax.shard_map(
        on_device,
        mesh=split,
        in_specs=(whole, whole, whole, whole, row, row, row, row, row, row),
        out_specs=(whole, whole, row),
        check_vma=False,
    )
```

time: 215 us -> 142 us (0.66)
  blocking collectives: 107 us -> 53.9 us
  waiting for transfers between devices: 64.7 us -> 42 us
  local copies, waits for them, and re-layouts: 5.95 us -> 8.22 us
    all_to_all x3 -> x1, waiting for transfers between devices: 64.7 us -> 9.84 us  [copies_from(): return lax.all_to_all(copies, axis, split_axis=0, concat_axis=0, tiled=True)]
    all_to_all x3, blocking collectives: 107 us -> 53.9 us  [copies_from(): return lax.all_to_all(copies, axis, split_axis=0, concat_axis=0, tiled=True)]
    ppermute x0 -> x8, waiting for transfers between devices: none -> 32.1 us  [moved(): return lax.ppermute(value, EVERY, pairs)]
    all_to_all x3 -> x1, starting transfers between devices: 18.6 us -> 6.15 us  [copies_from(): return lax.all_to_all(copies, axis, split_axis=0, concat_axis=0, tiled=True)]
    ppermute x0 -> x8, starting transfers between devices: none -> 12.3 us  [moved(): return lax.ppermute(value, EVERY, pairs)]
    add x6 -> x5, other arithmetic: 0.03 us -> 2.98 us  [the longest x1 1.42 us: summed_at_owner(): own[HALF:] + after_b + before_b]
    reshape x0 -> x1, local copies, waits for them, and re-layouts: none -> 2.82 us  [gathered_quarter(): return jnp.transpose(both, (0, 3, 1, 2, 4)).reshape(NX, 128, 2048)]
    all_to_all x1 -> x0, local copies, waits for them, and re-layouts: 2.69 us -> none  [on_device(): lax.all_to_all(full_rows, 'dp', split_axis=1, concat_axis=0, tiled=True)]
  transfers between devices with their start and end apart: 3 -> 9, of which waited for: 3 -> 7; matrix products, arithmetic and copies ran while one was open for 0% -> 2% of each run, Pallas kernels for 0% -> 0%
where the time goes in v1:
time: 142 us; the launch traced here: 141 us
  blocking collectives  53.9 us (38%)
  waiting for transfers between devices  42 us (30%)
  starting transfers between devices  18.5 us (13%)
  other arithmetic  9.99 us (7%)
  local copies, waits for them, and re-layouts  8.22 us (6%)
  matrix products  7.67 us (5%)
    all_to_all x3, blocking collectives, copies_from(): return lax.all_to_all(copies, axis, split_axis=0, concat_axis=0, tiled=True)  53.9 us
    ppermute x8, waiting for transfers between devices, moved(): return lax.ppermute(value, EVERY, pairs)  32.1 us
    ppermute x8, starting transfers between devices, moved(): return lax.ppermute(value, EVERY, pairs)  12.3 us
    all_to_all x1, waiting for transfers between devices, copies_from(): return lax.all_to_all(copies, axis, split_axis=0, concat_axis=0, tiled=True)  9.84 us
    dot_general x1, matrix products, on_device(): lax.dot_general(weights, groups, (((1,), (2,)), ((), ())), preferred_elem...  7.67 us
    all_to_all x1, starting transfers between devices, copies_from(): return lax.all_to_all(copies, axis, split_axis=0, concat_axis=0, tiled=True)  6.15 us
    reduce_max x1, other arithmetic, on_device(): local_top = jnp.max(softened, axis=1)  3.47 us
  transfers between devices with their start and end apart: 9, of which 7 were waited for; matrix products, arithmetic and copies ran while one was open for 2% of the time, Pallas kernels for 0%

profile of v1, /device:TPU:1, one launch (start us, length us, event | category | flops | bytes accessed | tf_op | source)
XLA Modules:
  0.0 141.1 jit_solution(15624143930725616905)
XLA Ops:
  0.6 1.4 %collective-permute-start = (bf16[128,128]{1,0:T(8,128)(2,1)}, bf16[128,128]{1,0:T(8,128)(2,1)S(1)}, u32[]{:S(2)}, u32[]{:S(2)}) collective-permute-start(bf16[128,128]{1,0:T(8,128)(2,1)} %param.10), channel_id=1, source_target_pairs={{0,0},{1,1},{2,2},{3,3},{4,4},{5,5},{6,6},{7,7},{8,8},{9,9},{10,10... | collective-permute-start | bytes 98312 | tf_op jit(solution)/shard_map/ppermute | solution.py:24
  2.1 19.3 %all_to_all.20 = bf16[8,128,128]{2,1,0:T(8,128)(2,1)S(1)} all-to-all(bf16[8,128,128]{2,1,0:T(8,128)(2,1)S(1)} %broadcast_in_dim.20), channel_id=1, replica_groups=mesh['x'=4,'y'=4,'z'=8,'c'=2] {'z'}, dimensions={0} | all-to-all | bytes 524288 | tf_op jit(solution)/shard_map/all_to_all | solution.py:30
  21.6 21.5 %all_to_all.21 = bf16[4,8,128,128]{3,2,1,0:T(8,128)(2,1)S(1)} all-to-all(bf16[4,8,128,128]{3,2,1,0:T(8,128)(2,1)S(1)} %broadcast_in_dim.21), channel_id=1, replica_groups=mesh['x'=4,'y'=4,'z'=8,'c'=2] {'y'}, dimensions={0} | all-to-all | bytes 2097152 | tf_op jit(solution)/shard_map/all_to_all | solution.py:30
  43.1 4.7 %collective-permute-start.1 = (bf16[4,8,128,128]{3,2,1,0:T(8,128)(2,1)S(1)}, bf16[4,8,128,128]{3,2,1,0:T(8,128)(2,1)S(1)}, u32[]{:S(2)}, u32[]{:S(2)}) collective-permute-start(bf16[4,8,128,128]{3,2,1,0:T(8,128)(2,1)S(1)} %all_to_all.21), channel_id=1, source_target_pairs={{0,1},{1,0},{2,3},{3,2},{4,5},{5,4},{6,7},{7,6},{8,9},{9,8},{10,11... | collective-permute-start | bytes 3145736 | tf_op jit(solution)/shard_map/ppermute | solution.py:24
  47.8 2.3 %collective-permute-done.1 = bf16[4,8,128,128]{3,2,1,0:T(8,128)(2,1)S(1)} collective-permute-done((bf16[4,8,128,128]{3,2,1,0:T(8,128)(2,1)S(1)}, bf16[4,8,128,128]{3,2,1,0:T(8,128)(2,1)S(1)}, u32[]{:S(2)}, u32[]{:S(2)}) %collective-permute-start.1) | collective-permute-done | bytes 1048608 | tf_op jit(solution)/shard_map/ppermute | solution.py:24
  50.4 2.2 %copy.24 = bf16[4,128,8,2,128]{4,3,2,1,0:T(2,128)(2,1)S(1)} copy(bf16[4,128,8,2,128]{4,1,2,0,3:T(8,128)(2,1)S(1)} %maximum_bitcast_fusion) | data formatting | bytes 4194304 | tf_op jit(solution)/shard_map/transpose | solution.py:42
  52.6 2.8 %reshape.64 = bf16[4,128,2048]{2,1,0:T(8,128)(2,1)} reshape(bf16[4,128,8,2,128]{4,3,2,1,0:T(2,128)(2,1)S(1)} %copy.24) | data formatting | bytes 4194304 | tf_op jit(solution)/shard_map/reshape | solution.py:42
  55.4 7.7 %fusion.2 = f32[2004,4,128]{2,0,1:T(8,128)S(1)} fusion(bf16[2048,2004]{0,1:T(8,128)(2,1)} %param.11, s32[]{:T(128)S(6)} %select_n.40, bf16[4,128,2048]{2,1,0:T(8,128)(2,1)} %reshape.64), kind=kOutput, calls=%fused_computation.4 | convolution fusion | flops 4203741184 | bytes 14409732 | tf_op jit(solution)/shard_map/dot_general | solution.py:85
  63.1 0.9 slice_bitcast_fusion.6
  64.0 0.9 collective-permute-start.3
  65.0 0.9 slice_bitcast_fusion.2
  65.9 1.8 %collective-permute-start.6 = (f32[1004,128]{1,0:T(8,128)S(1)}, f32[1004,128]{1,0:T(8,128)S(1)}, u32[]{:S(2)}, u32[]{:S(2)}) collective-permute-start(f32[1004,128]{1,0:T(8,128)S(1)} %get-tuple-element.11), channel_id=1, source_target_pairs={{0,192},{1,193},{2,194},{3,195},{4,196},{5,197},{6,198},{7,199},{8... | collective-permute-start | bytes 1542152 | tf_op jit(solution)/shard_map/ppermute | solution.py:24
  67.8 10.3 %collective-permute-done.3 = f32[1000,128]{1,0:T(8,128)S(1)} collective-permute-done((f32[1000,128]{1,0:T(8,128)S(1)}, f32[1000,128]{1,0:T(8,128)S(1)}, u32[]{:S(2)}, u32[]{:S(2)}) %collective-permute-start.3) | collective-permute-done | bytes 512032 | tf_op jit(solution)/shard_map/ppermute | solution.py:24
  78.7 3.2 %collective-permute-start.7 = (f32[1004,128]{1,0:T(8,128)S(1)}, f32[1004,128]{1,0:T(8,128)}, u32[]{:S(2)}, u32[]{:S(2)}) collective-permute-start(f32[1004,128]{1,0:T(8,128)S(1)} %fusion.15), channel_id=1, source_target_pairs={{0,192},{1,193},{2,194},{3,195},{4,196},{5,197},{6,198},{7,199},{8... | collective-permute-start | bytes 1542152 | tf_op jit(solution)/shard_map/ppermute | solution.py:24
  81.9 7.7 %collective-permute-done.2 = f32[1000,128]{1,0:T(8,128)} collective-permute-done((f32[1000,128]{1,0:T(8,128)}, f32[1000,128]{1,0:T(8,128)}, u32[]{:S(2)}, u32[]{:S(2)}) %collective-permute-start.2) | collective-permute-done | bytes 512032 | tf_op jit(solution)/shard_map/ppermute | solution.py:24
  89.7 1.9 %collective-permute-done.4 = f32[1000,128]{1,0:T(8,128)} collective-permute-done((f32[1000,128]{1,0:T(8,128)S(1)}, f32[1000,128]{1,0:T(8,128)}, u32[]{:S(2)}, u32[]{:S(2)}) %collective-permute-start.4) | collective-permute-done | bytes 512032 | tf_op jit(solution)/shard_map/ppermute | solution.py:24
  91.5 1.4 %fusion.20 = f32[1000,128]{1,0:T(8,128)S(1)} fusion(f32[1000,128]{1,0:T(8,128)} %collective-permute-done.4, f32[1000,128]{1,0:T(8,128)} %collective-permute-done.2, f32[2004,4,128]{2,0,1:T(8,128)} %copy-done), kind=kLoop, calls=%fused_computation.39 | loop fusion | flops 256000 | bytes 2048000 | tf_op jit(solution)/shard_map/add | solution.py:60
  93.0 9.6 %collective-permute-done.5 = f32[1004,128]{1,0:T(8,128)} collective-permute-done((f32[1004,128]{1,0:T(8,128)}, f32[1004,128]{1,0:T(8,128)}, u32[]{:S(2)}, u32[]{:S(2)}) %collective-permute-start.5) | collective-permute-done | bytes 514080 | tf_op jit(solution)/shard_map/ppermute | solution.py:24
  102.6 1.4 %fusion.17 = f32[1004,128]{1,0:T(8,128)S(1)} fusion(f32[1004,128]{1,0:T(8,128)} %collective-permute-done.7, f32[1004,128]{1,0:T(8,128)} %collective-permute-done.5, f32[2004,4,128]{2,0,1:T(8,128)} %copy-done), kind=kLoop, calls=%fused_computation.32 | loop fusion | flops 257024 | bytes 2056192 | tf_op jit(solution)/shard_map/add | solution.py:60
  104.1 3.5 %fusion.24 = (f32[128]{0:T(128)S(1)}, f32[128,2004]{0,1:T(8,128)S(1)}, s32[128,2004]{0,1:T(8,128)}) fusion(f32[128]{0:T(128)S(1)} %copy-done.3, f32[128]{0:T(128)S(1)} %copy-done.4, f32[128]{0:T(128)S(1)} %copy-done.5, f32[128]{0:T(128)S(1)} %copy-done.6, f32[1004,128]{1,0:T(8,128)S(1)} %fusion.17, f32[1000,128]{1,0:T(8,128)S(1)} %fusion.20, ...), kind=kLoop, calls=%fused_computation.50 | loop fusion | flops 4873600 | bytes 5141328 | tf_op jit(solution)/shard_map/reduce_max | solution.py:97
  108.5 6.2 %all-to-all-start.2 = ((f32[64,2,128]{2,1,0:T(2,128)}), f32[64,2,128]{2,1,0:T(2,128)S(1)}, u32[]{:S(2)}, u32[]{:S(2)}) async-start(f32[64,2,128]{2,1,0:T(2,128)} %broadcast_in_dim.22), calls=%async_computation.2 | async-start | bytes 131072 | tf_op jit(solution)/shard_map/all_to_all | solution.py:30
  114.7 9.8 %all-to-all-done.2 = f32[64,2,128]{2,1,0:T(2,128)S(1)} async-done(((f32[64,2,128]{2,1,0:T(2,128)}), f32[64,2,128]{2,1,0:T(2,128)S(1)}, u32[]{:S(2)}, u32[]{:S(2)}) %all-to-all-start.2) | async-done | bytes 65568 | tf_op jit(solution)/shard_map/all_to_all | solution.py:30
  124.7 1.1 exponential_divide_fusion
  127.4 13.2 %all_to_all.22 = f32[64,1,128]{2,1,0:T(1,128)S(1)} all-to-all(f32[64,1,128]{2,1,0:T(1,128)S(1)} %broadcast_in_dim.25), channel_id=1, replica_groups=mesh['x'=4,'y'=4,'z'=8,'c'=2] {'y','z','c'}, dimensions={0} | all-to-all | bytes 65536 | tf_op jit(solution)/shard_map/all_to_all | solution.py:30
  (50 shorter events, 4.5 us)
Async XLA Ops:
  0.6 1.4 %collective-permute-start = (bf16[128,128]{1,0:T(8,128)(2,1)}, bf16[128,128]{1,0:T(8,128)(2,1)S(1)}, u32[]{:S(2)}, u32[]{:S(2)}) collective-permute-start(bf16[128,128]{1,0:T(8,128)(2,1)} %param.10), channel_id=1, source_target_pairs={{0,0},{1,1},{2,2},{3,3},{4,4},{5,5},{6,6},{7,7},{8,8},{9,9},{10,10... | collective-permute-start | bytes 98312 | tf_op jit(solution)/shard_map/ppermute | solution.py:24
  43.1 7.0 %collective-permute-start.1 = (bf16[4,8,128,128]{3,2,1,0:T(8,128)(2,1)S(1)}, bf16[4,8,128,128]{3,2,1,0:T(8,128)(2,1)S(1)}, u32[]{:S(2)}, u32[]{:S(2)}) collective-permute-start(bf16[4,8,128,128]{3,2,1,0:T(8,128)(2,1)S(1)} %all_to_all.21), channel_id=1, source_target_pairs={{0,1},{1,0},{2,3},{3,2},{4,5},{5,4},{6,7},{7,6},{8,9},{9,8},{10,11... | collective-permute-start | bytes 3145736 | tf_op jit(solution)/shard_map/ppermute | solution.py:24
  63.1 15.5 %copy-start = (f32[2004,4,128]{2,0,1:T(8,128)}, f32[2004,4,128]{2,0,1:T(8,128)S(1)}, u32[]{:S(2)}) copy-start(f32[2004,4,128]{2,0,1:T(8,128)S(1)} %fusion.2) | copy-start | bytes 12312580
  64.0 14.1 %collective-permute-start.3 = (f32[1000,128]{1,0:T(8,128)S(1)}, f32[1000,128]{1,0:T(8,128)S(1)}, u32[]{:S(2)}, u32[]{:S(2)}) collective-permute-start(f32[1000,128]{1,0:T(8,128)S(1)} %get-tuple-element.9), channel_id=1, source_target_pairs={{0,64},{1,65},{2,66},{3,67},{4,68},{5,69},{6,70},{7,71},{8,72},{9,... | collective-permute-start | bytes 1536008 | tf_op jit(solution)/shard_map/ppermute | solution.py:24
  65.8 38.2 %copy-start.1 = (s32[128,2004]{0,1:T(8,128)S(1)}, s32[128,2004]{0,1:T(8,128)}, u32[]{:S(2)}) copy-start(s32[128,2004]{0,1:T(8,128)} %param.12) | copy-start | bytes 3078148
  65.8 38.2 %copy-start.2 = (s32[128,2004]{0,1:T(8,128)S(1)}, s32[128,2004]{0,1:T(8,128)}, u32[]{:S(2)}) copy-start(s32[128,2004]{0,1:T(8,128)} %param.13) | copy-start | bytes 3078148
  65.8 38.2 %copy-start.3 = (f32[128]{0:T(128)S(1)}, f32[128]{0:T(128)}, u32[]{:S(2)}) copy-start(f32[128]{0:T(128)} %param.18) | copy-start | bytes 1540
  65.8 38.2 %copy-start.4 = (f32[128]{0:T(128)S(1)}, f32[128]{0:T(128)}, u32[]{:S(2)}) copy-start(f32[128]{0:T(128)} %param.17) | copy-start | bytes 1540
  65.8 38.2 %copy-start.5 = (f32[128]{0:T(128)S(1)}, f32[128]{0:T(128)}, u32[]{:S(2)}) copy-start(f32[128]{0:T(128)} %param.16) | copy-start | bytes 1540
  65.8 38.2 %copy-start.6 = (f32[128]{0:T(128)S(1)}, f32[128]{0:T(128)}, u32[]{:S(2)}) copy-start(f32[128]{0:T(128)} %param.15) | copy-start | bytes 1540
  65.9 38.2 %copy-start.7 = (s32[128]{0:T(128)S(1)}, s32[128]{0:T(128)}, u32[]{:S(2)}) copy-start(s32[128]{0:T(128)} %param.14) | copy-start | bytes 1540
  65.9 12.7 %collective-permute-start.6 = (f32[1004,128]{1,0:T(8,128)S(1)}, f32[1004,128]{1,0:T(8,128)S(1)}, u32[]{:S(2)}, u32[]{:S(2)}) collective-permute-start(f32[1004,128]{1,0:T(8,128)S(1)} %get-tuple-element.11), channel_id=1, source_target_pairs={{0,192},{1,193},{2,194},{3,195},{4,196},{5,197},{6,198},{7,199},{8... | collective-permute-start | bytes 1542152 | tf_op jit(solution)/shard_map/ppermute | solution.py:24
  67.7 22.0 %collective-permute-start.2 = (f32[1000,128]{1,0:T(8,128)}, f32[1000,128]{1,0:T(8,128)}, u32[]{:S(2)}, u32[]{:S(2)}) collective-permute-start(f32[1000,128]{1,0:T(8,128)} %get-tuple-element.8), channel_id=1, source_target_pairs={{0,192},{1,193},{2,194},{3,195},{4,196},{5,197},{6,198},{7,199},{8... | collective-permute-start | bytes 1536008 | tf_op jit(solution)/shard_map/ppermute | solution.py:24
  78.2 13.4 %collective-permute-start.4 = (f32[1000,128]{1,0:T(8,128)S(1)}, f32[1000,128]{1,0:T(8,128)}, u32[]{:S(2)}, u32[]{:S(2)}) collective-permute-start(f32[1000,128]{1,0:T(8,128)S(1)} %fusion.18), channel_id=1, source_target_pairs={{0,64},{1,65},{2,66},{3,67},{4,68},{5,69},{6,70},{7,71},{8,72},{9,... | collective-permute-start | bytes 1536008 | tf_op jit(solution)/shard_map/ppermute | solution.py:24
  78.3 24.4 %collective-permute-start.5 = (f32[1004,128]{1,0:T(8,128)}, f32[1004,128]{1,0:T(8,128)}, u32[]{:S(2)}, u32[]{:S(2)}) collective-permute-start(f32[1004,128]{1,0:T(8,128)} %get-tuple-element.10), channel_id=1, source_target_pairs={{0,64},{1,65},{2,66},{3,67},{4,68},{5,69},{6,70},{7,71},{8,72},{9,... | collective-permute-start | bytes 1542152 | tf_op jit(solution)/shard_map/ppermute | solution.py:24
  78.7 23.9 %collective-permute-start.7 = (f32[1004,128]{1,0:T(8,128)S(1)}, f32[1004,128]{1,0:T(8,128)}, u32[]{:S(2)}, u32[]{:S(2)}) collective-permute-start(f32[1004,128]{1,0:T(8,128)S(1)} %fusion.15), channel_id=1, source_target_pairs={{0,192},{1,193},{2,194},{3,195},{4,196},{5,197},{6,198},{7,199},{8... | collective-permute-start | bytes 1542152 | tf_op jit(solution)/shard_map/ppermute | solution.py:24
  108.5 16.0 %all-to-all-start.2 = ((f32[64,2,128]{2,1,0:T(2,128)}), f32[64,2,128]{2,1,0:T(2,128)S(1)}, u32[]{:S(2)}, u32[]{:S(2)}) async-start(f32[64,2,128]{2,1,0:T(2,128)} %broadcast_in_dim.22), calls=%async_computation.2 | async-start | bytes 131072 | tf_op jit(solution)/shard_map/all_to_all | solution.py:30
  125.9 1.2 copy-start.8

commit v2 on v1

v2 whole, which is shorter than its diff:
```python
import jax
import jax.numpy as jnp
from jax import lax
from jax.experimental import pallas as pl
from jax.experimental.pallas import tpu as pltpu
from jax.sharding import Mesh
from jax.sharding import PartitionSpec as P


VOCAB = 128256
NX, NY, NZ, NC = 4, 4, 8, 2
PLANE = ("y", "z", "c")
EVERY = ("x", "y", "z", "c")

ROWS = 2004
LANES = 128
DEPTH = 2048
HALF = 1008
THIRD = HALF // 3
CHUNK = 56
STEPS = THIRD // CHUNK
BLOCKS = ((0, 256), (256, 512), (768, 512), (1280, ROWS - 1280))
CODED = 2 * THIRD + 8
BITS = 20

WHOLE = pl.BlockSpec(memory_space=pltpu.VMEM)


def moved(value, to):
    pairs = []
    for x in range(NX):
        for y in range(NY):
            for z in range(NZ):
                for c in range(NC):
                    tx, ty, tz, tc = to(x, y, z, c)
                    source = ((x * NY + y) * NZ + z) * NC + c
                    target = ((tx % NX * NY + ty % NY) * NZ + tz % NZ) * NC + tc % NC
                    pairs.append((source, target))
    return lax.ppermute(value, EVERY, pairs)


def up(value):
    return moved(value, lambda x, y, z, c: (x + 1, y, z, c))


def down(value):
    return moved(value, lambda x, y, z, c: (x - 1, y, z, c))


def copies_from(value, axis):
    size = lax.axis_size(axis)
    copies = jnp.broadcast_to(value, (size, *value.shape))
    return lax.all_to_all(copies, axis, split_axis=0, concat_axis=0, tiled=True)


def exchanged(copies):
    return lax.all_to_all(copies, PLANE, split_axis=0, concat_axis=0, tiled=True)


def coded(load, out_ref):
    def largest(j, top):
        for third in range(3):
            part = jnp.abs(load(third * THIRD + j * CHUNK))
            top = jnp.maximum(top, jnp.max(part.reshape(CHUNK // 8, 8, LANES), axis=0))
        return top

    top = lax.fori_loop(0, STEPS, largest, jnp.zeros((8, LANES), jnp.float32))
    top = jnp.maximum(jnp.max(top, axis=0, keepdims=True), 1e-30)
    exponent = jnp.ceil(4.0 * jnp.log2(top))
    scale = jnp.exp2(BITS - 0.25 * exponent)
    limit = float(2**BITS - 1)

    def put(j, carry):
        def whole(third):
            value = jnp.round(load(third * THIRD + j * CHUNK) * scale)
            return jnp.clip(value, -limit, limit).astype(jnp.int32)

        a, b, c = whole(0), whole(1), whole(2)
        mask = (1 << 21) - 1
        out_ref[pl.ds(pl.multiple_of(j * CHUNK, 8), CHUNK), :] = (a & mask) | (c << 21)
        out_ref[pl.ds(pl.multiple_of(THIRD + j * CHUNK, 8), CHUNK), :] = (b & mask) | ((c >> 11) << 21)
        return carry

    lax.fori_loop(0, STEPS, put, 0)
    out_ref[2 * THIRD :, :] = jnp.broadcast_to(exponent.astype(jnp.int32), (8, LANES))


def step_of(ref):
    return jnp.exp2(0.25 * ref[2 * THIRD : 2 * THIRD + 1, :].astype(jnp.float32) - BITS)


def decoded(ref, step, j):
    one = ref[pl.ds(pl.multiple_of(j * CHUNK, 8), CHUNK), :]
    two = ref[pl.ds(pl.multiple_of(THIRD + j * CHUNK, 8), CHUNK), :]
    a = (one << 11) >> 11
    b = (two << 11) >> 11
    c = ((two >> 21) << 11) | ((one >> 21) & 2047)
    return [value.astype(jnp.float32) * step for value in (a, b, c)]


def aligned(start):
    return pl.multiple_of(start, 8)


def shard_index():
    return (lax.axis_index("y") * NZ + lax.axis_index("z")) * NC + lax.axis_index("c")


def product_kernel(
    mine, other, source, far_a, far_b, after_b, before_a, after_a, before_b, own, weights, rows, part, here
):
    copies = [
        pltpu.make_async_copy(source.at[pl.ds(start, size)], weights.at[pl.ds(start, size)], here.at[n])
        for n, (start, size) in enumerate(BLOCKS)
    ]
    for copy in copies:
        copy.start()
    x, c = lax.axis_index("x"), lax.axis_index("c")
    for r in range(NX):
        group = lax.rem(x + r, NX)
        for z in range(NZ):
            at = pl.ds(r * LANES, LANES)
            rows[at, pl.ds(pl.multiple_of((2 * z + c) * 128, 128), 128)] = mine[group, z]
            rows[at, pl.ds(pl.multiple_of((2 * z + 1 - c) * 128, 128), 128)] = other[group, z]

    for (start, size), copy in zip(BLOCKS, copies):
        copy.wait()
        part[pl.ds(start, size), :] = lax.dot_general(
            weights[pl.ds(start, size), :],
            rows[...],
            (((1,), (1,)), ((), ())),
            preferred_element_type=jnp.float32,
        )
    part[ROWS : 2 * HALF, :] = jnp.zeros((2 * HALF - ROWS, NX * LANES), jnp.float32)

    def load(r, half):
        return lambda start: part[pl.ds(aligned(half * HALF + start), CHUNK), pl.ds(r * LANES, LANES)]

    coded(load(2, 0), far_a)
    coded(load(2, 1), far_b)
    coded(load(1, 1), after_b)
    coded(load(3, 0), before_a)
    after_a[...] = part[0:HALF, LANES : 2 * LANES]
    before_b[...] = part[HALF : 2 * HALF, 3 * LANES :]
    own[...] = part[0 : 2 * HALF, 0:LANES]


def products(mine, other, weights):
    code = jax.ShapeDtypeStruct((CODED, LANES), jnp.int32)
    half = jax.ShapeDtypeStruct((HALF, LANES), jnp.float32)
    return pl.pallas_call(
        product_kernel,
        out_shape=[code, code, code, code, half, half, jax.ShapeDtypeStruct((2 * HALF, LANES), jnp.float32)],
        in_specs=[WHOLE, WHOLE, pl.BlockSpec(memory_space=pltpu.HBM)],
        out_specs=[WHOLE] * 7,
        scratch_shapes=[
            pltpu.VMEM((ROWS, DEPTH), jnp.bfloat16),
            pltpu.VMEM((NX * LANES, DEPTH), jnp.bfloat16),
            pltpu.VMEM((2 * HALF, NX * LANES), jnp.float32),
            pltpu.SemaphoreType.DMA((len(BLOCKS),)),
        ],
        compiler_params=pltpu.CompilerParams(vmem_limit_bytes=44 << 20),
        cost_estimate=pl.CostEstimate(flops=2 * ROWS * 512 * DEPTH, bytes_accessed=ROWS * DEPTH * 2, transcendentals=0),
        name="products",
    )(mine, other, weights)


def relay_kernel(far_a, far_b, after_a, before_b, after_out, before_out, total):
    for far, own, out in ((far_a, after_a, after_out), (far_b, before_b, before_out)):
        step = step_of(far)

        def add(j, carry):
            for third, value in enumerate(decoded(far, step, j)):
                at = pl.ds(aligned(third * THIRD + j * CHUNK), CHUNK)
                total[at, :] = own[at, :] + value
            return carry

        lax.fori_loop(0, STEPS, add, 0)
        coded(lambda start: total[pl.ds(aligned(start), CHUNK), :], out)


def relayed(far_a, far_b, after_a, before_b):
    code = jax.ShapeDtypeStruct((CODED, LANES), jnp.int32)
    return pl.pallas_call(
        relay_kernel,
        out_shape=[code, code],
        in_specs=[WHOLE] * 4,
        out_specs=[WHOLE] * 2,
        scratch_shapes=[pltpu.VMEM((HALF, LANES), jnp.float32)],
        compiler_params=pltpu.CompilerParams(vmem_limit_bytes=16 << 20),
        cost_estimate=pl.CostEstimate(flops=20 * HALF * LANES, bytes_accessed=4 * HALF * LANES * 4, transcendentals=0),
        name="relayed",
    )(far_a, far_b, after_a, before_b)


def scores_kernel(
    own, a_one, a_two, b_one, b_two, context, emitted, fresh, divisor, fine, appearance, softness,
    scores, line, copies,
):
    factor = divisor[...]
    inverse = 1.0 / factor
    per_count = fine[...]
    per_word = appearance[...]
    cooling = 1.0 / softness[...]
    newest = fresh[...] - shard_index() * ROWS

    def chunk(j, carry, half, first, second, steps, sizes):
        pairs = zip(decoded(first, steps[0], j), decoded(second, steps[1], j))
        for third, (one, two) in enumerate(pairs):
            size = sizes[third]
            start = half * HALF + third * THIRD + j * CHUNK
            at = pl.ds(aligned(start), size)
            logits = own[at, :] + one[:size] + two[:size]
            ids = start + lax.broadcasted_iota(jnp.int32, (size, LANES), 0)
            counts = emitted[at, :] + (ids == newest).astype(jnp.int32)
            seen = context[at, :] + counts > 0
            moved_score = jnp.where(logits > 0, logits * inverse, logits * factor)
            score = jnp.where(seen, moved_score, logits)
            score = score - per_count * counts.astype(jnp.float32)
            score = score - jnp.where(counts > 0, per_word, 0.0)
            score = score * cooling
            scores[at, :] = score
            if size == CHUNK:
                score = jnp.max(score.reshape(CHUNK // 8, 8, LANES), axis=0)
            carry = jnp.maximum(carry, jnp.max(score, axis=0, keepdims=True) if size < CHUNK else score)
        return carry

    top = jnp.full((8, LANES), -jnp.inf, jnp.float32)
    for half, first, second in ((0, a_one, a_two), (1, b_one, b_two)):
        steps = (step_of(first), step_of(second))
        full = (CHUNK,) * 3

        def body(j, carry):
            return chunk(j, carry, half, first, second, steps, full)

        top = lax.fori_loop(0, STEPS - 1, body, top)
        last = CHUNK - half * (2 * HALF - ROWS)
        top = chunk(STEPS - 1, top, half, first, second, steps, (CHUNK, CHUNK, last))
    top = jnp.max(top, axis=0, keepdims=True)

    def run(j, total):
        value = jnp.exp(scores[pl.ds(aligned(j * 80), 80), :] - top)
        return total + jnp.sum(value.reshape(10, 8, LANES), axis=0)

    total = lax.fori_loop(0, 25, run, jnp.zeros((8, LANES), jnp.float32))
    total = jnp.sum(total, axis=0, keepdims=True)
    total = total + jnp.sum(jnp.exp(scores[2000:ROWS, :] - top), axis=0, keepdims=True)
    line[...] = top
    copies[:, 0:1, :] = jnp.broadcast_to(top[None], (64, 1, LANES))
    copies[:, 1:2, :] = jnp.broadcast_to(total[None], (64, 1, LANES))


def scored(*args):
    full = jax.ShapeDtypeStruct((ROWS, LANES), jnp.float32)
    line = jax.ShapeDtypeStruct((1, LANES), jnp.float32)
    return pl.pallas_call(
        scores_kernel,
        out_shape=[full, line, jax.ShapeDtypeStruct((64, 2, LANES), jnp.float32)],
        in_specs=[WHOLE] * 12,
        out_specs=[WHOLE] * 3,
        compiler_params=pltpu.CompilerParams(vmem_limit_bytes=24 << 20),
        cost_estimate=pl.CostEstimate(flops=30 * ROWS * LANES, bytes_accessed=6 * ROWS * LANES * 4, transcendentals=ROWS * LANES),
        name="scored",
    )(*args)


def prefix_kernel(scores, line, emitted, fresh, before, counts):
    newest = fresh[...] - shard_index() * ROWS
    ids = lax.broadcasted_iota(jnp.int32, (8, LANES), 0)
    top = line[...]

    def run(j, carry):
        for t in range(10):
            at = pl.ds(aligned(j * 80 + 8 * t), 8)
            value = jnp.exp(scores[at, :] - top)
            upto = value
            for shift in (1, 2, 4):
                upto = upto + jnp.where(ids >= shift, pltpu.roll(upto, shift, 0), 0.0)
            before[at, :] = (upto - value) + carry
            carry = carry + upto[7:8, :]
            counts[at, :] = emitted[at, :] + (ids + (j * 80 + 8 * t) == newest).astype(jnp.int32)
        return carry

    carry = lax.fori_loop(0, 25, run, jnp.zeros((1, LANES), jnp.float32))
    for row in range(2000, ROWS):
        before[row : row + 1, :] = carry
        carry = carry + jnp.exp(scores[row : row + 1, :] - top)
        counts[row : row + 1, :] = emitted[row : row + 1, :] + (newest == row).astype(jnp.int32)


def prefixes(scores, line, emitted, fresh):
    return pl.pallas_call(
        prefix_kernel,
        out_shape=[
            jax.ShapeDtypeStruct((ROWS, LANES), jnp.float32),
            jax.ShapeDtypeStruct((ROWS, LANES), jnp.int32),
        ],
        in_specs=[WHOLE] * 4,
        out_specs=[WHOLE] * 2,
        compiler_params=pltpu.CompilerParams(vmem_limit_bytes=8 << 20),
        cost_estimate=pl.CostEstimate(flops=400 * ROWS * LANES, bytes_accessed=2 * ROWS * LANES * 4, transcendentals=0),
        name="prefixes",
    )(scores, line, emitted, fresh)


def quantile_kernel(stats, line, draws, scores, before, copies, shift):
    shard = shard_index()
    top = jnp.max(stats[...], axis=0)[0:1, :]
    total = jnp.zeros((1, LANES), jnp.float32)
    lower = total
    for peer in range(64):
        part = stats[peer, 1:2, :] * jnp.exp(stats[peer, 0:1, :] - top)
        total = total + part
        lower = lower + jnp.where(peer < shard, part, 0.0)
    mine = line[...]
    share = jnp.exp(mine - top) / total
    room = draws[...] - lower / total
    first = shard * ROWS

    def taken(start, size):
        at = pl.ds(start, size)
        mass = jnp.exp(scores[at, :] - mine) * share
        value = jnp.minimum(jnp.maximum(room - before[at, :] * share, 0.0), mass)
        ids = first + start + lax.broadcasted_iota(jnp.int32, (size, LANES), 0)
        return value * ((ids.astype(jnp.float32) + 0.5) / VOCAB)

    def run(j, total):
        return total + jnp.sum(taken(aligned(j * 80), 80).reshape(10, 8, LANES), axis=0)

    amount = lax.fori_loop(0, 25, run, jnp.zeros((8, LANES), jnp.float32))
    amount = jnp.sum(amount, axis=0, keepdims=True) + jnp.sum(taken(2000, 4), axis=0, keepdims=True)
    copies[...] = jnp.broadcast_to(amount[None], (64, 1, LANES))
    shift[...] = top + jnp.log(total)


def quantiles(*args):
    return pl.pallas_call(
        quantile_kernel,
        out_shape=[
            jax.ShapeDtypeStruct((64, 1, LANES), jnp.float32),
            jax.ShapeDtypeStruct((1, LANES), jnp.float32),
        ],
        in_specs=[WHOLE] * 5,
        out_specs=[WHOLE] * 2,
        compiler_params=pltpu.CompilerParams(vmem_limit_bytes=8 << 20),
        cost_estimate=pl.CostEstimate(flops=10 * ROWS * LANES, bytes_accessed=2 * ROWS * LANES * 4, transcendentals=0),
        name="quantiles",
    )(*args)


def on_device(
    final_activation,
    output_projection_weights,
    context_word_tallies,
    emitted_word_tallies,
    freshest_word,
    recurrence_divisor,
    recurrence_fine,
    appearance_fine,
    softness_level,
    random_draws,
):
    fresh = freshest_word[None]
    emitted = emitted_word_tallies.T

    mine = moved(final_activation, lambda x, y, z, c: (y, x, z, c))
    mine = copies_from(mine, "z")
    mine = copies_from(mine, "y")
    other = moved(mine, lambda x, y, z, c: (x, y, z, 1 - c))
    far_a, far_b, after_b, before_a, after_a, before_b, own = products(
        mine, other, output_projection_weights.T
    )

    far_a, far_b = up(far_a), down(far_b)
    b_one, a_one = up(after_b), down(before_a)
    after_a, before_b = relayed(far_a, far_b, after_a, before_b)
    a_two, b_two = up(after_a), down(before_b)

    scores, local_top, copies = scored(
        own,
        a_one,
        a_two,
        b_one,
        b_two,
        context_word_tallies.T,
        emitted,
        fresh,
        recurrence_divisor[None],
        recurrence_fine[None],
        appearance_fine[None],
        softness_level[None],
    )

    stats = exchanged(copies)
    before, new_counts = prefixes(scores, local_top, emitted, fresh)
    copies, shift = quantiles(stats, local_top, random_draws[None], scores, before)
    sample_quantile = jnp.sum(exchanged(copies), axis=(0, 1))
    log_likelihoods = (scores - shift).T
    return new_counts.T, log_likelihoods, sample_quantile


def solution(mesh):
    split = Mesh(mesh.devices.reshape(NX, NY, NZ, NC), EVERY)
    whole = P("x", PLANE)
    row = P("x")
    return jax.shard_map(
        on_device,
        mesh=split,
        in_specs=(whole, whole, whole, whole, row, row, row, row, row, row),
        out_specs=(whole, whole, row),
        check_vma=False,
    )
```

time: 142 us -> 118 us (0.83)
  Pallas kernels: 0 us -> 14.6 us
  blocking collectives: 53.9 us -> 40.8 us
  other arithmetic: 9.99 us -> 1.62 us
  local copies, waits for them, and re-layouts: 8.22 us -> 0.3 us
  matrix products: 7.67 us -> 0 us
  waiting for transfers between devices: 42 us -> 36.5 us
  starting transfers between devices: 18.5 us -> 22.8 us
    pallas_call x0 -> x5, Pallas kernels: none -> 14.6 us  [the longest x1 8.19 us: products(): pl.pallas_call(product_kernel, out_shape=[code, code, code, code, half, h...]
    all_to_all x3 -> x2, blocking collectives: 53.9 us -> 40.8 us  [copies_from(): return lax.all_to_all(copies, axis, split_axis=0, concat_axis=0, tiled=True)]
    ppermute x8, waiting for transfers between devices: 32.1 us -> 20.2 us  [moved(): return lax.ppermute(value, EVERY, pairs)]
    dot_general x1 -> x0, matrix products: 7.67 us -> none  [on_device(): lax.dot_general(weights, groups, (((1,), (2,)), ((), ())), preferred_elem...]
    all_to_all x1 -> x2, waiting for transfers between devices: 9.84 us -> 16.3 us  [exchanged(): lax.all_to_all(copies, PLANE, split_axis=0, concat_axis=0, tiled=True)]
    all_to_all x1 -> x2, starting transfers between devices: 6.15 us -> 9.71 us  [exchanged(): lax.all_to_all(copies, PLANE, split_axis=0, concat_axis=0, tiled=True)]
    reduce_max x2 -> x0, other arithmetic: 3.49 us -> none  [the longest x1 3.47 us: on_device(): local_top = jnp.max(softened, axis=1)]
    add x5 -> x0, other arithmetic: 2.98 us -> none  [the longest x1 1.42 us: summed_at_owner(): own[HALF:] + after_b + before_b]
  transfers between devices with their start and end apart: 9 -> 10, of which waited for: 7 -> 7; matrix products, arithmetic and copies ran while one was open for 2% -> 1% of each run, Pallas kernels for 0% -> 2%
where the time goes in v2:
time: 118 us; the launch traced here: 117 us
  blocking collectives  40.8 us (35%)
  waiting for transfers between devices  36.5 us (31%)
  starting transfers between devices  22.8 us (19%)
  Pallas kernels  14.6 us (12%)
  other arithmetic  1.62 us (1%)
    all_to_all x2, blocking collectives, copies_from(): return lax.all_to_all(copies, axis, split_axis=0, concat_axis=0, tiled=True)  40.8 us
    ppermute x8, waiting for transfers between devices, moved(): return lax.ppermute(value, EVERY, pairs)  20.2 us
    all_to_all x2, waiting for transfers between devices, exchanged(): lax.all_to_all(copies, PLANE, split_axis=0, concat_axis=0, tiled=True)  16.3 us
    ppermute x8, starting transfers between devices, moved(): return lax.ppermute(value, EVERY, pairs)  13.1 us
    all_to_all x2, starting transfers between devices, exchanged(): lax.all_to_all(copies, PLANE, split_axis=0, concat_axis=0, tiled=True)  9.71 us
    pallas_call x1, Pallas kernels, products(): pl.pallas_call(product_kernel, out_shape=[code, code, code, code, half, h...  8.19 us
    pallas_call x1, Pallas kernels, scored(): pl.pallas_call(scores_kernel, out_shape=[full, line, jax.ShapeDtypeStruct...  2.37 us
  transfers between devices with their start and end apart: 10, of which 7 were waited for; matrix products, arithmetic and copies ran while one was open for 1% of the time, Pallas kernels for 2%

profile of v2, /device:TPU:1, one launch (start us, length us, event | category | flops | bytes accessed | tf_op | source)
XLA Modules:
  0.0 117.4 jit_solution(9180652179469243341)
XLA Ops:
  0.6 1.4 %collective-permute-start = (bf16[128,128]{1,0:T(8,128)(2,1)}, bf16[128,128]{1,0:T(8,128)(2,1)S(1)}, u32[]{:S(2)}, u32[]{:S(2)}) collective-permute-start(bf16[128,128]{1,0:T(8,128)(2,1)} %param.10), channel_id=1, source_target_pairs={{0,0},{1,1},{2,2},{3,3},{4,4},{5,5},{6,6},{7,7},{8,8},{9,9},{10,10... | collective-permute-start | bytes 98312 | tf_op jit(solution)/shard_map/ppermute | solution.py:39
  2.1 19.3 %all_to_all.20 = bf16[8,128,128]{2,1,0:T(8,128)(2,1)S(1)} all-to-all(bf16[8,128,128]{2,1,0:T(8,128)(2,1)S(1)} %broadcast_in_dim.24), channel_id=1, replica_groups=mesh['x'=4,'y'=4,'z'=8,'c'=2] {'z'}, dimensions={0} | all-to-all | bytes 524288 | tf_op jit(solution)/shard_map/all_to_all | solution.py:53
  21.6 21.5 %all_to_all.21.mine = bf16[4,8,128,128]{3,2,1,0:T(8,128)(2,1)S(1)} all-to-all(bf16[4,8,128,128]{3,2,1,0:T(8,128)(2,1)S(1)} %broadcast_in_dim.25), channel_id=1, replica_groups=mesh['x'=4,'y'=4,'z'=8,'c'=2] {'y'}, dimensions={0} | all-to-all | bytes 2097152 | tf_op jit(solution)/shard_map/all_to_all | solution.py:53
  43.1 4.7 %collective-permute-start.1 = (bf16[4,8,128,128]{3,2,1,0:T(8,128)(2,1)S(1)}, bf16[4,8,128,128]{3,2,1,0:T(8,128)(2,1)S(1)}, u32[]{:S(2)}, u32[]{:S(2)}) collective-permute-start(bf16[4,8,128,128]{3,2,1,0:T(8,128)(2,1)S(1)} %all_to_all.21.mine), channel_id=1, source_target_pairs={{0,1},{1,0},{2,3},{3,2},{4,5},{5,4},{6,7},{7,6},{8,9},{9,8},{10,11... | collective-permute-start | bytes 3145736 | tf_op jit(solution)/shard_map/ppermute | solution.py:39
  47.8 2.3 %collective-permute-done.1.other = bf16[4,8,128,128]{3,2,1,0:T(8,128)(2,1)S(1)} collective-permute-done((bf16[4,8,128,128]{3,2,1,0:T(8,128)(2,1)S(1)}, bf16[4,8,128,128]{3,2,1,0:T(8,128)(2,1)S(1)}, u32[]{:S(2)}, u32[]{:S(2)}) %collective-permute-start.1) | collective-permute-done | bytes 1048608 | tf_op jit(solution)/shard_map/ppermute | solution.py:39
  50.1 8.2 %products.1 = (s32[680,128]{1,0:T(8,128)S(1)}, s32[680,128]{1,0:T(8,128)S(1)}, s32[680,128]{1,0:T(8,128)S(1)}, s32[680,128]{1,0:T(8,128)S(1)}, f32[1008,128]{1,0...) custom-call(bf16[4,8,128,128]{3,2,1,0:T(8,128)(2,1)S(1)} %all_to_all.21.mine, ...), custom_call_target="tpu_custom_call" | custom-call | flops 4202692608 | bytes 8208384 | tf_op jit(solution)/shard_map/products/pallas_call | solution.py:151
  58.3 1.1 collective-permute-start.3
  59.4 1.6 %collective-permute-start.4 = (s32[680,128]{1,0:T(8,128)S(1)}, s32[680,128]{1,0:T(8,128)S(1)}, u32[]{:S(2)}, u32[]{:S(2)}) collective-permute-start(s32[680,128]{1,0:T(8,128)S(1)} %get-tuple-element.22), channel_id=1, source_target_pairs={{0,192},{1,193},{2,194},{3,195},{4,196},{5,197},{6,198},{7,199},{8... | collective-permute-start | bytes 1044488 | tf_op jit(solution)/shard_map/ppermute | solution.py:39
  61.1 1.4 %collective-permute-start.6 = (s32[680,128]{1,0:T(8,128)S(1)}, s32[680,128]{1,0:T(8,128)S(1)}, u32[]{:S(2)}, u32[]{:S(2)}) collective-permute-start(s32[680,128]{1,0:T(8,128)S(1)} %get-tuple-element.26), channel_id=1, source_target_pairs={{0,64},{1,65},{2,66},{3,67},{4,68},{5,69},{6,70},{7,71},{8,72},{9,... | collective-permute-start | bytes 1044488 | tf_op jit(solution)/shard_map/ppermute | solution.py:39
  62.5 6.4 %collective-permute-done.3.far_a = s32[680,128]{1,0:T(8,128)S(1)} collective-permute-done((s32[680,128]{1,0:T(8,128)S(1)}, s32[680,128]{1,0:T(8,128)S(1)}, u32[]{:S(2)}, u32[]{:S(2)}) %collective-permute-start.3) | collective-permute-done | bytes 348192 | tf_op jit(solution)/shard_map/ppermute | solution.py:39
  68.9 0.7 relayed.1
  69.7 2.7 %collective-permute-start.7 = (s32[680,128]{1,0:T(8,128)S(1)}, s32[680,128]{1,0:T(8,128)S(1)}, u32[]{:S(2)}, u32[]{:S(2)}) collective-permute-start(s32[680,128]{1,0:T(8,128)S(1)} %get-tuple-element.27), channel_id=1, source_target_pairs={{0,192},{1,193},{2,194},{3,195},{4,196},{5,197},{6,198},{7,199},{8... | collective-permute-start | bytes 1044488 | tf_op jit(solution)/shard_map/ppermute | solution.py:39
  72.4 3.6 %collective-permute-done.2.a_one = s32[680,128]{1,0:T(8,128)S(1)} collective-permute-done((s32[680,128]{1,0:T(8,128)S(1)}, s32[680,128]{1,0:T(8,128)S(1)}, u32[]{:S(2)}, u32[]{:S(2)}) %collective-permute-start.2) | collective-permute-done | bytes 348192 | tf_op jit(solution)/shard_map/ppermute | solution.py:39
  75.9 0.5 collective-permute-done.6.b_one
  76.4 7.5 %collective-permute-done.5.a_two = s32[680,128]{1,0:T(8,128)S(1)} collective-permute-done((s32[680,128]{1,0:T(8,128)S(1)}, s32[680,128]{1,0:T(8,128)S(1)}, u32[]{:S(2)}, u32[]{:S(2)}) %collective-permute-start.5) | collective-permute-done | bytes 348192 | tf_op jit(solution)/shard_map/ppermute | solution.py:39
  83.9 2.4 %scored.1 = (f32[2004,128]{1,0:T(8,128)S(1)}, f32[1,128]{1,0:T(1,128)S(1)}, f32[64,2,128]{2,1,0:T(2,128)}) custom-call(f32[2016,128]{1,0:T(8,128)S(1)} %get-tuple-element.19.own, s32[680,128]{1,0:T(8,128)S(1)} %collective-permute-done.2.a_one, s32[680,128]{1,0:T(8,128)S(1)} %collective-permute-done.5.a_two, s32[680,128]{1,0:T(8,128)S(1)} %collective-permute-done.6.b_one, ...), custom_call_target="tpu_custom_call" | custom-call | flops 7695360 | bytes 6156288 | tf_op jit(solution)/shard_map/scored/pallas_call | solution.py:256
  86.3 5.3 %all-to-all-start.2 = ((f32[64,2,128]{2,1,0:T(2,128)}), f32[64,2,128]{2,1,0:T(2,128)S(1)}, u32[]{:S(2)}, u32[]{:S(2)}) async-start(f32[64,2,128]{2,1,0:T(2,128)} %get-tuple-element.31), calls=%async_computation.2 | async-start | bytes 131072 | tf_op jit(solution)/shard_map/all_to_all | solution.py:57
  91.6 1.9 %prefixes.1 = (f32[2004,128]{1,0:T(8,128)S(1)}, s32[2004,128]{1,0:T(8,128)}) custom-call(f32[2004,128]{1,0:T(8,128)S(1)} %get-tuple-element.28.scores, f32[1,128]{1,0:T(1,128)S(1)} %get-tuple-element.29.line, s32[2004,128]{1,0:T(8,128)S(1)} %bitcast.14, s32[1,128]{1,0:T(1,128)S(1)} %bitcast.17), custom_call_target="tpu_custom_call" | custom-call | flops 102604800 | bytes 2052096 | tf_op jit(solution)/shard_map/prefixes/pallas_call | solution.py:292
  93.6 7.9 %all-to-all-done.2.stats = f32[64,2,128]{2,1,0:T(2,128)S(1)} async-done(((f32[64,2,128]{2,1,0:T(2,128)}), f32[64,2,128]{2,1,0:T(2,128)S(1)}, u32[]{:S(2)}, u32[]{:S(2)}) %all-to-all-start.2) | async-done | bytes 65568 | tf_op jit(solution)/shard_map/all_to_all | solution.py:57
  101.5 1.5 %quantiles.1 = (f32[64,1,128]{2,1,0:T(1,128)}, f32[1,128]{1,0:T(1,128)S(1)}) custom-call(f32[64,2,128]{2,1,0:T(2,128)S(1)} %all-to-all-done.2.stats, f32[1,128]{1,0:T(1,128)S(1)} %get-tuple-element.29.line, f32[1,128]{1,0:T(1,128)S(1)} %bitcast.23, f32[2004,128]{1,0:T(8,128)S(1)} %get-tuple-element.28.scores, f32[2004,128]{1,0:T(8,128)S(1)} %get-tuple-element.32.before), custom_call_target="tpu_custom_call" | custom-call | flops 2565120 | bytes 2052096 | tf_op jit(solution)/shard_map/quantiles/pallas_call | solution.py:337
  103.0 4.4 %all-to-all-start.3 = ((f32[64,1,128]{2,1,0:T(1,128)}), f32[64,1,128]{2,1,0:T(1,128)S(1)}, u32[]{:S(2)}, u32[]{:S(2)}) async-start(f32[64,1,128]{2,1,0:T(1,128)} %get-tuple-element.34), calls=%async_computation.3 | async-start | bytes 65536 | tf_op jit(solution)/shard_map/all_to_all | solution.py:57
  107.4 1.0 subtract_bitcast_fusion
  108.4 8.4 %all-to-all-done.3 = f32[64,1,128]{2,1,0:T(1,128)S(1)} async-done(((f32[64,1,128]{2,1,0:T(1,128)}), f32[64,1,128]{2,1,0:T(1,128)S(1)}, u32[]{:S(2)}, u32[]{:S(2)}) %all-to-all-start.3) | async-done | bytes 32800 | tf_op jit(solution)/shard_map/all_to_all | solution.py:57
  116.8 0.6 reduce_sum.9
  (23 shorter events, 0.4 us)
Async XLA Ops:
  0.6 1.4 %collective-permute-start = (bf16[128,128]{1,0:T(8,128)(2,1)}, bf16[128,128]{1,0:T(8,128)(2,1)S(1)}, u32[]{:S(2)}, u32[]{:S(2)}) collective-permute-start(bf16[128,128]{1,0:T(8,128)(2,1)} %param.10), channel_id=1, source_target_pairs={{0,0},{1,1},{2,2},{3,3},{4,4},{5,5},{6,6},{7,7},{8,8},{9,9},{10,10... | collective-permute-start | bytes 98312 | tf_op jit(solution)/shard_map/ppermute | solution.py:39
  43.1 7.0 %collective-permute-start.1 = (bf16[4,8,128,128]{3,2,1,0:T(8,128)(2,1)S(1)}, bf16[4,8,128,128]{3,2,1,0:T(8,128)(2,1)S(1)}, u32[]{:S(2)}, u32[]{:S(2)}) collective-permute-start(bf16[4,8,128,128]{3,2,1,0:T(8,128)(2,1)S(1)} %all_to_all.21.mine), channel_id=1, source_target_pairs={{0,1},{1,0},{2,3},{3,2},{4,5},{5,4},{6,7},{7,6},{8,9},{9,8},{10,11... | collective-permute-start | bytes 3145736 | tf_op jit(solution)/shard_map/ppermute | solution.py:39
  50.1 33.8 %copy-start = (s32[128,2004]{0,1:T(8,128)S(1)}, s32[128,2004]{0,1:T(8,128)}, u32[]{:S(2)}) copy-start(s32[128,2004]{0,1:T(8,128)} %param.13) | copy-start | bytes 3078148
  50.1 33.8 %copy-start.1 = (s32[128,2004]{0,1:T(8,128)S(1)}, s32[128,2004]{0,1:T(8,128)}, u32[]{:S(2)}) copy-start(s32[128,2004]{0,1:T(8,128)} %param.12) | copy-start | bytes 3078148
  50.1 33.8 %copy-start.2 = (s32[128]{0:T(128)S(1)}, s32[128]{0:T(128)}, u32[]{:S(2)}) copy-start(s32[128]{0:T(128)} %param.14) | copy-start | bytes 1540
  50.1 33.8 %copy-start.3 = (f32[128]{0:T(128)S(1)}, f32[128]{0:T(128)}, u32[]{:S(2)}) copy-start(f32[128]{0:T(128)} %param.15) | copy-start | bytes 1540
  50.1 33.8 %copy-start.4 = (f32[128]{0:T(128)S(1)}, f32[128]{0:T(128)}, u32[]{:S(2)}) copy-start(f32[128]{0:T(128)} %param.16) | copy-start | bytes 1540
  50.1 33.8 %copy-start.5 = (f32[128]{0:T(128)S(1)}, f32[128]{0:T(128)}, u32[]{:S(2)}) copy-start(f32[128]{0:T(128)} %param.17) | copy-start | bytes 1540
  50.1 33.8 %copy-start.6 = (f32[128]{0:T(128)S(1)}, f32[128]{0:T(128)}, u32[]{:S(2)}) copy-start(f32[128]{0:T(128)} %param.18) | copy-start | bytes 1540
  50.1 51.4 %copy-start.7 = (f32[128]{0:T(128)S(1)}, f32[128]{0:T(128)}, u32[]{:S(2)}) copy-start(f32[128]{0:T(128)} %param.19) | copy-start | bytes 1540
  58.3 10.6 %collective-permute-start.3 = (s32[680,128]{1,0:T(8,128)S(1)}, s32[680,128]{1,0:T(8,128)S(1)}, u32[]{:S(2)}, u32[]{:S(2)}) collective-permute-start(s32[680,128]{1,0:T(8,128)S(1)} %get-tuple-element.21), channel_id=1, source_target_pairs={{0,64},{1,65},{2,66},{3,67},{4,68},{5,69},{6,70},{7,71},{8,72},{9,... | collective-permute-start | bytes 1044488 | tf_op jit(solution)/shard_map/ppermute | solution.py:39
  59.4 9.5 %collective-permute-start.4 = (s32[680,128]{1,0:T(8,128)S(1)}, s32[680,128]{1,0:T(8,128)S(1)}, u32[]{:S(2)}, u32[]{:S(2)}) collective-permute-start(s32[680,128]{1,0:T(8,128)S(1)} %get-tuple-element.22), channel_id=1, source_target_pairs={{0,192},{1,193},{2,194},{3,195},{4,196},{5,197},{6,198},{7,199},{8... | collective-permute-start | bytes 1044488 | tf_op jit(solution)/shard_map/ppermute | solution.py:39
  61.1 14.9 %collective-permute-start.2 = (s32[680,128]{1,0:T(8,128)S(1)}, s32[680,128]{1,0:T(8,128)S(1)}, u32[]{:S(2)}, u32[]{:S(2)}) collective-permute-start(s32[680,128]{1,0:T(8,128)S(1)} %get-tuple-element.20), channel_id=1, source_target_pairs={{0,192},{1,193},{2,194},{3,195},{4,196},{5,197},{6,198},{7,199},{8... | collective-permute-start | bytes 1044488 | tf_op jit(solution)/shard_map/ppermute | solution.py:39
  61.1 15.3 %collective-permute-start.6 = (s32[680,128]{1,0:T(8,128)S(1)}, s32[680,128]{1,0:T(8,128)S(1)}, u32[]{:S(2)}, u32[]{:S(2)}) collective-permute-start(s32[680,128]{1,0:T(8,128)S(1)} %get-tuple-element.26), channel_id=1, source_target_pairs={{0,64},{1,65},{2,66},{3,67},{4,68},{5,69},{6,70},{7,71},{8,72},{9,... | collective-permute-start | bytes 1044488 | tf_op jit(solution)/shard_map/ppermute | solution.py:39
  69.6 14.3 %collective-permute-start.5 = (s32[680,128]{1,0:T(8,128)S(1)}, s32[680,128]{1,0:T(8,128)S(1)}, u32[]{:S(2)}, u32[]{:S(2)}) collective-permute-start(s32[680,128]{1,0:T(8,128)S(1)} %get-tuple-element.25), channel_id=1, source_target_pairs={{0,64},{1,65},{2,66},{3,67},{4,68},{5,69},{6,70},{7,71},{8,72},{9,... | collective-permute-start | bytes 1044488 | tf_op jit(solution)/shard_map/ppermute | solution.py:39
  69.7 14.2 %collective-permute-start.7 = (s32[680,128]{1,0:T(8,128)S(1)}, s32[680,128]{1,0:T(8,128)S(1)}, u32[]{:S(2)}, u32[]{:S(2)}) collective-permute-start(s32[680,128]{1,0:T(8,128)S(1)} %get-tuple-element.27), channel_id=1, source_target_pairs={{0,192},{1,193},{2,194},{3,195},{4,196},{5,197},{6,198},{7,199},{8... | collective-permute-start | bytes 1044488 | tf_op jit(solution)/shard_map/ppermute | solution.py:39
  86.3 15.2 %all-to-all-start.2 = ((f32[64,2,128]{2,1,0:T(2,128)}), f32[64,2,128]{2,1,0:T(2,128)S(1)}, u32[]{:S(2)}, u32[]{:S(2)}) async-start(f32[64,2,128]{2,1,0:T(2,128)} %get-tuple-element.31), calls=%async_computation.2 | async-start | bytes 131072 | tf_op jit(solution)/shard_map/all_to_all | solution.py:57
  103.0 13.8 %all-to-all-start.3 = ((f32[64,1,128]{2,1,0:T(1,128)}), f32[64,1,128]{2,1,0:T(1,128)S(1)}, u32[]{:S(2)}, u32[]{:S(2)}) async-start(f32[64,1,128]{2,1,0:T(1,128)} %get-tuple-element.34), calls=%async_computation.3 | async-start | bytes 65536 | tf_op jit(solution)/shard_map/all_to_all | solution.py:57

commit v3 on v2

--- a/solution.py
+++ b/solution.py
@@ -19,7 +19,7 @@
 THIRD = HALF // 3
 CHUNK = 56
 STEPS = THIRD // CHUNK
-BLOCKS = ((0, 256), (256, 512), (768, 512), (1280, ROWS - 1280))
+BLOCKS = ((0, 512), (512, 512), (1024, 512), (1536, ROWS - 1536))
 CODED = 2 * THIRD + 8
 BITS = 20
 
@@ -106,97 +106,175 @@
     return (lax.axis_index("y") * NZ + lax.axis_index("z")) * NC + lax.axis_index("c")
 
 
-def product_kernel(
-    mine, other, source, far_a, far_b, after_b, before_a, after_a, before_b, own, weights, rows, part, here
-):
+def slot_of(r):
+    return lax.rem(lax.axis_index("x") + r + NY - lax.axis_index("y"), NY)
+
+
+def fetch_kernel(source, out, here):
     copies = [
-        pltpu.make_async_copy(source.at[pl.ds(start, size)], weights.at[pl.ds(start, size)], here.at[n])
+        pltpu.make_async_copy(source.at[pl.ds(start, size)], out.at[pl.ds(start, size)], here.at[n])
         for n, (start, size) in enumerate(BLOCKS)
     ]
     for copy in copies:
         copy.start()
-    x, c = lax.axis_index("x"), lax.axis_index("c")
-    for r in range(NX):
-        group = lax.rem(x + r, NX)
-        for z in range(NZ):
-            at = pl.ds(r * LANES, LANES)
-            rows[at, pl.ds(pl.multiple_of((2 * z + c) * 128, 128), 128)] = mine[group, z]
-            rows[at, pl.ds(pl.multiple_of((2 * z + 1 - c) * 128, 128), 128)] = other[group, z]
-
-    for (start, size), copy in zip(BLOCKS, copies):
+    for copy in copies:
         copy.wait()
-        part[pl.ds(start, size), :] = lax.dot_general(
-            weights[pl.ds(start, size), :],
-            rows[...],
-            (((1,), (1,)), ((), ())),
-            preferred_element_type=jnp.float32,
+
+
+def fetched(weights):
+    return pl.pallas_call(
+        fetch_kernel,
+        out_shape=jax.ShapeDtypeStruct(weights.shape, weights.dtype),
+        in_specs=[pl.BlockSpec(memory_space=pltpu.HBM)],
+        out_specs=WHOLE,
+        scratch_shapes=[pltpu.SemaphoreType.DMA((len(BLOCKS),))],
+        compiler_params=pltpu.CompilerParams(vmem_limit_bytes=44 << 20),
+        cost_estimate=pl.CostEstimate(flops=ROWS * DEPTH * 512, bytes_accessed=ROWS * DEPTH * 4, transcendentals=0),
+        name="fetched",
+    )(weights)
+
+
+def lay_out(rows, row, block, core):
+    for z in range(NZ):
+        at = pl.ds(pl.multiple_of((2 * z + core) * 128, 128), 128)
+        rows[pl.ds(pl.multiple_of(row, 128), LANES), at] = block[z]
+
+
+def multiplied(weights, rows, put):
+    for start, size in BLOCKS:
+        put(
+            start,
+            size,
+            lax.dot_general(
+                weights[pl.ds(start, size), :],
+                rows[...],
+                (((1,), (1,)), ((), ())),
+                preferred_element_type=jnp.float32,
+            ),
         )
-    part[ROWS : 2 * HALF, :] = jnp.zeros((2 * HALF - ROWS, NX * LANES), jnp.float32)
-
-    def load(r, half):
-        return lambda start: part[pl.ds(aligned(half * HALF + start), CHUNK), pl.ds(r * LANES, LANES)]
-
-    coded(load(2, 0), far_a)
-    coded(load(2, 1), far_b)
-    coded(load(1, 1), after_b)
-    coded(load(3, 0), before_a)
-    after_a[...] = part[0:HALF, LANES : 2 * LANES]
-    before_b[...] = part[HALF : 2 * HALF, 3 * LANES :]
-    own[...] = part[0 : 2 * HALF, 0:LANES]
-
-
-def products(mine, other, weights):
-    code = jax.ShapeDtypeStruct((CODED, LANES), jnp.int32)
-    half = jax.ShapeDtypeStruct((HALF, LANES), jnp.float32)
-    return pl.pallas_call(
-        product_kernel,
-        out_shape=[code, code, code, code, half, half, jax.ShapeDtypeStruct((2 * HALF, LANES), jnp.float32)],
-        in_specs=[WHOLE, WHOLE, pl.BlockSpec(memory_space=pltpu.HBM)],
-        out_specs=[WHOLE] * 7,
-        scratch_shapes=[
-            pltpu.VMEM((ROWS, DEPTH), jnp.bfloat16),
-            pltpu.VMEM((NX * LANES, DEPTH), jnp.bfloat16),
-            pltpu.VMEM((2 * HALF, NX * LANES), jnp.float32),
-            pltpu.SemaphoreType.DMA((len(BLOCKS),)),
-        ],
-        compiler_params=pltpu.CompilerParams(vmem_limit_bytes=44 << 20),
-        cost_estimate=pl.CostEstimate(flops=2 * ROWS * 512 * DEPTH, bytes_accessed=ROWS * DEPTH * 2, transcendentals=0),
-        name="products",
-    )(mine, other, weights)
-
-
-def relay_kernel(far_a, far_b, after_a, before_b, after_out, before_out, total):
-    for far, own, out in ((far_a, after_a, after_out), (far_b, before_b, before_out)):
+
+
+def clear_tail(parts, slot):
+    parts[slot, ROWS : 2 * HALF, :] = jnp.zeros((2 * HALF - ROWS, LANES), jnp.float32)
+
+
+def first_kernel(mine, other, weights, parts, rows):
+    c = lax.axis_index("c")
+    lay_out(rows, 0, mine, c)
+    lay_out(rows, 0, other, 1 - c)
+
+    def put(start, size, value):
+        parts[0, pl.ds(start, size), :] = value
+
+    multiplied(weights, rows, put)
+    clear_tail(parts, 0)
+
+
+def second_kernel(one, two, other_one, other_two, weights, given, parts, rows):
+    c = lax.axis_index("c")
+    lay_out(rows, c * LANES, one, c)
+    lay_out(rows, (1 - c) * LANES, two, c)
+    lay_out(rows, (1 - c) * LANES, other_one, 1 - c)
+    lay_out(rows, c * LANES, other_two, 1 - c)
+
+    def put(start, size, value):
+        parts[3, pl.ds(start, size), :] = value[:, :LANES]
+        parts[1, pl.ds(start, size), :] = value[:, LANES:]
+
+    multiplied(weights, rows, put)
+    clear_tail(parts, 3)
+    clear_tail(parts, 1)
+
+
+def part_of(parts, r, half):
+    slot = slot_of(r)
+    return lambda start: parts[slot, pl.ds(aligned(half * HALF + start), CHUNK), :]
+
+
+def third_kernel(mine, other, weights, given, parts, far_a, far_b, rows):
+    c = lax.axis_index("c")
+    lay_out(rows, 0, mine, c)
+    lay_out(rows, 0, other, 1 - c)
+
+    def put(start, size, value):
+        parts[2, pl.ds(start, size), :] = value
+
+    multiplied(weights, rows, put)
+    clear_tail(parts, 2)
+    coded(part_of(parts, 2, 0), far_a)
+    coded(part_of(parts, 2, 1), far_b)
+
+
+def near_kernel(parts, after_b, before_a):
+    coded(part_of(parts, 1, 1), after_b)
+    coded(part_of(parts, 3, 0), before_a)
+
+
+PARTS = jax.ShapeDtypeStruct((NY, 2 * HALF, LANES), jnp.float32)
+CODE = jax.ShapeDtypeStruct((CODED, LANES), jnp.int32)
+
+
+def multiply(kernel, groups, extra, *args):
+    given = len(args) - 1 if kernel is not first_kernel else None
+    return pl.pallas_call(
+        kernel,
+        out_shape=[PARTS] + extra,
+        in_specs=[WHOLE] * len(args),
+        out_specs=[WHOLE] * (1 + len(extra)),
+        scratch_shapes=[pltpu.VMEM((groups * LANES, DEPTH), jnp.bfloat16)],
+        input_output_aliases={} if given is None else {given: 0},
+        compiler_params=pltpu.CompilerParams(vmem_limit_bytes=12 << 20),
+        cost_estimate=pl.CostEstimate(
+            flops=2 * ROWS * 256 * DEPTH, bytes_accessed=ROWS * DEPTH * 2, transcendentals=0
+        ),
+    )(*args)
+
+
+def near(parts):
+    return pl.pallas_call(
+        near_kernel,
+        out_shape=[CODE, CODE],
+        in_specs=[WHOLE],
+        out_specs=[WHOLE] * 2,
+        compiler_params=pltpu.CompilerParams(vmem_limit_bytes=8 << 20),
+        cost_estimate=pl.CostEstimate(flops=20 * HALF * LANES, bytes_accessed=4 * HALF * LANES * 4, transcendentals=0),
+        name="near",
+    )(parts)
+
+
+def relay_kernel(far_a, far_b, parts, after_out, before_out, total):
+    for r, half, far, out in ((1, 0, far_a, after_out), (3, 1, far_b, before_out)):
         step = step_of(far)
+        own = part_of(parts, r, half)
 
         def add(j, carry):
             for third, value in enumerate(decoded(far, step, j)):
-                at = pl.ds(aligned(third * THIRD + j * CHUNK), CHUNK)
-                total[at, :] = own[at, :] + value
+                start = third * THIRD + j * CHUNK
+                total[pl.ds(aligned(start), CHUNK), :] = own(start) + value
             return carry
 
         lax.fori_loop(0, STEPS, add, 0)
         coded(lambda start: total[pl.ds(aligned(start), CHUNK), :], out)
 
 
-def relayed(far_a, far_b, after_a, before_b):
-    code = jax.ShapeDtypeStruct((CODED, LANES), jnp.int32)
+def relayed(far_a, far_b, parts):
     return pl.pallas_call(
         relay_kernel,
-        out_shape=[code, code],
-        in_specs=[WHOLE] * 4,
+        out_shape=[CODE, CODE],
+        in_specs=[WHOLE] * 3,
         out_specs=[WHOLE] * 2,
         scratch_shapes=[pltpu.VMEM((HALF, LANES), jnp.float32)],
-        compiler_params=pltpu.CompilerParams(vmem_limit_bytes=16 << 20),
+        compiler_params=pltpu.CompilerParams(vmem_limit_bytes=8 << 20),
         cost_estimate=pl.CostEstimate(flops=20 * HALF * LANES, bytes_accessed=4 * HALF * LANES * 4, transcendentals=0),
         name="relayed",
-    )(far_a, far_b, after_a, before_b)
+    )(far_a, far_b, parts)
 
 
 def scores_kernel(
-    own, a_one, a_two, b_one, b_two, context, emitted, fresh, divisor, fine, appearance, softness,
+    parts, a_one, a_two, b_one, b_two, context, emitted, fresh, divisor, fine, appearance, softness,
     scores, line, copies,
 ):
+    slot = slot_of(0)
     factor = divisor[...]
     inverse = 1.0 / factor
     per_count = fine[...]
@@ -210,7 +288,7 @@
             size = sizes[third]
             start = half * HALF + third * THIRD + j * CHUNK
             at = pl.ds(aligned(start), size)
-            logits = own[at, :] + one[:size] + two[:size]
+            logits = parts[slot, at, :] + one[:size] + two[:size]
             ids = start + lax.broadcasted_iota(jnp.int32, (size, LANES), 0)
             counts = emitted[at, :] + (ids == newest).astype(jnp.int32)
             seen = context[at, :] + counts > 0
@@ -348,7 +426,7 @@
     )(*args)
 
 
-def on_device(
+def step(
     final_activation,
     output_projection_weights,
     context_word_tallies,
@@ -365,19 +443,37 @@
 
     mine = moved(final_activation, lambda x, y, z, c: (y, x, z, c))
     mine = copies_from(mine, "z")
-    mine = copies_from(mine, "y")
-    other = moved(mine, lambda x, y, z, c: (x, y, z, 1 - c))
-    far_a, far_b, after_b, before_a, after_a, before_b, own = products(
-        mine, other, output_projection_weights.T
-    )
-
-    far_a, far_b = up(far_a), down(far_b)
+
+    def partner(value):
+        return moved(value, lambda x, y, z, c: (x, y, z, 1 - c))
+
+    def onward(value):
+        return moved(value, lambda x, y, z, c: (x, y + 1 - 2 * c, z, c))
+
+    def backward(value):
+        return moved(value, lambda x, y, z, c: (x, y - 1 + 2 * c, z, c))
+
+    other = partner(mine)
+    one = onward(mine)
+    two = backward(mine)
+    weights = fetched(output_projection_weights.T)
+    last = onward(one)
+    other_one = partner(one)
+    other_two = partner(two)
+    (parts,) = multiply(first_kernel, 1, [], mine, other, weights)
+    (parts,) = multiply(second_kernel, 2, [], one, two, other_one, other_two, weights, parts)
+    other_last = partner(last)
+    parts, far_a, far_b = multiply(third_kernel, 1, [CODE, CODE], last, other_last, weights, parts)
+
+    far_a = up(far_a)
+    far_b = down(far_b)
+    after_b, before_a = near(parts)
     b_one, a_one = up(after_b), down(before_a)
-    after_a, before_b = relayed(far_a, far_b, after_a, before_b)
+    after_a, before_b = relayed(far_a, far_b, parts)
     a_two, b_two = up(after_a), down(before_b)
 
     scores, local_top, copies = scored(
-        own,
+        parts,
         a_one,
         a_two,
         b_one,
@@ -404,7 +500,7 @@
     whole = P("x", PLANE)
     row = P("x")
     return jax.shard_map(
-        on_device,
+        step,
         mesh=split,
         in_specs=(whole, whole, whole, whole, row, row, row, row, row, row),
         out_specs=(whole, whole, row),

time: 118 us -> 115 us (0.975)
  blocking collectives: 40.8 us -> 19.3 us
  starting transfers between devices: 22.8 us -> 37.7 us
  Pallas kernels: 14.6 us -> 18.1 us
    all_to_all x2 -> x1, blocking collectives: 40.8 us -> 19.3 us  [copies_from(): return lax.all_to_all(copies, axis, split_axis=0, concat_axis=0, tiled=True)]
    ppermute x8 -> x14, starting transfers between devices: 13.1 us -> 28.1 us  [moved(): return lax.ppermute(value, EVERY, pairs)]
    pallas_call x2 -> x6, Pallas kernels: 8.85 us -> 12.3 us  [the longest x3 7.8 us: multiply(): pl.pallas_call(kernel, out_shape=[PARTS] + extra, in_specs=[WHOLE] * len(...]
    ppermute x8 -> x14, waiting for transfers between devices: 20.2 us -> 21.2 us  [moved(): return lax.ppermute(value, EVERY, pairs)]
  transfers between devices with their start and end apart: 10 -> 16, of which waited for: 7 -> 7; matrix products, arithmetic and copies ran while one was open for 1% -> 1% of each run, Pallas kernels for 2% -> 10%
where the time goes in v3:
time: 115 us
  starting transfers between devices  37.7 us (33%)
  waiting for transfers between devices  37.5 us (33%)
  blocking collectives  19.3 us (17%)
  Pallas kernels  18.1 us (16%)
  other arithmetic  1.62 us (1%)
    ppermute x14, starting transfers between devices, moved(): return lax.ppermute(value, EVERY, pairs)  28.1 us
    ppermute x14, waiting for transfers between devices, moved(): return lax.ppermute(value, EVERY, pairs)  21.2 us
    all_to_all x1, blocking collectives, copies_from(): return lax.all_to_all(copies, axis, split_axis=0, concat_axis=0, tiled=True)  19.3 us
    all_to_all x2, waiting for transfers between devices, exchanged(): lax.all_to_all(copies, PLANE, split_axis=0, concat_axis=0, tiled=True)  16.3 us
    all_to_all x2, starting transfers between devices, exchanged(): lax.all_to_all(copies, PLANE, split_axis=0, concat_axis=0, tiled=True)  9.59 us
    pallas_call x3, Pallas kernels, multiply(): pl.pallas_call(kernel, out_shape=[PARTS] + extra, in_specs=[WHOLE] * len(...  7.8 us
    pallas_call x1, Pallas kernels, fetched(): pl.pallas_call(fetch_kernel, out_shape=jax.ShapeDtypeStruct(weights.shape...  3.44 us
    pallas_call x1, Pallas kernels, scored(): pl.pallas_call(scores_kernel, out_shape=[full, line, jax.ShapeDtypeStruct...  2.38 us
  transfers between devices with their start and end apart: 16, of which 7 were waited for; matrix products, arithmetic and copies ran while one was open for 1% of the time, Pallas kernels for 10%

profile of v3, /device:TPU:1, one launch (start us, length us, event | category | flops | bytes accessed | tf_op | source)
XLA Modules:
  0.0 115.1 jit_solution(11475051348008003461)
XLA Ops:
  0.6 1.4 %collective-permute-start = (bf16[128,128]{1,0:T(8,128)(2,1)}, bf16[128,128]{1,0:T(8,128)(2,1)S(1)}, u32[]{:S(2)}, u32[]{:S(2)}) collective-permute-start(bf16[128,128]{1,0:T(8,128)(2,1)} %param.10), channel_id=1, source_target_pairs={{0,0},{1,1},{2,2},{3,3},{4,4},{5,5},{6,6},{7,7},{8,8},{9,9},{10,10... | collective-permute-start | bytes 98312 | tf_op jit(solution)/shard_map/ppermute | solution.py:39
  2.1 19.3 %all_to_all.15.mine = bf16[8,128,128]{2,1,0:T(8,128)(2,1)S(1)} all-to-all(bf16[8,128,128]{2,1,0:T(8,128)(2,1)S(1)} %broadcast_in_dim.21), channel_id=1, replica_groups=mesh['x'=4,'y'=4,'z'=8,'c'=2] {'z'}, dimensions={0} | all-to-all | bytes 524288 | tf_op jit(solution)/shard_map/all_to_all | solution.py:53
  21.4 8.3 %collective-permute-start.1 = (bf16[8,128,128]{2,1,0:T(8,128)(2,1)S(1)}, bf16[8,128,128]{2,1,0:T(8,128)(2,1)S(1)}, u32[]{:S(2)}, u32[]{:S(2)}) collective-permute-start(bf16[8,128,128]{2,1,0:T(8,128)(2,1)S(1)} %all_to_all.15.mine), channel_id=1, source_target_pairs={{0,16},{1,49},{2,18},{3,51},{4,20},{5,53},{6,22},{7,55},{8,24},{9,... | collective-permute-start | bytes 786440 | tf_op jit(solution)/shard_map/ppermute | solution.py:39
  29.7 3.3 %collective-permute-done.1.one = bf16[8,128,128]{2,1,0:T(8,128)(2,1)S(1)} collective-permute-done((bf16[8,128,128]{2,1,0:T(8,128)(2,1)S(1)}, bf16[8,128,128]{2,1,0:T(8,128)(2,1)S(1)}, u32[]{:S(2)}, u32[]{:S(2)}) %collective-permute-start.1) | collective-permute-done | bytes 262176 | tf_op jit(solution)/shard_map/ppermute | solution.py:39
  33.0 3.1 %collective-permute-start.2 = (bf16[8,128,128]{2,1,0:T(8,128)(2,1)S(1)}, bf16[8,128,128]{2,1,0:T(8,128)(2,1)S(1)}, u32[]{:S(2)}, u32[]{:S(2)}) collective-permute-start(bf16[8,128,128]{2,1,0:T(8,128)(2,1)S(1)} %collective-permute-done.1.one), channel_id=1, source_target_pairs={{0,16},{1,49},{2,18},{3,51},{4,20},{5,53},{6,22},{7,55},{8,24},{9,... | collective-permute-start | bytes 786440 | tf_op jit(solution)/shard_map/ppermute | solution.py:39
  36.1 3.5 %collective-permute-start.7 = (bf16[8,128,128]{2,1,0:T(8,128)(2,1)S(1)}, bf16[8,128,128]{2,1,0:T(8,128)(2,1)S(1)}, u32[]{:S(2)}, u32[]{:S(2)}) collective-permute-start(bf16[8,128,128]{2,1,0:T(8,128)(2,1)S(1)} %all_to_all.15.mine), channel_id=1, source_target_pairs={{0,1},{1,0},{2,3},{3,2},{4,5},{5,4},{6,7},{7,6},{8,9},{9,8},{10,11... | collective-permute-start | bytes 786440 | tf_op jit(solution)/shard_map/ppermute | solution.py:39
  39.6 1.5 %collective-permute-start.6 = (bf16[8,128,128]{2,1,0:T(8,128)(2,1)S(1)}, bf16[8,128,128]{2,1,0:T(8,128)(2,1)S(1)}, u32[]{:S(2)}, u32[]{:S(2)}) collective-permute-start(bf16[8,128,128]{2,1,0:T(8,128)(2,1)S(1)} %collective-permute-done.4.two), channel_id=1, source_target_pairs={{0,1},{1,0},{2,3},{3,2},{4,5},{5,4},{6,7},{7,6},{8,9},{9,8},{10,11... | collective-permute-start | bytes 786440 | tf_op jit(solution)/shard_map/ppermute | solution.py:39
  41.1 3.4 %fetched.1.weights = bf16[2004,2048]{1,0:T(8,128)(2,1)S(1)} custom-call(bf16[2004,2048]{1,0:T(8,128)(2,1)} %bitcast.24), custom_call_target="tpu_custom_call" | custom-call | flops 2101346304 | bytes 16416768 | tf_op jit(solution)/shard_map/fetched/pallas_call | solution.py:125
  44.5 2.7 %collective-permute-start.3 = (bf16[8,128,128]{2,1,0:T(8,128)(2,1)S(1)}, bf16[8,128,128]{2,1,0:T(8,128)(2,1)S(1)}, u32[]{:S(2)}, u32[]{:S(2)}) collective-permute-start(bf16[8,128,128]{2,1,0:T(8,128)(2,1)S(1)} %collective-permute-done.2.mine), channel_id=1, source_target_pairs={{0,1},{1,0},{2,3},{3,2},{4,5},{5,4},{6,7},{7,6},{8,9},{9,8},{10,11... | collective-permute-start | bytes 786440 | tf_op jit(solution)/shard_map/ppermute | solution.py:39
  47.2 2.4 %shard_map.121.given = f32[4,2016,128]{2,1,0:T(8,128)S(1)} custom-call(bf16[8,128,128]{2,1,0:T(8,128)(2,1)S(1)} %all_to_all.15.mine, bf16[8,128,128]{2,1,0:T(8,128)(2,1)S(1)} %collective-permute-done.7.other, bf16[2004,2048]{1,0:T(8,128)(2,1)S(1)} %fetched.1.weights), custom_call_target="tpu_custom_call" | custom-call | flops 2101346304 | bytes 8208384 | tf_op jit(solution)/shard_map/pallas_call | solution.py:219
  49.6 2.6 %shard_map.122.given = f32[4,2016,128]{2,1,0:T(8,128)S(1)} custom-call(bf16[8,128,128]{2,1,0:T(8,128)(2,1)S(1)} %collective-permute-done.1.one, bf16[8,128,128]{2,1,0:T(8,128)(2,1)S(1)} %collective-permute-done.4.two, bf16[8,128,128]{2,1,0:T(8,128)(2,1)S(1)} %collective-permute-done.5.other_one, ...), custom_call_target="tpu_custom_call", output_to_operand_aliasing={{}: (5, {})} | custom-call | flops 2101346304 | bytes 8208384 | tf_op jit(solution)/shard_map/pallas_call | solution.py:219
  52.2 2.8 %shard_map.123 = (f32[4,2016,128]{2,1,0:T(8,128)S(1)}, s32[680,128]{1,0:T(8,128)S(1)}, s32[680,128]{1,0:T(8,128)S(1)}) custom-call(bf16[8,128,128]{2,1,0:T(8,128)(2,1)S(1)} %collective-permute-done.2.mine, bf16[8,128,128]{2,1,0:T(8,128)(2,1)S(1)} %collective-permute-done.3.other, ...), custom_call_target="tpu_custom_call", output_to_operand_aliasing={{0}: (3, {})} | custom-call | flops 2101346304 | bytes 8208384 | tf_op jit(solution)/shard_map/pallas_call | solution.py:219
  57.5 1.6 %collective-permute-start.12 = (s32[680,128]{1,0:T(8,128)S(1)}, s32[680,128]{1,0:T(8,128)S(1)}, u32[]{:S(2)}, u32[]{:S(2)}) collective-permute-start(s32[680,128]{1,0:T(8,128)S(1)} %get-tuple-element.22), channel_id=1, source_target_pairs={{0,64},{1,65},{2,66},{3,67},{4,68},{5,69},{6,70},{7,71},{8,72},{9,... | collective-permute-start | bytes 1044488 | tf_op jit(solution)/shard_map/ppermute | solution.py:39
  60.4 5.0 %collective-permute-done.10.far_b = s32[680,128]{1,0:T(8,128)S(1)} collective-permute-done((s32[680,128]{1,0:T(8,128)S(1)}, s32[680,128]{1,0:T(8,128)S(1)}, u32[]{:S(2)}, u32[]{:S(2)}) %collective-permute-start.10) | collective-permute-done | bytes 348192 | tf_op jit(solution)/shard_map/ppermute | solution.py:39
  67.5 2.7 %collective-permute-start.13 = (s32[680,128]{1,0:T(8,128)S(1)}, s32[680,128]{1,0:T(8,128)S(1)}, u32[]{:S(2)}, u32[]{:S(2)}) collective-permute-start(s32[680,128]{1,0:T(8,128)S(1)} %get-tuple-element.23), channel_id=1, source_target_pairs={{0,192},{1,193},{2,194},{3,195},{4,196},{5,197},{6,198},{7,199},{8... | collective-permute-start | bytes 1044488 | tf_op jit(solution)/shard_map/ppermute | solution.py:39
  70.2 4.0 %collective-permute-done.12.b_one = s32[680,128]{1,0:T(8,128)S(1)} collective-permute-done((s32[680,128]{1,0:T(8,128)S(1)}, s32[680,128]{1,0:T(8,128)S(1)}, u32[]{:S(2)}, u32[]{:S(2)}) %collective-permute-start.12) | collective-permute-done | bytes 348192 | tf_op jit(solution)/shard_map/ppermute | solution.py:39
  74.3 7.5 %collective-permute-done.11.a_two = s32[680,128]{1,0:T(8,128)S(1)} collective-permute-done((s32[680,128]{1,0:T(8,128)S(1)}, s32[680,128]{1,0:T(8,128)S(1)}, u32[]{:S(2)}, u32[]{:S(2)}) %collective-permute-start.11) | collective-permute-done | bytes 348192 | tf_op jit(solution)/shard_map/ppermute | solution.py:39
  81.8 2.4 %scored.1 = (f32[2004,128]{1,0:T(8,128)S(1)}, f32[1,128]{1,0:T(1,128)S(1)}, f32[64,2,128]{2,1,0:T(2,128)}) custom-call(f32[4,2016,128]{2,1,0:T(8,128)S(1)} %get-tuple-element.17.parts, s32[680,128]{1,0:T(8,128)S(1)} %collective-permute-done.8.a_one, s32[680,128]{1,0:T(8,128)S(1)} %collective-permute-done.11.a_two, ...), custom_call_target="tpu_custom_call" | custom-call | flops 7695360 | bytes 6156288 | tf_op jit(solution)/shard_map/scored/pallas_call | solution.py:334
  84.2 5.2 %all-to-all-start.1 = ((f32[64,2,128]{2,1,0:T(2,128)}), f32[64,2,128]{2,1,0:T(2,128)S(1)}, u32[]{:S(2)}, u32[]{:S(2)}) async-start(f32[64,2,128]{2,1,0:T(2,128)} %get-tuple-element.27), calls=%async_computation.1 | async-start | bytes 131072 | tf_op jit(solution)/shard_map/all_to_all | solution.py:57
  89.4 1.9 %prefixes.1 = (f32[2004,128]{1,0:T(8,128)S(1)}, s32[2004,128]{1,0:T(8,128)}) custom-call(f32[2004,128]{1,0:T(8,128)S(1)} %get-tuple-element.24.scores, f32[1,128]{1,0:T(1,128)S(1)} %get-tuple-element.25.line, s32[2004,128]{1,0:T(8,128)S(1)} %bitcast.14, s32[1,128]{1,0:T(1,128)S(1)} %bitcast.17), custom_call_target="tpu_custom_call" | custom-call | flops 102604800 | bytes 2052096 | tf_op jit(solution)/shard_map/prefixes/pallas_call | solution.py:370
  91.3 7.9 %all-to-all-done.1.stats = f32[64,2,128]{2,1,0:T(2,128)S(1)} async-done(((f32[64,2,128]{2,1,0:T(2,128)}), f32[64,2,128]{2,1,0:T(2,128)S(1)}, u32[]{:S(2)}, u32[]{:S(2)}) %all-to-all-start.1) | async-done | bytes 65568 | tf_op jit(solution)/shard_map/all_to_all | solution.py:57
  99.3 1.5 %quantiles.1 = (f32[64,1,128]{2,1,0:T(1,128)}, f32[1,128]{1,0:T(1,128)S(1)}) custom-call(f32[64,2,128]{2,1,0:T(2,128)S(1)} %all-to-all-done.1.stats, f32[1,128]{1,0:T(1,128)S(1)} %get-tuple-element.25.line, f32[1,128]{1,0:T(1,128)S(1)} %bitcast.23, f32[2004,128]{1,0:T(8,128)S(1)} %get-tuple-element.24.scores, f32[2004,128]{1,0:T(8,128)S(1)} %get-tuple-element.28.before), custom_call_target="tpu_custom_call" | custom-call | flops 2565120 | bytes 2052096 | tf_op jit(solution)/shard_map/quantiles/pallas_call | solution.py:415
  100.7 4.4 %all-to-all-start.2 = ((f32[64,1,128]{2,1,0:T(1,128)}), f32[64,1,128]{2,1,0:T(1,128)S(1)}, u32[]{:S(2)}, u32[]{:S(2)}) async-start(f32[64,1,128]{2,1,0:T(1,128)} %get-tuple-element.30), calls=%async_computation.2 | async-start | bytes 65536 | tf_op jit(solution)/shard_map/all_to_all | solution.py:57
  106.2 8.4 %all-to-all-done.2 = f32[64,1,128]{2,1,0:T(1,128)S(1)} async-done(((f32[64,1,128]{2,1,0:T(1,128)}), f32[64,1,128]{2,1,0:T(1,128)S(1)}, u32[]{:S(2)}, u32[]{:S(2)}) %all-to-all-start.2) | async-done | bytes 32800 | tf_op jit(solution)/shard_map/all_to_all | solution.py:57
  (37 shorter events, 7.5 us)
Async XLA Ops:
  0.6 1.4 %collective-permute-start = (bf16[128,128]{1,0:T(8,128)(2,1)}, bf16[128,128]{1,0:T(8,128)(2,1)S(1)}, u32[]{:S(2)}, u32[]{:S(2)}) collective-permute-start(bf16[128,128]{1,0:T(8,128)(2,1)} %param.10), channel_id=1, source_target_pairs={{0,0},{1,1},{2,2},{3,3},{4,4},{5,5},{6,6},{7,7},{8,8},{9,9},{10,10... | collective-permute-start | bytes 98312 | tf_op jit(solution)/shard_map/ppermute | solution.py:39
  21.4 11.6 %collective-permute-start.1 = (bf16[8,128,128]{2,1,0:T(8,128)(2,1)S(1)}, bf16[8,128,128]{2,1,0:T(8,128)(2,1)S(1)}, u32[]{:S(2)}, u32[]{:S(2)}) collective-permute-start(bf16[8,128,128]{2,1,0:T(8,128)(2,1)S(1)} %all_to_all.15.mine), channel_id=1, source_target_pairs={{0,16},{1,49},{2,18},{3,51},{4,20},{5,53},{6,22},{7,55},{8,24},{9,... | collective-permute-start | bytes 786440 | tf_op jit(solution)/shard_map/ppermute | solution.py:39
  29.7 9.9 %collective-permute-start.4 = (bf16[8,128,128]{2,1,0:T(8,128)(2,1)S(1)}, bf16[8,128,128]{2,1,0:T(8,128)(2,1)S(1)}, u32[]{:S(2)}, u32[]{:S(2)}) collective-permute-start(bf16[8,128,128]{2,1,0:T(8,128)(2,1)S(1)} %all_to_all.15.mine), channel_id=1, source_target_pairs={{0,48},{1,17},{2,50},{3,19},{4,52},{5,21},{6,54},{7,23},{8,56},{9,... | collective-permute-start | bytes 786440 | tf_op jit(solution)/shard_map/ppermute | solution.py:39
  33.0 11.5 %collective-permute-start.2 = (bf16[8,128,128]{2,1,0:T(8,128)(2,1)S(1)}, bf16[8,128,128]{2,1,0:T(8,128)(2,1)S(1)}, u32[]{:S(2)}, u32[]{:S(2)}) collective-permute-start(bf16[8,128,128]{2,1,0:T(8,128)(2,1)S(1)} %collective-permute-done.1.one), channel_id=1, source_target_pairs={{0,16},{1,49},{2,18},{3,51},{4,20},{5,53},{6,22},{7,55},{8,24},{9,... | collective-permute-start | bytes 786440 | tf_op jit(solution)/shard_map/ppermute | solution.py:39
  36.1 11.1 %collective-permute-start.7 = (bf16[8,128,128]{2,1,0:T(8,128)(2,1)S(1)}, bf16[8,128,128]{2,1,0:T(8,128)(2,1)S(1)}, u32[]{:S(2)}, u32[]{:S(2)}) collective-permute-start(bf16[8,128,128]{2,1,0:T(8,128)(2,1)S(1)} %all_to_all.15.mine), channel_id=1, source_target_pairs={{0,1},{1,0},{2,3},{3,2},{4,5},{5,4},{6,7},{7,6},{8,9},{9,8},{10,11... | collective-permute-start | bytes 786440 | tf_op jit(solution)/shard_map/ppermute | solution.py:39
  39.6 10.0 %collective-permute-start.5 = (bf16[8,128,128]{2,1,0:T(8,128)(2,1)S(1)}, bf16[8,128,128]{2,1,0:T(8,128)(2,1)S(1)}, u32[]{:S(2)}, u32[]{:S(2)}) collective-permute-start(bf16[8,128,128]{2,1,0:T(8,128)(2,1)S(1)} %collective-permute-done.1.one), channel_id=1, source_target_pairs={{0,1},{1,0},{2,3},{3,2},{4,5},{5,4},{6,7},{7,6},{8,9},{9,8},{10,11... | collective-permute-start | bytes 786440 | tf_op jit(solution)/shard_map/ppermute | solution.py:39
  39.6 10.0 %collective-permute-start.6 = (bf16[8,128,128]{2,1,0:T(8,128)(2,1)S(1)}, bf16[8,128,128]{2,1,0:T(8,128)(2,1)S(1)}, u32[]{:S(2)}, u32[]{:S(2)}) collective-permute-start(bf16[8,128,128]{2,1,0:T(8,128)(2,1)S(1)} %collective-permute-done.4.two), channel_id=1, source_target_pairs={{0,1},{1,0},{2,3},{3,2},{4,5},{5,4},{6,7},{7,6},{8,9},{9,8},{10,11... | collective-permute-start | bytes 786440 | tf_op jit(solution)/shard_map/ppermute | solution.py:39
  44.5 7.7 %collective-permute-start.3 = (bf16[8,128,128]{2,1,0:T(8,128)(2,1)S(1)}, bf16[8,128,128]{2,1,0:T(8,128)(2,1)S(1)}, u32[]{:S(2)}, u32[]{:S(2)}) collective-permute-start(bf16[8,128,128]{2,1,0:T(8,128)(2,1)S(1)} %collective-permute-done.2.mine), channel_id=1, source_target_pairs={{0,1},{1,0},{2,3},{3,2},{4,5},{5,4},{6,7},{7,6},{8,9},{9,8},{10,11... | collective-permute-start | bytes 786440 | tf_op jit(solution)/shard_map/ppermute | solution.py:39
  55.0 10.4 %collective-permute-start.10 = (s32[680,128]{1,0:T(8,128)S(1)}, s32[680,128]{1,0:T(8,128)S(1)}, u32[]{:S(2)}, u32[]{:S(2)}) collective-permute-start(s32[680,128]{1,0:T(8,128)S(1)} %get-tuple-element.20), channel_id=1, source_target_pairs={{0,192},{1,193},{2,194},{3,195},{4,196},{5,197},{6,198},{7,199},{8... | collective-permute-start | bytes 1044488 | tf_op jit(solution)/shard_map/ppermute | solution.py:39
  56.2 10.6 %collective-permute-start.9 = (s32[680,128]{1,0:T(8,128)S(1)}, s32[680,128]{1,0:T(8,128)S(1)}, u32[]{:S(2)}, u32[]{:S(2)}) collective-permute-start(s32[680,128]{1,0:T(8,128)S(1)} %get-tuple-element.19), channel_id=1, source_target_pairs={{0,64},{1,65},{2,66},{3,67},{4,68},{5,69},{6,70},{7,71},{8,72},{9,... | collective-permute-start | bytes 1044488 | tf_op jit(solution)/shard_map/ppermute | solution.py:39
  57.0 24.7 %copy-start = (s32[128,2004]{0,1:T(8,128)S(1)}, s32[128,2004]{0,1:T(8,128)}, u32[]{:S(2)}) copy-start(s32[128,2004]{0,1:T(8,128)} %param.13) | copy-start | bytes 3078148
  57.0 24.7 %copy-start.1 = (s32[128,2004]{0,1:T(8,128)S(1)}, s32[128,2004]{0,1:T(8,128)}, u32[]{:S(2)}) copy-start(s32[128,2004]{0,1:T(8,128)} %param.12) | copy-start | bytes 3078148
  57.0 24.7 %copy-start.2 = (s32[128]{0:T(128)S(1)}, s32[128]{0:T(128)}, u32[]{:S(2)}) copy-start(s32[128]{0:T(128)} %param.14) | copy-start | bytes 1540
  57.0 24.7 %copy-start.3 = (f32[128]{0:T(128)S(1)}, f32[128]{0:T(128)}, u32[]{:S(2)}) copy-start(f32[128]{0:T(128)} %param.15) | copy-start | bytes 1540
  57.0 24.7 %copy-start.4 = (f32[128]{0:T(128)S(1)}, f32[128]{0:T(128)}, u32[]{:S(2)}) copy-start(f32[128]{0:T(128)} %param.16) | copy-start | bytes 1540
  57.0 24.7 %copy-start.5 = (f32[128]{0:T(128)S(1)}, f32[128]{0:T(128)}, u32[]{:S(2)}) copy-start(f32[128]{0:T(128)} %param.17) | copy-start | bytes 1540
  57.0 24.7 %copy-start.6 = (f32[128]{0:T(128)S(1)}, f32[128]{0:T(128)}, u32[]{:S(2)}) copy-start(f32[128]{0:T(128)} %param.18) | copy-start | bytes 1540
  57.5 16.8 %collective-permute-start.12 = (s32[680,128]{1,0:T(8,128)S(1)}, s32[680,128]{1,0:T(8,128)S(1)}, u32[]{:S(2)}, u32[]{:S(2)}) collective-permute-start(s32[680,128]{1,0:T(8,128)S(1)} %get-tuple-element.22), channel_id=1, source_target_pairs={{0,64},{1,65},{2,66},{3,67},{4,68},{5,69},{6,70},{7,71},{8,72},{9,... | collective-permute-start | bytes 1044488 | tf_op jit(solution)/shard_map/ppermute | solution.py:39
  59.1 15.1 %collective-permute-start.8 = (s32[680,128]{1,0:T(8,128)S(1)}, s32[680,128]{1,0:T(8,128)S(1)}, u32[]{:S(2)}, u32[]{:S(2)}) collective-permute-start(s32[680,128]{1,0:T(8,128)S(1)} %get-tuple-element.18), channel_id=1, source_target_pairs={{0,192},{1,193},{2,194},{3,195},{4,196},{5,197},{6,198},{7,199},{8... | collective-permute-start | bytes 1044488 | tf_op jit(solution)/shard_map/ppermute | solution.py:39
  67.5 14.3 %collective-permute-start.11 = (s32[680,128]{1,0:T(8,128)S(1)}, s32[680,128]{1,0:T(8,128)S(1)}, u32[]{:S(2)}, u32[]{:S(2)}) collective-permute-start(s32[680,128]{1,0:T(8,128)S(1)} %get-tuple-element.21), channel_id=1, source_target_pairs={{0,64},{1,65},{2,66},{3,67},{4,68},{5,69},{6,70},{7,71},{8,72},{9,... | collective-permute-start | bytes 1044488 | tf_op jit(solution)/shard_map/ppermute | solution.py:39
  67.5 14.2 %collective-permute-start.13 = (s32[680,128]{1,0:T(8,128)S(1)}, s32[680,128]{1,0:T(8,128)S(1)}, u32[]{:S(2)}, u32[]{:S(2)}) collective-permute-start(s32[680,128]{1,0:T(8,128)S(1)} %get-tuple-element.23), channel_id=1, source_target_pairs={{0,192},{1,193},{2,194},{3,195},{4,196},{5,197},{6,198},{7,199},{8... | collective-permute-start | bytes 1044488 | tf_op jit(solution)/shard_map/ppermute | solution.py:39
  81.8 17.5 %copy-start.7 = (f32[128]{0:T(128)S(1)}, f32[128]{0:T(128)}, u32[]{:S(2)}) copy-start(f32[128]{0:T(128)} %param.19) | copy-start | bytes 1540
  84.2 15.1 %all-to-all-start.1 = ((f32[64,2,128]{2,1,0:T(2,128)}), f32[64,2,128]{2,1,0:T(2,128)S(1)}, u32[]{:S(2)}, u32[]{:S(2)}) async-start(f32[64,2,128]{2,1,0:T(2,128)} %get-tuple-element.27), calls=%async_computation.1 | async-start | bytes 131072 | tf_op jit(solution)/shard_map/all_to_all | solution.py:57
  100.7 13.8 %all-to-all-start.2 = ((f32[64,1,128]{2,1,0:T(1,128)}), f32[64,1,128]{2,1,0:T(1,128)S(1)}, u32[]{:S(2)}, u32[]{:S(2)}) async-start(f32[64,1,128]{2,1,0:T(1,128)} %get-tuple-element.30), calls=%async_computation.2 | async-start | bytes 65536 | tf_op jit(solution)/shard_map/all_to_all | solution.py:57

commit v4 on v3

--- a/solution.py
+++ b/solution.py
@@ -16,12 +16,12 @@
 LANES = 128
 DEPTH = 2048
 HALF = 1008
-THIRD = HALF // 3
-CHUNK = 56
-STEPS = THIRD // CHUNK
+PIECE = HALF // 7
+CHUNK = 48
+STEPS = PIECE // CHUNK
 BLOCKS = ((0, 512), (512, 512), (1024, 512), (1536, ROWS - 1536))
-CODED = 2 * THIRD + 8
-BITS = 20
+CODED = 4 * PIECE + 8
+BITS = 17
 
 WHOLE = pl.BlockSpec(memory_space=pltpu.VMEM)
 
@@ -59,8 +59,8 @@
 
 def coded(load, out_ref):
     def largest(j, top):
-        for third in range(3):
-            part = jnp.abs(load(third * THIRD + j * CHUNK))
+        for piece in range(7):
+            part = jnp.abs(load(piece * PIECE + j * CHUNK))
             top = jnp.maximum(top, jnp.max(part.reshape(CHUNK // 8, 8, LANES), axis=0))
         return top
 
@@ -71,31 +71,34 @@
     limit = float(2**BITS - 1)
 
     def put(j, carry):
-        def whole(third):
-            value = jnp.round(load(third * THIRD + j * CHUNK) * scale)
+        def whole(piece):
+            value = jnp.round(load(piece * PIECE + j * CHUNK) * scale)
             return jnp.clip(value, -limit, limit).astype(jnp.int32)
 
-        a, b, c = whole(0), whole(1), whole(2)
-        mask = (1 << 21) - 1
-        out_ref[pl.ds(pl.multiple_of(j * CHUNK, 8), CHUNK), :] = (a & mask) | (c << 21)
-        out_ref[pl.ds(pl.multiple_of(THIRD + j * CHUNK, 8), CHUNK), :] = (b & mask) | ((c >> 11) << 21)
+        low = (1 << 18) - 1
+        last = whole(3) & low
+        for word in range(3):
+            high = whole(4 + word)
+            out_ref[pl.ds(aligned(word * PIECE + j * CHUNK), CHUNK), :] = (whole(word) & low) | (high << 18)
+            last = last | (((high >> 14) & 15) << (18 + 4 * word))
+        out_ref[pl.ds(aligned(3 * PIECE + j * CHUNK), CHUNK), :] = last
         return carry
 
     lax.fori_loop(0, STEPS, put, 0)
-    out_ref[2 * THIRD :, :] = jnp.broadcast_to(exponent.astype(jnp.int32), (8, LANES))
+    out_ref[4 * PIECE :, :] = jnp.broadcast_to(exponent.astype(jnp.int32), (8, LANES))
 
 
 def step_of(ref):
-    return jnp.exp2(0.25 * ref[2 * THIRD : 2 * THIRD + 1, :].astype(jnp.float32) - BITS)
+    return jnp.exp2(0.25 * ref[4 * PIECE : 4 * PIECE + 1, :].astype(jnp.float32) - BITS)
 
 
 def decoded(ref, step, j):
-    one = ref[pl.ds(pl.multiple_of(j * CHUNK, 8), CHUNK), :]
-    two = ref[pl.ds(pl.multiple_of(THIRD + j * CHUNK, 8), CHUNK), :]
-    a = (one << 11) >> 11
-    b = (two << 11) >> 11
-    c = ((two >> 21) << 11) | ((one >> 21) & 2047)
-    return [value.astype(jnp.float32) * step for value in (a, b, c)]
+    words = [ref[pl.ds(aligned(word * PIECE + j * CHUNK), CHUNK), :] for word in range(4)]
+    values = [(word << 14) >> 14 for word in words]
+    for n in range(3):
+        high = (words[3] << (10 - 4 * n)) >> 28
+        values.append((high << 14) | ((words[n] >> 18) & 0x3FFF))
+    return [value.astype(jnp.float32) * step for value in values]
 
 
 def aligned(start):
@@ -248,8 +251,8 @@
         own = part_of(parts, r, half)
 
         def add(j, carry):
-            for third, value in enumerate(decoded(far, step, j)):
-                start = third * THIRD + j * CHUNK
+            for piece, value in enumerate(decoded(far, step, j)):
+                start = piece * PIECE + j * CHUNK
                 total[pl.ds(aligned(start), CHUNK), :] = own(start) + value
             return carry
 
@@ -270,50 +273,84 @@
     )(far_a, far_b, parts)
 
 
-def scores_kernel(
-    parts, a_one, a_two, b_one, b_two, context, emitted, fresh, divisor, fine, appearance, softness,
-    scores, line, copies,
+def chunks(half):
+    full = [(piece, CHUNK) for piece in range(7)]
+    last = full[:-1] + [(6, CHUNK - half * (2 * HALF - ROWS))]
+    return full, last
+
+
+def each_chunk(half, body, carry):
+    full, last = chunks(half)
+
+    def run(j, carry):
+        return body(j, carry, full)
+
+    carry = lax.fori_loop(0, STEPS - 1, run, carry)
+    return body(STEPS - 1, carry, last)
+
+
+def early_kernel(
+    parts, a_one, b_one, context, emitted, fresh, divisor, fine, appearance, softness, sums, rising, falling, fines
 ):
     slot = slot_of(0)
-    factor = divisor[...]
-    inverse = 1.0 / factor
-    per_count = fine[...]
-    per_word = appearance[...]
     cooling = 1.0 / softness[...]
+    seen_up = cooling / divisor[...]
+    seen_down = cooling * divisor[...]
+    per_count = fine[...] * cooling
+    per_word = appearance[...] * cooling
     newest = fresh[...] - shard_index() * ROWS
 
-    def chunk(j, carry, half, first, second, steps, sizes):
-        pairs = zip(decoded(first, steps[0], j), decoded(second, steps[1], j))
-        for third, (one, two) in enumerate(pairs):
-            size = sizes[third]
-            start = half * HALF + third * THIRD + j * CHUNK
-            at = pl.ds(aligned(start), size)
-            logits = parts[slot, at, :] + one[:size] + two[:size]
-            ids = start + lax.broadcasted_iota(jnp.int32, (size, LANES), 0)
-            counts = emitted[at, :] + (ids == newest).astype(jnp.int32)
-            seen = context[at, :] + counts > 0
-            moved_score = jnp.where(logits > 0, logits * inverse, logits * factor)
-            score = jnp.where(seen, moved_score, logits)
-            score = score - per_count * counts.astype(jnp.float32)
-            score = score - jnp.where(counts > 0, per_word, 0.0)
-            score = score * cooling
-            scores[at, :] = score
-            if size == CHUNK:
-                score = jnp.max(score.reshape(CHUNK // 8, 8, LANES), axis=0)
-            carry = jnp.maximum(carry, jnp.max(score, axis=0, keepdims=True) if size < CHUNK else score)
-        return carry
-
+    for half, one in ((0, a_one), (1, b_one)):
+        step = step_of(one)
+
+        def body(j, carry, pieces):
+            for (piece, size), value in zip(pieces, decoded(one, step, j)):
+                start = half * HALF + piece * PIECE + j * CHUNK
+                at = pl.ds(aligned(start), size)
+                sums[at, :] = parts[slot, at, :] + value[:size]
+                ids = start + lax.broadcasted_iota(jnp.int32, (size, LANES), 0)
+                counts = emitted[at, :] + (ids == newest).astype(jnp.int32)
+                seen = context[at, :] + counts > 0
+                rising[at, :] = jnp.where(seen, seen_up, cooling)
+                falling[at, :] = jnp.where(seen, seen_down, cooling)
+                fines[at, :] = per_count * counts.astype(jnp.float32) + jnp.where(counts > 0, per_word, 0.0)
+            return carry
+
+        each_chunk(half, body, 0)
+
+
+def early(*args):
+    full = jax.ShapeDtypeStruct((ROWS, LANES), jnp.float32)
+    return pl.pallas_call(
+        early_kernel,
+        out_shape=[full] * 4,
+        in_specs=[WHOLE] * 10,
+        out_specs=[WHOLE] * 4,
+        compiler_params=pltpu.CompilerParams(vmem_limit_bytes=8 << 20),
+        cost_estimate=pl.CostEstimate(flops=30 * ROWS * LANES, bytes_accessed=9 * ROWS * LANES * 4, transcendentals=0),
+        name="early",
+    )(*args)
+
+
+def scores_kernel(sums, rising, falling, fines, a_two, b_two, scores, line, copies):
     top = jnp.full((8, LANES), -jnp.inf, jnp.float32)
-    for half, first, second in ((0, a_one, a_two), (1, b_one, b_two)):
-        steps = (step_of(first), step_of(second))
-        full = (CHUNK,) * 3
-
-        def body(j, carry):
-            return chunk(j, carry, half, first, second, steps, full)
-
-        top = lax.fori_loop(0, STEPS - 1, body, top)
-        last = CHUNK - half * (2 * HALF - ROWS)
-        top = chunk(STEPS - 1, top, half, first, second, steps, (CHUNK, CHUNK, last))
+    for half, two in ((0, a_two), (1, b_two)):
+        step = step_of(two)
+
+        def body(j, carry, pieces):
+            for (piece, size), value in zip(pieces, decoded(two, step, j)):
+                at = pl.ds(aligned(half * HALF + piece * PIECE + j * CHUNK), size)
+                logits = sums[at, :] + value[:size]
+                score = logits * jnp.where(logits > 0, rising[at, :], falling[at, :]) - fines[at, :]
+                scores[at, :] = score
+                if size == CHUNK:
+                    score = jnp.max(score.reshape(CHUNK // 8, 8, LANES), axis=0)
+                else:
+                    score = jnp.max(score, axis=0, keepdims=True)
+                carry = jnp.maximum(carry, score)
+            return carry
+
+        top = each_chunk(half, body, top)
     top = jnp.max(top, axis=0, keepdims=True)
 
     def run(j, total):
@@ -334,9 +371,9 @@
     return pl.pallas_call(
         scores_kernel,
         out_shape=[full, line, jax.ShapeDtypeStruct((64, 2, LANES), jnp.float32)],
-        in_specs=[WHOLE] * 12,
+        in_specs=[WHOLE] * 6,
         out_specs=[WHOLE] * 3,
-        compiler_params=pltpu.CompilerParams(vmem_limit_bytes=24 << 20),
+        compiler_params=pltpu.CompilerParams(vmem_limit_bytes=8 << 20),
         cost_estimate=pl.CostEstimate(flops=30 * ROWS * LANES, bytes_accessed=6 * ROWS * LANES * 4, transcendentals=ROWS * LANES),
         name="scored",
     )(*args)
@@ -470,14 +507,12 @@
     after_b, before_a = near(parts)
     b_one, a_one = up(after_b), down(before_a)
     after_a, before_b = relayed(far_a, far_b, parts)
-    a_two, b_two = up(after_a), down(before_b)
-
-    scores, local_top, copies = scored(
+    a_two = up(after_a)
+    b_two = down(before_b)
+    prepared = early(
         parts,
         a_one,
-        a_two,
         b_one,
-        b_two,
         context_word_tallies.T,
         emitted,
         fresh,
@@ -486,6 +521,7 @@
         appearance_fine[None],
         softness_level[None],
     )
+    scores, local_top, copies = scored(*prepared, a_two, b_two)
 
     stats = exchanged(copies)
     before, new_counts = prefixes(scores, local_top, emitted, fresh)

time: 115 us -> 111 us (0.965)
  waiting for transfers between devices: 37.5 us -> 33.6 us
    ppermute x14, waiting for transfers between devices: 21.2 us -> 17.3 us  [moved(): return lax.ppermute(value, EVERY, pairs)]
  transfers between devices with their start and end apart: 16 -> 16, of which waited for: 7 -> 8; matrix products, arithmetic and copies ran while one was open for 1% -> 1% of each run, Pallas kernels for 10% -> 11%
where the time goes in v4:
time: 111 us
  starting transfers between devices  37.3 us (34%)
  waiting for transfers between devices  33.6 us (30%)
  blocking collectives  19.3 us (17%)
  Pallas kernels  18 us (16%)
  other arithmetic  1.62 us (1%)
    ppermute x14, starting transfers between devices, moved(): return lax.ppermute(value, EVERY, pairs)  27.7 us
    all_to_all x1, blocking collectives, copies_from(): return lax.all_to_all(copies, axis, split_axis=0, concat_axis=0, tiled=True)  19.3 us
    ppermute x14, waiting for transfers between devices, moved(): return lax.ppermute(value, EVERY, pairs)  17.3 us
    all_to_all x2, waiting for transfers between devices, exchanged(): lax.all_to_all(copies, PLANE, split_axis=0, concat_axis=0, tiled=True)  16.3 us
    all_to_all x2, starting transfers between devices, exchanged(): lax.all_to_all(copies, PLANE, split_axis=0, concat_axis=0, tiled=True)  9.61 us
    pallas_call x3, Pallas kernels, multiply(): pl.pallas_call(kernel, out_shape=[PARTS] + extra, in_specs=[WHOLE] * len(...  7.75 us
    pallas_call x1, Pallas kernels, fetched(): pl.pallas_call(fetch_kernel, out_shape=jax.ShapeDtypeStruct(weights.shape...  3.44 us
  transfers between devices with their start and end apart: 16, of which 8 were waited for; matrix products, arithmetic and copies ran while one was open for 1% of the time, Pallas kernels for 11%

profile of v4, /device:TPU:1, one launch (start us, length us, event | category | flops | bytes accessed | tf_op | source)
XLA Modules:
  0.0 110.7 jit_solution(12087705408407355785)
XLA Ops:
  2.1 19.3 %all_to_all.15.mine = bf16[8,128,128]{2,1,0:T(8,128)(2,1)S(1)} all-to-all(bf16[8,128,128]{2,1,0:T(8,128)(2,1)S(1)} %broadcast_in_dim.21), channel_id=1, replica_groups=mesh['x'=4,'y'=4,'z'=8,'c'=2] {'z'}, dimensions={0} | all-to-all | bytes 524288 | tf_op jit(solution)/shard_map/all_to_all | solution.py:53
  21.4 8.3 %collective-permute-start.1 = (bf16[8,128,128]{2,1,0:T(8,128)(2,1)S(1)}, bf16[8,128,128]{2,1,0:T(8,128)(2,1)S(1)}, u32[]{:S(2)}, u32[]{:S(2)}) collective-permute-start(bf16[8,128,128]{2,1,0:T(8,128)(2,1)S(1)} %all_to_all.15.mine), channel_id=1, source_target_pairs={{0,16},{1,49},{2,18},{3,51},{4,20},{5,53},{6,22},{7,55},{8,24},{9,... | collective-permute-start | bytes 786440 | tf_op jit(solution)/shard_map/ppermute | solution.py:39
  29.7 3.3 %collective-permute-done.1.one = bf16[8,128,128]{2,1,0:T(8,128)(2,1)S(1)} collective-permute-done((bf16[8,128,128]{2,1,0:T(8,128)(2,1)S(1)}, bf16[8,128,128]{2,1,0:T(8,128)(2,1)S(1)}, u32[]{:S(2)}, u32[]{:S(2)}) %collective-permute-start.1) | collective-permute-done | bytes 262176 | tf_op jit(solution)/shard_map/ppermute | solution.py:39
  33.0 3.1 %collective-permute-start.2 = (bf16[8,128,128]{2,1,0:T(8,128)(2,1)S(1)}, bf16[8,128,128]{2,1,0:T(8,128)(2,1)S(1)}, u32[]{:S(2)}, u32[]{:S(2)}) collective-permute-start(bf16[8,128,128]{2,1,0:T(8,128)(2,1)S(1)} %collective-permute-done.1.one), channel_id=1, source_target_pairs={{0,16},{1,49},{2,18},{3,51},{4,20},{5,53},{6,22},{7,55},{8,24},{9,... | collective-permute-start | bytes 786440 | tf_op jit(solution)/shard_map/ppermute | solution.py:39
  36.1 3.5 %collective-permute-start.7 = (bf16[8,128,128]{2,1,0:T(8,128)(2,1)S(1)}, bf16[8,128,128]{2,1,0:T(8,128)(2,1)S(1)}, u32[]{:S(2)}, u32[]{:S(2)}) collective-permute-start(bf16[8,128,128]{2,1,0:T(8,128)(2,1)S(1)} %all_to_all.15.mine), channel_id=1, source_target_pairs={{0,1},{1,0},{2,3},{3,2},{4,5},{5,4},{6,7},{7,6},{8,9},{9,8},{10,11... | collective-permute-start | bytes 786440 | tf_op jit(solution)/shard_map/ppermute | solution.py:39
  39.6 1.5 %collective-permute-start.6 = (bf16[8,128,128]{2,1,0:T(8,128)(2,1)S(1)}, bf16[8,128,128]{2,1,0:T(8,128)(2,1)S(1)}, u32[]{:S(2)}, u32[]{:S(2)}) collective-permute-start(bf16[8,128,128]{2,1,0:T(8,128)(2,1)S(1)} %collective-permute-done.4.two), channel_id=1, source_target_pairs={{0,1},{1,0},{2,3},{3,2},{4,5},{5,4},{6,7},{7,6},{8,9},{9,8},{10,11... | collective-permute-start | bytes 786440 | tf_op jit(solution)/shard_map/ppermute | solution.py:39
  41.1 3.4 %fetched.1.weights = bf16[2004,2048]{1,0:T(8,128)(2,1)S(1)} custom-call(bf16[2004,2048]{1,0:T(8,128)(2,1)} %bitcast.24), custom_call_target="tpu_custom_call" | custom-call | flops 2101346304 | bytes 16416768 | tf_op jit(solution)/shard_map/fetched/pallas_call | solution.py:128
  44.5 2.7 %collective-permute-start.3 = (bf16[8,128,128]{2,1,0:T(8,128)(2,1)S(1)}, bf16[8,128,128]{2,1,0:T(8,128)(2,1)S(1)}, u32[]{:S(2)}, u32[]{:S(2)}) collective-permute-start(bf16[8,128,128]{2,1,0:T(8,128)(2,1)S(1)} %collective-permute-done.2.mine), channel_id=1, source_target_pairs={{0,1},{1,0},{2,3},{3,2},{4,5},{5,4},{6,7},{7,6},{8,9},{9,8},{10,11... | collective-permute-start | bytes 786440 | tf_op jit(solution)/shard_map/ppermute | solution.py:39
  47.2 2.4 %shard_map.121.given = f32[4,2016,128]{2,1,0:T(8,128)S(1)} custom-call(bf16[8,128,128]{2,1,0:T(8,128)(2,1)S(1)} %all_to_all.15.mine, bf16[8,128,128]{2,1,0:T(8,128)(2,1)S(1)} %collective-permute-done.7.other, bf16[2004,2048]{1,0:T(8,128)(2,1)S(1)} %fetched.1.weights), custom_call_target="tpu_custom_call" | custom-call | flops 2101346304 | bytes 8208384 | tf_op jit(solution)/shard_map/pallas_call | solution.py:222
  49.6 2.6 %shard_map.122.given = f32[4,2016,128]{2,1,0:T(8,128)S(1)} custom-call(bf16[8,128,128]{2,1,0:T(8,128)(2,1)S(1)} %collective-permute-done.1.one, bf16[8,128,128]{2,1,0:T(8,128)(2,1)S(1)} %collective-permute-done.4.two, bf16[8,128,128]{2,1,0:T(8,128)(2,1)S(1)} %collective-permute-done.5.other_one, ...), custom_call_target="tpu_custom_call", output_to_operand_aliasing={{}: (5, {})} | custom-call | flops 2101346304 | bytes 8208384 | tf_op jit(solution)/shard_map/pallas_call | solution.py:222
  52.2 2.8 %shard_map.123 = (f32[4,2016,128]{2,1,0:T(8,128)S(1)}, s32[584,128]{1,0:T(8,128)S(1)}, s32[584,128]{1,0:T(8,128)S(1)}) custom-call(bf16[8,128,128]{2,1,0:T(8,128)(2,1)S(1)} %collective-permute-done.2.mine, bf16[8,128,128]{2,1,0:T(8,128)(2,1)S(1)} %collective-permute-done.3.other, ...), custom_call_target="tpu_custom_call", output_to_operand_aliasing={{0}: (3, {})} | custom-call | flops 2101346304 | bytes 8208384 | tf_op jit(solution)/shard_map/pallas_call | solution.py:222
  55.0 1.9 %collective-permute-start.10 = (s32[584,128]{1,0:T(8,128)S(1)}, s32[584,128]{1,0:T(8,128)S(1)}, u32[]{:S(2)}, u32[]{:S(2)}) collective-permute-start(s32[584,128]{1,0:T(8,128)S(1)} %get-tuple-element.28), channel_id=1, source_target_pairs={{0,64},{1,65},{2,66},{3,67},{4,68},{5,69},{6,70},{7,71},{8,72},{9,... | collective-permute-start | bytes 897032 | tf_op jit(solution)/shard_map/ppermute | solution.py:39
  58.5 1.5 %collective-permute-start.9 = (s32[584,128]{1,0:T(8,128)S(1)}, s32[584,128]{1,0:T(8,128)S(1)}, u32[]{:S(2)}, u32[]{:S(2)}) collective-permute-start(s32[584,128]{1,0:T(8,128)S(1)} %get-tuple-element.23), channel_id=1, source_target_pairs={{0,64},{1,65},{2,66},{3,67},{4,68},{5,69},{6,70},{7,71},{8,72},{9,... | collective-permute-start | bytes 897032 | tf_op jit(solution)/shard_map/ppermute | solution.py:39
  59.9 5.0 %collective-permute-done.10.far_a = s32[584,128]{1,0:T(8,128)S(1)} collective-permute-done((s32[584,128]{1,0:T(8,128)S(1)}, s32[584,128]{1,0:T(8,128)S(1)}, u32[]{:S(2)}, u32[]{:S(2)}) %collective-permute-start.10) | collective-permute-done | bytes 299040 | tf_op jit(solution)/shard_map/ppermute | solution.py:39
  66.3 2.3 %collective-permute-start.13 = (s32[584,128]{1,0:T(8,128)S(1)}, s32[584,128]{1,0:T(8,128)S(1)}, u32[]{:S(2)}, u32[]{:S(2)}) collective-permute-start(s32[584,128]{1,0:T(8,128)S(1)} %get-tuple-element.31), channel_id=1, source_target_pairs={{0,192},{1,193},{2,194},{3,195},{4,196},{5,197},{6,198},{7,199},{8... | collective-permute-start | bytes 897032 | tf_op jit(solution)/shard_map/ppermute | solution.py:39
  68.6 3.0 %collective-permute-done.8.a_one = s32[584,128]{1,0:T(8,128)S(1)} collective-permute-done((s32[584,128]{1,0:T(8,128)S(1)}, s32[584,128]{1,0:T(8,128)S(1)}, u32[]{:S(2)}, u32[]{:S(2)}) %collective-permute-start.8) | collective-permute-done | bytes 299040 | tf_op jit(solution)/shard_map/ppermute | solution.py:39
  72.4 5.3 %collective-permute-done.12.a_two = s32[584,128]{1,0:T(8,128)S(1)} collective-permute-done((s32[584,128]{1,0:T(8,128)S(1)}, s32[584,128]{1,0:T(8,128)S(1)}, u32[]{:S(2)}, u32[]{:S(2)}) %collective-permute-start.12) | collective-permute-done | bytes 299040 | tf_op jit(solution)/shard_map/ppermute | solution.py:39
  78.0 1.7 %scored.1 = (f32[2004,128]{1,0:T(8,128)S(1)}, f32[1,128]{1,0:T(1,128)S(1)}, f32[64,2,128]{2,1,0:T(2,128)}) custom-call(f32[2004,128]{1,0:T(8,128)S(1)} %get-tuple-element.24.sums, f32[2004,128]{1,0:T(8,128)S(1)} %get-tuple-element.25.rising, f32[2004,128]{1,0:T(8,128)S(1)} %get-tuple-element.26.falling, f32[2004,128]{1,0:T(8,128)S(1)} %get-tuple-element.27.fines, ...), custom_call_target="tpu_custom_call" | custom-call | flops 7695360 | bytes 6156288 | tf_op jit(solution)/shard_map/scored/pallas_call | solution.py:371
  79.7 5.2 %all-to-all-start.1 = ((f32[64,2,128]{2,1,0:T(2,128)}), f32[64,2,128]{2,1,0:T(2,128)S(1)}, u32[]{:S(2)}, u32[]{:S(2)}) async-start(f32[64,2,128]{2,1,0:T(2,128)} %get-tuple-element.35), calls=%async_computation.1 | async-start | bytes 131072 | tf_op jit(solution)/shard_map/all_to_all | solution.py:57
  84.9 1.9 %prefixes.1 = (f32[2004,128]{1,0:T(8,128)S(1)}, s32[2004,128]{1,0:T(8,128)}) custom-call(f32[2004,128]{1,0:T(8,128)S(1)} %get-tuple-element.32.scores, f32[1,128]{1,0:T(1,128)S(1)} %get-tuple-element.33.line, s32[2004,128]{1,0:T(8,128)S(1)} %bitcast.14, s32[1,128]{1,0:T(1,128)S(1)} %bitcast.17), custom_call_target="tpu_custom_call" | custom-call | flops 102604800 | bytes 2052096 | tf_op jit(solution)/shard_map/prefixes/pallas_call | solution.py:407
  86.9 7.9 %all-to-all-done.1.stats = f32[64,2,128]{2,1,0:T(2,128)S(1)} async-done(((f32[64,2,128]{2,1,0:T(2,128)}), f32[64,2,128]{2,1,0:T(2,128)S(1)}, u32[]{:S(2)}, u32[]{:S(2)}) %all-to-all-start.1) | async-done | bytes 65568 | tf_op jit(solution)/shard_map/all_to_all | solution.py:57
  94.8 1.5 %quantiles.1 = (f32[64,1,128]{2,1,0:T(1,128)}, f32[1,128]{1,0:T(1,128)S(1)}) custom-call(f32[64,2,128]{2,1,0:T(2,128)S(1)} %all-to-all-done.1.stats, f32[1,128]{1,0:T(1,128)S(1)} %get-tuple-element.33.line, f32[1,128]{1,0:T(1,128)S(1)} %bitcast.23, f32[2004,128]{1,0:T(8,128)S(1)} %get-tuple-element.32.scores, f32[2004,128]{1,0:T(8,128)S(1)} %get-tuple-element.36.before), custom_call_target="tpu_custom_call" | custom-call | flops 2565120 | bytes 2052096 | tf_op jit(solution)/shard_map/quantiles/pallas_call | solution.py:452
  96.3 4.4 %all-to-all-start.2 = ((f32[64,1,128]{2,1,0:T(1,128)}), f32[64,1,128]{2,1,0:T(1,128)S(1)}, u32[]{:S(2)}, u32[]{:S(2)}) async-start(f32[64,1,128]{2,1,0:T(1,128)} %get-tuple-element.38), calls=%async_computation.2 | async-start | bytes 65536 | tf_op jit(solution)/shard_map/all_to_all | solution.py:57
  101.7 8.4 %all-to-all-done.2 = f32[64,1,128]{2,1,0:T(1,128)S(1)} async-done(((f32[64,1,128]{2,1,0:T(1,128)}), f32[64,1,128]{2,1,0:T(1,128)S(1)}, u32[]{:S(2)}, u32[]{:S(2)}) %all-to-all-start.2) | async-done | bytes 32800 | tf_op jit(solution)/shard_map/all_to_all | solution.py:57
  (38 shorter events, 7.1 us)
Async XLA Ops:
  0.6 1.4 %collective-permute-start = (bf16[128,128]{1,0:T(8,128)(2,1)}, bf16[128,128]{1,0:T(8,128)(2,1)S(1)}, u32[]{:S(2)}, u32[]{:S(2)}) collective-permute-start(bf16[128,128]{1,0:T(8,128)(2,1)} %param.10), channel_id=1, source_target_pairs={{0,0},{1,1},{2,2},{3,3},{4,4},{5,5},{6,6},{7,7},{8,8},{9,9},{10,10... | collective-permute-start | bytes 98312 | tf_op jit(solution)/shard_map/ppermute | solution.py:39
  21.4 11.6 %collective-permute-start.1 = (bf16[8,128,128]{2,1,0:T(8,128)(2,1)S(1)}, bf16[8,128,128]{2,1,0:T(8,128)(2,1)S(1)}, u32[]{:S(2)}, u32[]{:S(2)}) collective-permute-start(bf16[8,128,128]{2,1,0:T(8,128)(2,1)S(1)} %all_to_all.15.mine), channel_id=1, source_target_pairs={{0,16},{1,49},{2,18},{3,51},{4,20},{5,53},{6,22},{7,55},{8,24},{9,... | collective-permute-start | bytes 786440 | tf_op jit(solution)/shard_map/ppermute | solution.py:39
  29.7 9.9 %collective-permute-start.4 = (bf16[8,128,128]{2,1,0:T(8,128)(2,1)S(1)}, bf16[8,128,128]{2,1,0:T(8,128)(2,1)S(1)}, u32[]{:S(2)}, u32[]{:S(2)}) collective-permute-start(bf16[8,128,128]{2,1,0:T(8,128)(2,1)S(1)} %all_to_all.15.mine), channel_id=1, source_target_pairs={{0,48},{1,17},{2,50},{3,19},{4,52},{5,21},{6,54},{7,23},{8,56},{9,... | collective-permute-start | bytes 786440 | tf_op jit(solution)/shard_map/ppermute | solution.py:39
  33.0 11.5 %collective-permute-start.2 = (bf16[8,128,128]{2,1,0:T(8,128)(2,1)S(1)}, bf16[8,128,128]{2,1,0:T(8,128)(2,1)S(1)}, u32[]{:S(2)}, u32[]{:S(2)}) collective-permute-start(bf16[8,128,128]{2,1,0:T(8,128)(2,1)S(1)} %collective-permute-done.1.one), channel_id=1, source_target_pairs={{0,16},{1,49},{2,18},{3,51},{4,20},{5,53},{6,22},{7,55},{8,24},{9,... | collective-permute-start | bytes 786440 | tf_op jit(solution)/shard_map/ppermute | solution.py:39
  36.1 11.1 %collective-permute-start.7 = (bf16[8,128,128]{2,1,0:T(8,128)(2,1)S(1)}, bf16[8,128,128]{2,1,0:T(8,128)(2,1)S(1)}, u32[]{:S(2)}, u32[]{:S(2)}) collective-permute-start(bf16[8,128,128]{2,1,0:T(8,128)(2,1)S(1)} %all_to_all.15.mine), channel_id=1, source_target_pairs={{0,1},{1,0},{2,3},{3,2},{4,5},{5,4},{6,7},{7,6},{8,9},{9,8},{10,11... | collective-permute-start | bytes 786440 | tf_op jit(solution)/shard_map/ppermute | solution.py:39
  39.6 10.0 %collective-permute-start.5 = (bf16[8,128,128]{2,1,0:T(8,128)(2,1)S(1)}, bf16[8,128,128]{2,1,0:T(8,128)(2,1)S(1)}, u32[]{:S(2)}, u32[]{:S(2)}) collective-permute-start(bf16[8,128,128]{2,1,0:T(8,128)(2,1)S(1)} %collective-permute-done.1.one), channel_id=1, source_target_pairs={{0,1},{1,0},{2,3},{3,2},{4,5},{5,4},{6,7},{7,6},{8,9},{9,8},{10,11... | collective-permute-start | bytes 786440 | tf_op jit(solution)/shard_map/ppermute | solution.py:39
  39.6 10.0 %collective-permute-start.6 = (bf16[8,128,128]{2,1,0:T(8,128)(2,1)S(1)}, bf16[8,128,128]{2,1,0:T(8,128)(2,1)S(1)}, u32[]{:S(2)}, u32[]{:S(2)}) collective-permute-start(bf16[8,128,128]{2,1,0:T(8,128)(2,1)S(1)} %collective-permute-done.4.two), channel_id=1, source_target_pairs={{0,1},{1,0},{2,3},{3,2},{4,5},{5,4},{6,7},{7,6},{8,9},{9,8},{10,11... | collective-permute-start | bytes 786440 | tf_op jit(solution)/shard_map/ppermute | solution.py:39
  44.5 7.7 %collective-permute-start.3 = (bf16[8,128,128]{2,1,0:T(8,128)(2,1)S(1)}, bf16[8,128,128]{2,1,0:T(8,128)(2,1)S(1)}, u32[]{:S(2)}, u32[]{:S(2)}) collective-permute-start(bf16[8,128,128]{2,1,0:T(8,128)(2,1)S(1)} %collective-permute-done.2.mine), channel_id=1, source_target_pairs={{0,1},{1,0},{2,3},{3,2},{4,5},{5,4},{6,7},{7,6},{8,9},{9,8},{10,11... | collective-permute-start | bytes 786440 | tf_op jit(solution)/shard_map/ppermute | solution.py:39
  55.0 9.9 %collective-permute-start.10 = (s32[584,128]{1,0:T(8,128)S(1)}, s32[584,128]{1,0:T(8,128)S(1)}, u32[]{:S(2)}, u32[]{:S(2)}) collective-permute-start(s32[584,128]{1,0:T(8,128)S(1)} %get-tuple-element.28), channel_id=1, source_target_pairs={{0,64},{1,65},{2,66},{3,67},{4,68},{5,69},{6,70},{7,71},{8,72},{9,... | collective-permute-start | bytes 897032 | tf_op jit(solution)/shard_map/ppermute | solution.py:39
  56.9 8.3 %collective-permute-start.11 = (s32[584,128]{1,0:T(8,128)S(1)}, s32[584,128]{1,0:T(8,128)S(1)}, u32[]{:S(2)}, u32[]{:S(2)}) collective-permute-start(s32[584,128]{1,0:T(8,128)S(1)} %get-tuple-element.29), channel_id=1, source_target_pairs={{0,192},{1,193},{2,194},{3,195},{4,196},{5,197},{6,198},{7,199},{8... | collective-permute-start | bytes 897032 | tf_op jit(solution)/shard_map/ppermute | solution.py:39
  57.7 13.9 %copy-start = (s32[128,2004]{0,1:T(8,128)S(1)}, s32[128,2004]{0,1:T(8,128)}, u32[]{:S(2)}) copy-start(s32[128,2004]{0,1:T(8,128)} %param.13) | copy-start | bytes 3078148
  57.7 13.9 %copy-start.1 = (s32[128,2004]{0,1:T(8,128)S(1)}, s32[128,2004]{0,1:T(8,128)}, u32[]{:S(2)}) copy-start(s32[128,2004]{0,1:T(8,128)} %param.12) | copy-start | bytes 3078148
  57.7 13.9 %copy-start.2 = (s32[128]{0:T(128)S(1)}, s32[128]{0:T(128)}, u32[]{:S(2)}) copy-start(s32[128]{0:T(128)} %param.14) | copy-start | bytes 1540
  57.7 13.9 %copy-start.3 = (f32[128]{0:T(128)S(1)}, f32[128]{0:T(128)}, u32[]{:S(2)}) copy-start(f32[128]{0:T(128)} %param.15) | copy-start | bytes 1540
  57.7 13.9 %copy-start.4 = (f32[128]{0:T(128)S(1)}, f32[128]{0:T(128)}, u32[]{:S(2)}) copy-start(f32[128]{0:T(128)} %param.16) | copy-start | bytes 1540
  57.8 13.9 %copy-start.5 = (f32[128]{0:T(128)S(1)}, f32[128]{0:T(128)}, u32[]{:S(2)}) copy-start(f32[128]{0:T(128)} %param.17) | copy-start | bytes 1540
  57.8 13.9 %copy-start.6 = (f32[128]{0:T(128)S(1)}, f32[128]{0:T(128)}, u32[]{:S(2)}) copy-start(f32[128]{0:T(128)} %param.18) | copy-start | bytes 1540
  58.2 13.4 %collective-permute-start.8 = (s32[584,128]{1,0:T(8,128)S(1)}, s32[584,128]{1,0:T(8,128)S(1)}, u32[]{:S(2)}, u32[]{:S(2)}) collective-permute-start(s32[584,128]{1,0:T(8,128)S(1)} %get-tuple-element.22), channel_id=1, source_target_pairs={{0,192},{1,193},{2,194},{3,195},{4,196},{5,197},{6,198},{7,199},{8... | collective-permute-start | bytes 897032 | tf_op jit(solution)/shard_map/ppermute | solution.py:39
  58.5 13.2 %collective-permute-start.9 = (s32[584,128]{1,0:T(8,128)S(1)}, s32[584,128]{1,0:T(8,128)S(1)}, u32[]{:S(2)}, u32[]{:S(2)}) collective-permute-start(s32[584,128]{1,0:T(8,128)S(1)} %get-tuple-element.23), channel_id=1, source_target_pairs={{0,64},{1,65},{2,66},{3,67},{4,68},{5,69},{6,70},{7,71},{8,72},{9,... | collective-permute-start | bytes 897032 | tf_op jit(solution)/shard_map/ppermute | solution.py:39
  65.8 11.9 %collective-permute-start.12 = (s32[584,128]{1,0:T(8,128)S(1)}, s32[584,128]{1,0:T(8,128)S(1)}, u32[]{:S(2)}, u32[]{:S(2)}) collective-permute-start(s32[584,128]{1,0:T(8,128)S(1)} %get-tuple-element.30), channel_id=1, source_target_pairs={{0,64},{1,65},{2,66},{3,67},{4,68},{5,69},{6,70},{7,71},{8,72},{9,... | collective-permute-start | bytes 897032 | tf_op jit(solution)/shard_map/ppermute | solution.py:39
  66.3 11.7 %collective-permute-start.13 = (s32[584,128]{1,0:T(8,128)S(1)}, s32[584,128]{1,0:T(8,128)S(1)}, u32[]{:S(2)}, u32[]{:S(2)}) collective-permute-start(s32[584,128]{1,0:T(8,128)S(1)} %get-tuple-element.31), channel_id=1, source_target_pairs={{0,192},{1,193},{2,194},{3,195},{4,196},{5,197},{6,198},{7,199},{8... | collective-permute-start | bytes 897032 | tf_op jit(solution)/shard_map/ppermute | solution.py:39
  72.4 22.4 %copy-start.7 = (f32[128]{0:T(128)S(1)}, f32[128]{0:T(128)}, u32[]{:S(2)}) copy-start(f32[128]{0:T(128)} %param.19) | copy-start | bytes 1540
  79.7 15.1 %all-to-all-start.1 = ((f32[64,2,128]{2,1,0:T(2,128)}), f32[64,2,128]{2,1,0:T(2,128)S(1)}, u32[]{:S(2)}, u32[]{:S(2)}) async-start(f32[64,2,128]{2,1,0:T(2,128)} %get-tuple-element.35), calls=%async_computation.1 | async-start | bytes 131072 | tf_op jit(solution)/shard_map/all_to_all | solution.py:57
  96.3 13.8 %all-to-all-start.2 = ((f32[64,1,128]{2,1,0:T(1,128)}), f32[64,1,128]{2,1,0:T(1,128)S(1)}, u32[]{:S(2)}, u32[]{:S(2)}) async-start(f32[64,1,128]{2,1,0:T(1,128)} %get-tuple-element.38), calls=%async_computation.2 | async-start | bytes 65536 | tf_op jit(solution)/shard_map/all_to_all | solution.py:57

commit v5 on v4

--- a/solution.py
+++ b/solution.py
@@ -16,12 +16,12 @@
 LANES = 128
 DEPTH = 2048
 HALF = 1008
-PIECE = HALF // 7
-CHUNK = 48
-STEPS = PIECE // CHUNK
+GROUP = 144
+CHUNK = GROUP // 2
+STEPS = HALF // GROUP
 BLOCKS = ((0, 512), (512, 512), (1024, 512), (1536, ROWS - 1536))
-CODED = 4 * PIECE + 8
-BITS = 17
+CODED = HALF // 2 + 8
+LARGEST = 2**15 - 1
 
 WHOLE = pl.BlockSpec(memory_space=pltpu.VMEM)
 
@@ -57,48 +57,38 @@
     return lax.all_to_all(copies, PLANE, split_axis=0, concat_axis=0, tiled=True)
 
 
+def step_for(k):
+    return jnp.exp2(0.25 * k)
+
+
 def coded(load, out_ref):
-    def largest(j, top):
-        for piece in range(7):
-            part = jnp.abs(load(piece * PIECE + j * CHUNK))
-            top = jnp.maximum(top, jnp.max(part.reshape(CHUNK // 8, 8, LANES), axis=0))
-        return top
-
-    top = lax.fori_loop(0, STEPS, largest, jnp.zeros((8, LANES), jnp.float32))
-    top = jnp.maximum(jnp.max(top, axis=0, keepdims=True), 1e-30)
-    exponent = jnp.ceil(4.0 * jnp.log2(top))
-    scale = jnp.exp2(BITS - 0.25 * exponent)
-    limit = float(2**BITS - 1)
-
-    def put(j, carry):
-        def whole(piece):
-            value = jnp.round(load(piece * PIECE + j * CHUNK) * scale)
-            return jnp.clip(value, -limit, limit).astype(jnp.int32)
-
-        low = (1 << 18) - 1
-        last = whole(3) & low
-        for word in range(3):
-            high = whole(4 + word)
-            out_ref[pl.ds(aligned(word * PIECE + j * CHUNK), CHUNK), :] = (whole(word) & low) | (high << 18)
-            last = last | (((high >> 14) & 15) << (18 + 4 * word))
-        out_ref[pl.ds(aligned(3 * PIECE + j * CHUNK), CHUNK), :] = last
-        return carry
-
-    lax.fori_loop(0, STEPS, put, 0)
-    out_ref[4 * PIECE :, :] = jnp.broadcast_to(exponent.astype(jnp.int32), (8, LANES))
-
-
-def step_of(ref):
-    return jnp.exp2(0.25 * ref[4 * PIECE : 4 * PIECE + 1, :].astype(jnp.float32) - BITS)
-
-
-def decoded(ref, step, j):
-    words = [ref[pl.ds(aligned(word * PIECE + j * CHUNK), CHUNK), :] for word in range(4)]
-    values = [(word << 14) >> 14 for word in words]
-    for n in range(3):
-        high = (words[3] << (10 - 4 * n)) >> 28
-        values.append((high << 14) | ((words[n] >> 18) & 0x3FFF))
-    return [value.astype(jnp.float32) * step for value in values]
+    for group in range(STEPS):
+        values = [load(group * GROUP), load(group * GROUP + CHUNK)]
+        folded = [value.reshape(CHUNK // 8, 8, LANES) for value in values]
+        high = jnp.maximum(jnp.max(folded[0], axis=0), jnp.max(folded[1], axis=0))
+        low = jnp.minimum(jnp.min(folded[0], axis=0), jnp.min(folded[1], axis=0))
+        high = jnp.max(high, axis=0, keepdims=True)
+        low = jnp.min(low, axis=0, keepdims=True)
+        middle = 0.5 * (high + low)
+        need = jnp.maximum(0.5 * (high - low) * (1.0 / (LARGEST - 1)), jnp.abs(middle) * 2.0**-20)
+        k = jnp.ceil(4.0 * jnp.log2(jnp.maximum(need, 1e-30)))
+        scale = step_for(-k)
+        offset = jnp.round(middle * scale)
+        low_word, high_word = (
+            jnp.clip(jnp.round(value * scale) - offset, -LARGEST, LARGEST).astype(jnp.int32) for value in values
+        )
+        out_ref[group * CHUNK : (group + 1) * CHUNK, :] = (low_word & 0xFFFF) | (high_word << 16)
+        row = HALF // 2 + group
+        out_ref[row : row + 1, :] = (offset.astype(jnp.int32) << 10) | (k.astype(jnp.int32) & 1023)
+    out_ref[HALF // 2 + STEPS :, :] = jnp.zeros((8 - STEPS, LANES), jnp.int32)
+
+
+def decoded(ref, group):
+    word = ref[group * CHUNK : (group + 1) * CHUNK, :]
+    row = ref[HALF // 2 + group : HALF // 2 + group + 1, :]
+    offset = row >> 10
+    step = step_for(((row << 22) >> 22).astype(jnp.float32))
+    return [(value + offset).astype(jnp.float32) * step for value in ((word << 16) >> 16, word >> 16)]
 
 
 def aligned(start):
@@ -247,17 +237,12 @@
 
 def relay_kernel(far_a, far_b, parts, after_out, before_out, total):
     for r, half, far, out in ((1, 0, far_a, after_out), (3, 1, far_b, before_out)):
-        step = step_of(far)
         own = part_of(parts, r, half)
-
-        def add(j, carry):
-            for piece, value in enumerate(decoded(far, step, j)):
-                start = piece * PIECE + j * CHUNK
-                total[pl.ds(aligned(start), CHUNK), :] = own(start) + value
-            return carry
-
-        lax.fori_loop(0, STEPS, add, 0)
-        coded(lambda start: total[pl.ds(aligned(start), CHUNK), :], out)
+        for group in range(STEPS):
+            for side, value in enumerate(decoded(far, group)):
+                start = group * GROUP + side * CHUNK
+                total[start : start + CHUNK, :] = own(start) + value
+        coded(lambda start: total[start : start + CHUNK, :], out)
 
 
 def relayed(far_a, far_b, parts):
@@ -273,20 +258,9 @@
     )(far_a, far_b, parts)
 
 
-def chunks(half):
-    full = [(piece, CHUNK) for piece in range(7)]
-    last = full[:-1] + [(6, CHUNK - half * (2 * HALF - ROWS))]
-    return full, last
-
-
-def each_chunk(half, body, carry):
-    full, last = chunks(half)
-
-    def run(j, carry):
-        return body(j, carry, full)
-
-    carry = lax.fori_loop(0, STEPS - 1, run, carry)
-    return body(STEPS - 1, carry, last)
+def pieces_of(half, group):
+    start = half * HALF + group * GROUP
+    return [(side, at, min(CHUNK, ROWS - at)) for side, at in enumerate((start, start + CHUNK))]
 
 
 def early_kernel(
@@ -301,22 +275,17 @@
     newest = fresh[...] - shard_index() * ROWS
 
     for half, one in ((0, a_one), (1, b_one)):
-        step = step_of(one)
-
-        def body(j, carry, pieces):
-            for (piece, size), value in zip(pieces, decoded(one, step, j)):
-                start = half * HALF + piece * PIECE + j * CHUNK
-                at = pl.ds(aligned(start), size)
-                sums[at, :] = parts[slot, at, :] + value[:size]
+        for group in range(STEPS):
+            values = decoded(one, group)
+            for side, start, size in pieces_of(half, group):
+                at = pl.ds(start, size)
+                sums[at, :] = parts[slot, at, :] + values[side][:size]
                 ids = start + lax.broadcasted_iota(jnp.int32, (size, LANES), 0)
                 counts = emitted[at, :] + (ids == newest).astype(jnp.int32)
                 seen = context[at, :] + counts > 0
                 rising[at, :] = jnp.where(seen, seen_up, cooling)
                 falling[at, :] = jnp.where(seen, seen_down, cooling)
                 fines[at, :] = per_count * counts.astype(jnp.float32) + jnp.where(counts > 0, per_word, 0.0)
-            return carry
-
-        each_chunk(half, body, 0)
 
 
 def early(*args):
@@ -335,22 +304,18 @@
 def scores_kernel(sums, rising, falling, fines, a_two, b_two, scores, line, copies):
     top = jnp.full((8, LANES), -jnp.inf, jnp.float32)
     for half, two in ((0, a_two), (1, b_two)):
-        step = step_of(two)
-
-        def body(j, carry, pieces):
-            for (piece, size), value in zip(pieces, decoded(two, step, j)):
-                at = pl.ds(aligned(half * HALF + piece * PIECE + j * CHUNK), size)
-                logits = sums[at, :] + value[:size]
+        for group in range(STEPS):
+            values = decoded(two, group)
+            for side, start, size in pieces_of(half, group):
+                at = pl.ds(start, size)
+                logits = sums[at, :] + values[side][:size]
                 score = logits * jnp.where(logits > 0, rising[at, :], falling[at, :]) - fines[at, :]
                 scores[at, :] = score
                 if size == CHUNK:
                     score = jnp.max(score.reshape(CHUNK // 8, 8, LANES), axis=0)
                 else:
                     score = jnp.max(score, axis=0, keepdims=True)
-                carry = jnp.maximum(carry, score)
-            return carry
-
-        top = each_chunk(half, body, top)
+                top = jnp.maximum(top, score)
     top = jnp.max(top, axis=0, keepdims=True)
 
     def run(j, total):
@@ -379,7 +344,7 @@
     )(*args)
 
 
-def prefix_kernel(scores, line, emitted, fresh, before, counts):
+def prefix_kernel(scores, line, emitted, fresh, before, end, counts):
     newest = fresh[...] - shard_index() * ROWS
     ids = lax.broadcasted_iota(jnp.int32, (8, LANES), 0)
     top = line[...]
@@ -401,6 +366,7 @@
         before[row : row + 1, :] = carry
         carry = carry + jnp.exp(scores[row : row + 1, :] - top)
         counts[row : row + 1, :] = emitted[row : row + 1, :] + (newest == row).astype(jnp.int32)
+    end[...] = carry
 
 
 def prefixes(scores, line, emitted, fresh):
@@ -408,17 +374,18 @@
         prefix_kernel,
         out_shape=[
             jax.ShapeDtypeStruct((ROWS, LANES), jnp.float32),
+            jax.ShapeDtypeStruct((1, LANES), jnp.float32),
             jax.ShapeDtypeStruct((ROWS, LANES), jnp.int32),
         ],
         in_specs=[WHOLE] * 4,
-        out_specs=[WHOLE] * 2,
+        out_specs=[WHOLE] * 3,
         compiler_params=pltpu.CompilerParams(vmem_limit_bytes=8 << 20),
         cost_estimate=pl.CostEstimate(flops=400 * ROWS * LANES, bytes_accessed=2 * ROWS * LANES * 4, transcendentals=0),
         name="prefixes",
     )(scores, line, emitted, fresh)
 
 
-def quantile_kernel(stats, line, draws, scores, before, copies, shift):
+def quantile_kernel(stats, line, draws, before, end, copies, shift):
     shard = shard_index()
     top = jnp.max(stats[...], axis=0)[0:1, :]
     total = jnp.zeros((1, LANES), jnp.float32)
@@ -427,23 +394,19 @@
         part = stats[peer, 1:2, :] * jnp.exp(stats[peer, 0:1, :] - top)
         total = total + part
         lower = lower + jnp.where(peer < shard, part, 0.0)
-    mine = line[...]
-    share = jnp.exp(mine - top) / total
-    room = draws[...] - lower / total
-    first = shard * ROWS
-
-    def taken(start, size):
-        at = pl.ds(start, size)
-        mass = jnp.exp(scores[at, :] - mine) * share
-        value = jnp.minimum(jnp.maximum(room - before[at, :] * share, 0.0), mass)
-        ids = first + start + lax.broadcasted_iota(jnp.int32, (size, LANES), 0)
-        return value * ((ids.astype(jnp.float32) + 0.5) / VOCAB)
+    share = jnp.exp(line[...] - top) / total
+    room = jnp.maximum(draws[...] - lower / total, 0.0)
+    whole = jnp.minimum(room, end[...] * share)
+
+    def missing(start, size):
+        return whole - jnp.minimum(room, before[pl.ds(start, size), :] * share)
 
     def run(j, total):
-        return total + jnp.sum(taken(aligned(j * 80), 80).reshape(10, 8, LANES), axis=0)
+        return total + jnp.sum(missing(aligned(j * 80), 80).reshape(10, 8, LANES), axis=0)
 
     amount = lax.fori_loop(0, 25, run, jnp.zeros((8, LANES), jnp.float32))
-    amount = jnp.sum(amount, axis=0, keepdims=True) + jnp.sum(taken(2000, 4), axis=0, keepdims=True)
+    amount = jnp.sum(amount, axis=0, keepdims=True) + jnp.sum(missing(2000, 4), axis=0, keepdims=True)
+    amount = (amount + whole * ((shard * ROWS).astype(jnp.float32) - 0.5)) / VOCAB
     copies[...] = jnp.broadcast_to(amount[None], (64, 1, LANES))
     shift[...] = top + jnp.log(total)
 
@@ -524,8 +487,8 @@
     scores, local_top, copies = scored(*prepared, a_two, b_two)
 
     stats = exchanged(copies)
-    before, new_counts = prefixes(scores, local_top, emitted, fresh)
-    copies, shift = quantiles(stats, local_top, random_draws[None], scores, before)
+    before, end, new_counts = prefixes(scores, local_top, emitted, fresh)
+    copies, shift = quantiles(stats, local_top, random_draws[None], before, end)
     sample_quantile = jnp.sum(exchanged(copies), axis=(0, 1))
     log_likelihoods = (scores - shift).T
     return new_counts.T, log_likelihoods, sample_quantile

time: 111 us -> 108 us (0.973)
  waiting for transfers between devices: 33.6 us -> 31.5 us
    ppermute x14, waiting for transfers between devices: 17.3 us -> 15.2 us  [moved(): return lax.ppermute(value, EVERY, pairs)]
where the time goes in v5:
time: 108 us
  starting transfers between devices  37.1 us (34%)
  waiting for transfers between devices  31.5 us (29%)
  blocking collectives  19.3 us (18%)
  Pallas kernels  17.6 us (16%)
  other arithmetic  1.62 us (2%)
    ppermute x14, starting transfers between devices, moved(): return lax.ppermute(value, EVERY, pairs)  27.5 us
    all_to_all x1, blocking collectives, copies_from(): return lax.all_to_all(copies, axis, split_axis=0, concat_axis=0, tiled=True)  19.3 us
    all_to_all x2, waiting for transfers between devices, exchanged(): lax.all_to_all(copies, PLANE, split_axis=0, concat_axis=0, tiled=True)  16.4 us
    ppermute x14, waiting for transfers between devices, moved(): return lax.ppermute(value, EVERY, pairs)  15.2 us
    all_to_all x2, starting transfers between devices, exchanged(): lax.all_to_all(copies, PLANE, split_axis=0, concat_axis=0, tiled=True)  9.6 us
    pallas_call x3, Pallas kernels, multiply(): pl.pallas_call(kernel, out_shape=[PARTS] + extra, in_specs=[WHOLE] * len(...  7.74 us
    pallas_call x1, Pallas kernels, fetched(): pl.pallas_call(fetch_kernel, out_shape=jax.ShapeDtypeStruct(weights.shape...  3.44 us
  transfers between devices with their start and end apart: 16, of which 8 were waited for; matrix products, arithmetic and copies ran while one was open for 1% of the time, Pallas kernels for 11%

profile of v5, /device:TPU:1, one launch (start us, length us, event | category | flops | bytes accessed | tf_op | source)
XLA Modules:
  0.0 108.0 jit_solution(613752024992505950)
XLA Ops:
  0.6 1.4 %collective-permute-start = (bf16[128,128]{1,0:T(8,128)(2,1)}, bf16[128,128]{1,0:T(8,128)(2,1)S(1)}, u32[]{:S(2)}, u32[]{:S(2)}) collective-permute-start(bf16[128,128]{1,0:T(8,128)(2,1)} %param.10), channel_id=1, source_target_pairs={{0,0},{1,1},{2,2},{3,3},{4,4},{5,5},{6,6},{7,7},{8,8},{9,9},{10,10... | collective-permute-start | bytes 98312 | tf_op jit(solution)/shard_map/ppermute | solution.py:39
  2.1 19.3 %all_to_all.15.mine = bf16[8,128,128]{2,1,0:T(8,128)(2,1)S(1)} all-to-all(bf16[8,128,128]{2,1,0:T(8,128)(2,1)S(1)} %broadcast_in_dim.21), channel_id=1, replica_groups=mesh['x'=4,'y'=4,'z'=8,'c'=2] {'z'}, dimensions={0} | all-to-all | bytes 524288 | tf_op jit(solution)/shard_map/all_to_all | solution.py:53
  21.4 8.3 %collective-permute-start.1 = (bf16[8,128,128]{2,1,0:T(8,128)(2,1)S(1)}, bf16[8,128,128]{2,1,0:T(8,128)(2,1)S(1)}, u32[]{:S(2)}, u32[]{:S(2)}) collective-permute-start(bf16[8,128,128]{2,1,0:T(8,128)(2,1)S(1)} %all_to_all.15.mine), channel_id=1, source_target_pairs={{0,16},{1,49},{2,18},{3,51},{4,20},{5,53},{6,22},{7,55},{8,24},{9,... | collective-permute-start | bytes 786440 | tf_op jit(solution)/shard_map/ppermute | solution.py:39
  29.7 3.3 %collective-permute-done.1.one = bf16[8,128,128]{2,1,0:T(8,128)(2,1)S(1)} collective-permute-done((bf16[8,128,128]{2,1,0:T(8,128)(2,1)S(1)}, bf16[8,128,128]{2,1,0:T(8,128)(2,1)S(1)}, u32[]{:S(2)}, u32[]{:S(2)}) %collective-permute-start.1) | collective-permute-done | bytes 262176 | tf_op jit(solution)/shard_map/ppermute | solution.py:39
  33.0 3.1 %collective-permute-start.2 = (bf16[8,128,128]{2,1,0:T(8,128)(2,1)S(1)}, bf16[8,128,128]{2,1,0:T(8,128)(2,1)S(1)}, u32[]{:S(2)}, u32[]{:S(2)}) collective-permute-start(bf16[8,128,128]{2,1,0:T(8,128)(2,1)S(1)} %collective-permute-done.1.one), channel_id=1, source_target_pairs={{0,16},{1,49},{2,18},{3,51},{4,20},{5,53},{6,22},{7,55},{8,24},{9,... | collective-permute-start | bytes 786440 | tf_op jit(solution)/shard_map/ppermute | solution.py:39
  36.1 3.5 %collective-permute-start.7 = (bf16[8,128,128]{2,1,0:T(8,128)(2,1)S(1)}, bf16[8,128,128]{2,1,0:T(8,128)(2,1)S(1)}, u32[]{:S(2)}, u32[]{:S(2)}) collective-permute-start(bf16[8,128,128]{2,1,0:T(8,128)(2,1)S(1)} %all_to_all.15.mine), channel_id=1, source_target_pairs={{0,1},{1,0},{2,3},{3,2},{4,5},{5,4},{6,7},{7,6},{8,9},{9,8},{10,11... | collective-permute-start | bytes 786440 | tf_op jit(solution)/shard_map/ppermute | solution.py:39
  39.6 1.5 %collective-permute-start.6 = (bf16[8,128,128]{2,1,0:T(8,128)(2,1)S(1)}, bf16[8,128,128]{2,1,0:T(8,128)(2,1)S(1)}, u32[]{:S(2)}, u32[]{:S(2)}) collective-permute-start(bf16[8,128,128]{2,1,0:T(8,128)(2,1)S(1)} %collective-permute-done.4.two), channel_id=1, source_target_pairs={{0,1},{1,0},{2,3},{3,2},{4,5},{5,4},{6,7},{7,6},{8,9},{9,8},{10,11... | collective-permute-start | bytes 786440 | tf_op jit(solution)/shard_map/ppermute | solution.py:39
  41.1 3.4 %fetched.1.weights = bf16[2004,2048]{1,0:T(8,128)(2,1)S(1)} custom-call(bf16[2004,2048]{1,0:T(8,128)(2,1)} %bitcast.24), custom_call_target="tpu_custom_call" | custom-call | flops 2101346304 | bytes 16416768 | tf_op jit(solution)/shard_map/fetched/pallas_call | solution.py:118
  44.5 2.7 %collective-permute-start.3 = (bf16[8,128,128]{2,1,0:T(8,128)(2,1)S(1)}, bf16[8,128,128]{2,1,0:T(8,128)(2,1)S(1)}, u32[]{:S(2)}, u32[]{:S(2)}) collective-permute-start(bf16[8,128,128]{2,1,0:T(8,128)(2,1)S(1)} %collective-permute-done.2.mine), channel_id=1, source_target_pairs={{0,1},{1,0},{2,3},{3,2},{4,5},{5,4},{6,7},{7,6},{8,9},{9,8},{10,11... | collective-permute-start | bytes 786440 | tf_op jit(solution)/shard_map/ppermute | solution.py:39
  47.2 2.4 %shard_map.121.given = f32[4,2016,128]{2,1,0:T(8,128)S(1)} custom-call(bf16[8,128,128]{2,1,0:T(8,128)(2,1)S(1)} %all_to_all.15.mine, bf16[8,128,128]{2,1,0:T(8,128)(2,1)S(1)} %collective-permute-done.7.other, bf16[2004,2048]{1,0:T(8,128)(2,1)S(1)} %fetched.1.weights), custom_call_target="tpu_custom_call" | custom-call | flops 2101346304 | bytes 8208384 | tf_op jit(solution)/shard_map/pallas_call | solution.py:212
  49.6 2.6 %shard_map.122.given = f32[4,2016,128]{2,1,0:T(8,128)S(1)} custom-call(bf16[8,128,128]{2,1,0:T(8,128)(2,1)S(1)} %collective-permute-done.1.one, bf16[8,128,128]{2,1,0:T(8,128)(2,1)S(1)} %collective-permute-done.4.two, bf16[8,128,128]{2,1,0:T(8,128)(2,1)S(1)} %collective-permute-done.5.other_one, ...), custom_call_target="tpu_custom_call", output_to_operand_aliasing={{}: (5, {})} | custom-call | flops 2101346304 | bytes 8208384 | tf_op jit(solution)/shard_map/pallas_call | solution.py:212
  52.2 2.7 %shard_map.123 = (f32[4,2016,128]{2,1,0:T(8,128)S(1)}, s32[512,128]{1,0:T(8,128)S(1)}, s32[512,128]{1,0:T(8,128)S(1)}) custom-call(bf16[8,128,128]{2,1,0:T(8,128)(2,1)S(1)} %collective-permute-done.2.mine, bf16[8,128,128]{2,1,0:T(8,128)(2,1)S(1)} %collective-permute-done.3.other, ...), custom_call_target="tpu_custom_call", output_to_operand_aliasing={{0}: (3, {})} | custom-call | flops 2101346304 | bytes 8208384 | tf_op jit(solution)/shard_map/pallas_call | solution.py:212
  55.0 1.9 %collective-permute-start.10 = (s32[512,128]{1,0:T(8,128)S(1)}, s32[512,128]{1,0:T(8,128)S(1)}, u32[]{:S(2)}, u32[]{:S(2)}) collective-permute-start(s32[512,128]{1,0:T(8,128)S(1)} %get-tuple-element.29), channel_id=1, source_target_pairs={{0,64},{1,65},{2,66},{3,67},{4,68},{5,69},{6,70},{7,71},{8,72},{9,... | collective-permute-start | bytes 786440 | tf_op jit(solution)/shard_map/ppermute | solution.py:39
  58.3 1.5 %collective-permute-start.9 = (s32[512,128]{1,0:T(8,128)S(1)}, s32[512,128]{1,0:T(8,128)S(1)}, u32[]{:S(2)}, u32[]{:S(2)}) collective-permute-start(s32[512,128]{1,0:T(8,128)S(1)} %get-tuple-element.24), channel_id=1, source_target_pairs={{0,64},{1,65},{2,66},{3,67},{4,68},{5,69},{6,70},{7,71},{8,72},{9,... | collective-permute-start | bytes 786440 | tf_op jit(solution)/shard_map/ppermute | solution.py:39
  59.7 4.4 %collective-permute-done.10.far_a = s32[512,128]{1,0:T(8,128)S(1)} collective-permute-done((s32[512,128]{1,0:T(8,128)S(1)}, s32[512,128]{1,0:T(8,128)S(1)}, u32[]{:S(2)}, u32[]{:S(2)}) %collective-permute-start.10) | collective-permute-done | bytes 262176 | tf_op jit(solution)/shard_map/ppermute | solution.py:39
  65.7 2.1 %collective-permute-start.13 = (s32[512,128]{1,0:T(8,128)S(1)}, s32[512,128]{1,0:T(8,128)S(1)}, u32[]{:S(2)}, u32[]{:S(2)}) collective-permute-start(s32[512,128]{1,0:T(8,128)S(1)} %get-tuple-element.32), channel_id=1, source_target_pairs={{0,192},{1,193},{2,194},{3,195},{4,196},{5,197},{6,198},{7,199},{8... | collective-permute-start | bytes 786440 | tf_op jit(solution)/shard_map/ppermute | solution.py:39
  67.8 2.3 %collective-permute-done.8.a_one = s32[512,128]{1,0:T(8,128)S(1)} collective-permute-done((s32[512,128]{1,0:T(8,128)S(1)}, s32[512,128]{1,0:T(8,128)S(1)}, u32[]{:S(2)}, u32[]{:S(2)}) %collective-permute-start.8) | collective-permute-done | bytes 262176 | tf_op jit(solution)/shard_map/ppermute | solution.py:39
  70.8 3.9 %collective-permute-done.12.a_two = s32[512,128]{1,0:T(8,128)S(1)} collective-permute-done((s32[512,128]{1,0:T(8,128)S(1)}, s32[512,128]{1,0:T(8,128)S(1)}, u32[]{:S(2)}, u32[]{:S(2)}) %collective-permute-start.12) | collective-permute-done | bytes 262176 | tf_op jit(solution)/shard_map/ppermute | solution.py:39
  75.7 1.7 %scored.1 = (f32[2004,128]{1,0:T(8,128)S(1)}, f32[1,128]{1,0:T(1,128)S(1)}, f32[64,2,128]{2,1,0:T(2,128)}) custom-call(f32[2004,128]{1,0:T(8,128)S(1)} %get-tuple-element.25.sums, f32[2004,128]{1,0:T(8,128)S(1)} %get-tuple-element.26.rising, f32[2004,128]{1,0:T(8,128)S(1)} %get-tuple-element.27.falling, f32[2004,128]{1,0:T(8,128)S(1)} %get-tuple-element.28.fines, ...), custom_call_target="tpu_custom_call" | custom-call | flops 7695360 | bytes 6156288 | tf_op jit(solution)/shard_map/scored/pallas_call | solution.py:336
  77.3 5.2 %all-to-all-start.1 = ((f32[64,2,128]{2,1,0:T(2,128)}), f32[64,2,128]{2,1,0:T(2,128)S(1)}, u32[]{:S(2)}, u32[]{:S(2)}) async-start(f32[64,2,128]{2,1,0:T(2,128)} %get-tuple-element.36), calls=%async_computation.1 | async-start | bytes 131072 | tf_op jit(solution)/shard_map/all_to_all | solution.py:57
  82.5 1.9 %prefixes.1 = (f32[2004,128]{1,0:T(8,128)S(1)}, f32[1,128]{1,0:T(1,128)S(1)}, s32[2004,128]{1,0:T(8,128)}) custom-call(f32[2004,128]{1,0:T(8,128)S(1)} %get-tuple-element.33.scores, f32[1,128]{1,0:T(1,128)S(1)} %get-tuple-element.34.line, s32[2004,128]{1,0:T(8,128)S(1)} %bitcast.14, s32[1,128]{1,0:T(1,128)S(1)} %bitcast.17), custom_call_target="tpu_custom_call" | custom-call | flops 102604800 | bytes 2052096 | tf_op jit(solution)/shard_map/prefixes/pallas_call | solution.py:373
  84.4 8.0 %all-to-all-done.1.stats = f32[64,2,128]{2,1,0:T(2,128)S(1)} async-done(((f32[64,2,128]{2,1,0:T(2,128)}), f32[64,2,128]{2,1,0:T(2,128)S(1)}, u32[]{:S(2)}, u32[]{:S(2)}) %all-to-all-start.1) | async-done | bytes 65568 | tf_op jit(solution)/shard_map/all_to_all | solution.py:57
  93.5 4.4 %all-to-all-start.2 = ((f32[64,1,128]{2,1,0:T(1,128)}), f32[64,1,128]{2,1,0:T(1,128)S(1)}, u32[]{:S(2)}, u32[]{:S(2)}) async-start(f32[64,1,128]{2,1,0:T(1,128)} %get-tuple-element.40), calls=%async_computation.2 | async-start | bytes 65536 | tf_op jit(solution)/shard_map/all_to_all | solution.py:57
  99.0 8.4 %all-to-all-done.2 = f32[64,1,128]{2,1,0:T(1,128)S(1)} async-done(((f32[64,1,128]{2,1,0:T(1,128)}), f32[64,1,128]{2,1,0:T(1,128)S(1)}, u32[]{:S(2)}, u32[]{:S(2)}) %all-to-all-start.2) | async-done | bytes 32800 | tf_op jit(solution)/shard_map/all_to_all | solution.py:57
  (38 shorter events, 7.4 us)
Async XLA Ops:
  0.6 1.4 %collective-permute-start = (bf16[128,128]{1,0:T(8,128)(2,1)}, bf16[128,128]{1,0:T(8,128)(2,1)S(1)}, u32[]{:S(2)}, u32[]{:S(2)}) collective-permute-start(bf16[128,128]{1,0:T(8,128)(2,1)} %param.10), channel_id=1, source_target_pairs={{0,0},{1,1},{2,2},{3,3},{4,4},{5,5},{6,6},{7,7},{8,8},{9,9},{10,10... | collective-permute-start | bytes 98312 | tf_op jit(solution)/shard_map/ppermute | solution.py:39
  21.4 11.6 %collective-permute-start.1 = (bf16[8,128,128]{2,1,0:T(8,128)(2,1)S(1)}, bf16[8,128,128]{2,1,0:T(8,128)(2,1)S(1)}, u32[]{:S(2)}, u32[]{:S(2)}) collective-permute-start(bf16[8,128,128]{2,1,0:T(8,128)(2,1)S(1)} %all_to_all.15.mine), channel_id=1, source_target_pairs={{0,16},{1,49},{2,18},{3,51},{4,20},{5,53},{6,22},{7,55},{8,24},{9,... | collective-permute-start | bytes 786440 | tf_op jit(solution)/shard_map/ppermute | solution.py:39
  29.7 9.9 %collective-permute-start.4 = (bf16[8,128,128]{2,1,0:T(8,128)(2,1)S(1)}, bf16[8,128,128]{2,1,0:T(8,128)(2,1)S(1)}, u32[]{:S(2)}, u32[]{:S(2)}) collective-permute-start(bf16[8,128,128]{2,1,0:T(8,128)(2,1)S(1)} %all_to_all.15.mine), channel_id=1, source_target_pairs={{0,48},{1,17},{2,50},{3,19},{4,52},{5,21},{6,54},{7,23},{8,56},{9,... | collective-permute-start | bytes 786440 | tf_op jit(solution)/shard_map/ppermute | solution.py:39
  33.0 11.5 %collective-permute-start.2 = (bf16[8,128,128]{2,1,0:T(8,128)(2,1)S(1)}, bf16[8,128,128]{2,1,0:T(8,128)(2,1)S(1)}, u32[]{:S(2)}, u32[]{:S(2)}) collective-permute-start(bf16[8,128,128]{2,1,0:T(8,128)(2,1)S(1)} %collective-permute-done.1.one), channel_id=1, source_target_pairs={{0,16},{1,49},{2,18},{3,51},{4,20},{5,53},{6,22},{7,55},{8,24},{9,... | collective-permute-start | bytes 786440 | tf_op jit(solution)/shard_map/ppermute | solution.py:39
  36.1 11.1 %collective-permute-start.7 = (bf16[8,128,128]{2,1,0:T(8,128)(2,1)S(1)}, bf16[8,128,128]{2,1,0:T(8,128)(2,1)S(1)}, u32[]{:S(2)}, u32[]{:S(2)}) collective-permute-start(bf16[8,128,128]{2,1,0:T(8,128)(2,1)S(1)} %all_to_all.15.mine), channel_id=1, source_target_pairs={{0,1},{1,0},{2,3},{3,2},{4,5},{5,4},{6,7},{7,6},{8,9},{9,8},{10,11... | collective-permute-start | bytes 786440 | tf_op jit(solution)/shard_map/ppermute | solution.py:39
  39.6 10.0 %collective-permute-start.5 = (bf16[8,128,128]{2,1,0:T(8,128)(2,1)S(1)}, bf16[8,128,128]{2,1,0:T(8,128)(2,1)S(1)}, u32[]{:S(2)}, u32[]{:S(2)}) collective-permute-start(bf16[8,128,128]{2,1,0:T(8,128)(2,1)S(1)} %collective-permute-done.1.one), channel_id=1, source_target_pairs={{0,1},{1,0},{2,3},{3,2},{4,5},{5,4},{6,7},{7,6},{8,9},{9,8},{10,11... | collective-permute-start | bytes 786440 | tf_op jit(solution)/shard_map/ppermute | solution.py:39
  39.6 10.0 %collective-permute-start.6 = (bf16[8,128,128]{2,1,0:T(8,128)(2,1)S(1)}, bf16[8,128,128]{2,1,0:T(8,128)(2,1)S(1)}, u32[]{:S(2)}, u32[]{:S(2)}) collective-permute-start(bf16[8,128,128]{2,1,0:T(8,128)(2,1)S(1)} %collective-permute-done.4.two), channel_id=1, source_target_pairs={{0,1},{1,0},{2,3},{3,2},{4,5},{5,4},{6,7},{7,6},{8,9},{9,8},{10,11... | collective-permute-start | bytes 786440 | tf_op jit(solution)/shard_map/ppermute | solution.py:39
  44.5 7.7 %collective-permute-start.3 = (bf16[8,128,128]{2,1,0:T(8,128)(2,1)S(1)}, bf16[8,128,128]{2,1,0:T(8,128)(2,1)S(1)}, u32[]{:S(2)}, u32[]{:S(2)}) collective-permute-start(bf16[8,128,128]{2,1,0:T(8,128)(2,1)S(1)} %collective-permute-done.2.mine), channel_id=1, source_target_pairs={{0,1},{1,0},{2,3},{3,2},{4,5},{5,4},{6,7},{7,6},{8,9},{9,8},{10,11... | collective-permute-start | bytes 786440 | tf_op jit(solution)/shard_map/ppermute | solution.py:39
  55.0 9.1 %collective-permute-start.10 = (s32[512,128]{1,0:T(8,128)S(1)}, s32[512,128]{1,0:T(8,128)S(1)}, u32[]{:S(2)}, u32[]{:S(2)}) collective-permute-start(s32[512,128]{1,0:T(8,128)S(1)} %get-tuple-element.29), channel_id=1, source_target_pairs={{0,64},{1,65},{2,66},{3,67},{4,68},{5,69},{6,70},{7,71},{8,72},{9,... | collective-permute-start | bytes 786440 | tf_op jit(solution)/shard_map/ppermute | solution.py:39
  56.9 7.6 %collective-permute-start.11 = (s32[512,128]{1,0:T(8,128)S(1)}, s32[512,128]{1,0:T(8,128)S(1)}, u32[]{:S(2)}, u32[]{:S(2)}) collective-permute-start(s32[512,128]{1,0:T(8,128)S(1)} %get-tuple-element.30), channel_id=1, source_target_pairs={{0,192},{1,193},{2,194},{3,195},{4,196},{5,197},{6,198},{7,199},{8... | collective-permute-start | bytes 786440 | tf_op jit(solution)/shard_map/ppermute | solution.py:39
  57.7 12.3 %copy-start = (s32[128,2004]{0,1:T(8,128)S(1)}, s32[128,2004]{0,1:T(8,128)}, u32[]{:S(2)}) copy-start(s32[128,2004]{0,1:T(8,128)} %param.13) | copy-start | bytes 3078148
  57.7 12.3 %copy-start.1 = (s32[128,2004]{0,1:T(8,128)S(1)}, s32[128,2004]{0,1:T(8,128)}, u32[]{:S(2)}) copy-start(s32[128,2004]{0,1:T(8,128)} %param.12) | copy-start | bytes 3078148
  57.7 12.3 %copy-start.2 = (s32[128]{0:T(128)S(1)}, s32[128]{0:T(128)}, u32[]{:S(2)}) copy-start(s32[128]{0:T(128)} %param.14) | copy-start | bytes 1540
  57.7 12.3 %copy-start.3 = (f32[128]{0:T(128)S(1)}, f32[128]{0:T(128)}, u32[]{:S(2)}) copy-start(f32[128]{0:T(128)} %param.15) | copy-start | bytes 1540
  57.7 12.3 %copy-start.4 = (f32[128]{0:T(128)S(1)}, f32[128]{0:T(128)}, u32[]{:S(2)}) copy-start(f32[128]{0:T(128)} %param.16) | copy-start | bytes 1540
  57.8 12.3 %copy-start.5 = (f32[128]{0:T(128)S(1)}, f32[128]{0:T(128)}, u32[]{:S(2)}) copy-start(f32[128]{0:T(128)} %param.17) | copy-start | bytes 1540
  57.8 12.3 %copy-start.6 = (f32[128]{0:T(128)S(1)}, f32[128]{0:T(128)}, u32[]{:S(2)}) copy-start(f32[128]{0:T(128)} %param.18) | copy-start | bytes 1540
  58.2 11.9 %collective-permute-start.8 = (s32[512,128]{1,0:T(8,128)S(1)}, s32[512,128]{1,0:T(8,128)S(1)}, u32[]{:S(2)}, u32[]{:S(2)}) collective-permute-start(s32[512,128]{1,0:T(8,128)S(1)} %get-tuple-element.23), channel_id=1, source_target_pairs={{0,192},{1,193},{2,194},{3,195},{4,196},{5,197},{6,198},{7,199},{8... | collective-permute-start | bytes 786440 | tf_op jit(solution)/shard_map/ppermute | solution.py:39
  58.3 11.8 %collective-permute-start.9 = (s32[512,128]{1,0:T(8,128)S(1)}, s32[512,128]{1,0:T(8,128)S(1)}, u32[]{:S(2)}, u32[]{:S(2)}) collective-permute-start(s32[512,128]{1,0:T(8,128)S(1)} %get-tuple-element.24), channel_id=1, source_target_pairs={{0,64},{1,65},{2,66},{3,67},{4,68},{5,69},{6,70},{7,71},{8,72},{9,... | collective-permute-start | bytes 786440 | tf_op jit(solution)/shard_map/ppermute | solution.py:39
  65.0 9.6 %collective-permute-start.12 = (s32[512,128]{1,0:T(8,128)S(1)}, s32[512,128]{1,0:T(8,128)S(1)}, u32[]{:S(2)}, u32[]{:S(2)}) collective-permute-start(s32[512,128]{1,0:T(8,128)S(1)} %get-tuple-element.31), channel_id=1, source_target_pairs={{0,64},{1,65},{2,66},{3,67},{4,68},{5,69},{6,70},{7,71},{8,72},{9,... | collective-permute-start | bytes 786440 | tf_op jit(solution)/shard_map/ppermute | solution.py:39
  65.7 10.0 %collective-permute-start.13 = (s32[512,128]{1,0:T(8,128)S(1)}, s32[512,128]{1,0:T(8,128)S(1)}, u32[]{:S(2)}, u32[]{:S(2)}) collective-permute-start(s32[512,128]{1,0:T(8,128)S(1)} %get-tuple-element.32), channel_id=1, source_target_pairs={{0,192},{1,193},{2,194},{3,195},{4,196},{5,197},{6,198},{7,199},{8... | collective-permute-start | bytes 786440 | tf_op jit(solution)/shard_map/ppermute | solution.py:39
  70.8 21.6 %copy-start.7 = (f32[128]{0:T(128)S(1)}, f32[128]{0:T(128)}, u32[]{:S(2)}) copy-start(f32[128]{0:T(128)} %param.19) | copy-start | bytes 1540
  77.3 15.1 %all-to-all-start.1 = ((f32[64,2,128]{2,1,0:T(2,128)}), f32[64,2,128]{2,1,0:T(2,128)S(1)}, u32[]{:S(2)}, u32[]{:S(2)}) async-start(f32[64,2,128]{2,1,0:T(2,128)} %get-tuple-element.36), calls=%async_computation.1 | async-start | bytes 131072 | tf_op jit(solution)/shard_map/all_to_all | solution.py:57
  93.5 13.8 %all-to-all-start.2 = ((f32[64,1,128]{2,1,0:T(1,128)}), f32[64,1,128]{2,1,0:T(1,128)S(1)}, u32[]{:S(2)}, u32[]{:S(2)}) async-start(f32[64,1,128]{2,1,0:T(1,128)} %get-tuple-element.40), calls=%async_computation.2 | async-start | bytes 65536 | tf_op jit(solution)/shard_map/all_to_all | solution.py:57

commit v6 on v5

--- a/solution.py
+++ b/solution.py
@@ -184,15 +184,32 @@
     return lambda start: parts[slot, pl.ds(aligned(half * HALF + start), CHUNK), :]
 
 
-def third_kernel(mine, other, weights, given, parts, far_a, far_b, rows):
+def half_kernel(mine, weights, given, parts, rows):
     c = lax.axis_index("c")
-    lay_out(rows, 0, mine, c)
-    lay_out(rows, 0, other, 1 - c)
-
-    def put(start, size, value):
-        parts[2, pl.ds(start, size), :] = value
-
-    multiplied(weights, rows, put)
+    for z in range(NZ):
+        rows[:, z * 128 : (z + 1) * 128] = mine[z]
+    for start, size in BLOCKS:
+        own = jnp.concatenate(
+            [weights[pl.ds(start, size), pl.ds(pl.multiple_of((2 * z + c) * 128, 128), 128)] for z in range(NZ)], axis=1
+        )
+        parts[2, pl.ds(start, size), :] = lax.dot_general(
+            own, rows[...], (((1,), (1,)), ((), ())), preferred_element_type=jnp.float32
+        )
+
+
+def third_kernel(other, weights, given, parts, far_a, far_b, rows):
+    c = lax.axis_index("c")
+    for z in range(NZ):
+        rows[:, z * 128 : (z + 1) * 128] = other[z]
+    for start, size in BLOCKS:
+        theirs = jnp.concatenate(
+            [weights[pl.ds(start, size), pl.ds(pl.multiple_of((2 * z + 1 - c) * 128, 128), 128)] for z in range(NZ)],
+            axis=1,
+        )
+        at = pl.ds(start, size)
+        parts[2, at, :] = parts[2, at, :] + lax.dot_general(
+            theirs, rows[...], (((1,), (1,)), ((), ())), preferred_element_type=jnp.float32
+        )
     clear_tail(parts, 2)
     coded(part_of(parts, 2, 0), far_a)
     coded(part_of(parts, 2, 1), far_b)
@@ -207,14 +224,14 @@
 CODE = jax.ShapeDtypeStruct((CODED, LANES), jnp.int32)
 
 
-def multiply(kernel, groups, extra, *args):
+def multiply(kernel, groups, extra, *args, depth=DEPTH):
     given = len(args) - 1 if kernel is not first_kernel else None
     return pl.pallas_call(
         kernel,
         out_shape=[PARTS] + extra,
         in_specs=[WHOLE] * len(args),
         out_specs=[WHOLE] * (1 + len(extra)),
-        scratch_shapes=[pltpu.VMEM((groups * LANES, DEPTH), jnp.bfloat16)],
+        scratch_shapes=[pltpu.VMEM((groups * LANES, depth), jnp.bfloat16)],
         input_output_aliases={} if given is None else {given: 0},
         compiler_params=pltpu.CompilerParams(vmem_limit_bytes=12 << 20),
         cost_estimate=pl.CostEstimate(
@@ -463,7 +480,8 @@
     (parts,) = multiply(first_kernel, 1, [], mine, other, weights)
     (parts,) = multiply(second_kernel, 2, [], one, two, other_one, other_two, weights, parts)
     other_last = partner(last)
-    parts, far_a, far_b = multiply(third_kernel, 1, [CODE, CODE], last, other_last, weights, parts)
+    (parts,) = multiply(half_kernel, 1, [], last, weights, parts, depth=DEPTH // 2)
+    parts, far_a, far_b = multiply(third_kernel, 1, [CODE, CODE], other_last, weights, parts, depth=DEPTH // 2)
 
     far_a = up(far_a)
     far_b = down(far_b)

time: 108 us -> 106 us (0.981)
  waiting for transfers between devices: 31.5 us -> 28.2 us
    ppermute x14, waiting for transfers between devices: 15.2 us -> 11.8 us  [moved(): return lax.ppermute(value, EVERY, pairs)]
    pallas_call x3 -> x4, Pallas kernels: 7.74 us -> 8.12 us  [multiply(): pl.pallas_call(kernel, out_shape=[PARTS] + extra, in_specs=[WHOLE] * len(...]
  transfers between devices with their start and end apart: 16 -> 16, of which waited for: 8 -> 7; matrix products, arithmetic and copies ran while one was open for 1% -> 1% of each run, Pallas kernels for 11% -> 13%
where the time goes in v6:
time: 106 us
  starting transfers between devices  38 us (36%)
  waiting for transfers between devices  28.2 us (27%)
  blocking collectives  19.3 us (18%)
  Pallas kernels  17.9 us (17%)
  other arithmetic  1.62 us (2%)
    ppermute x14, starting transfers between devices, moved(): return lax.ppermute(value, EVERY, pairs)  28.4 us
    all_to_all x1, blocking collectives, copies_from(): return lax.all_to_all(copies, axis, split_axis=0, concat_axis=0, tiled=True)  19.3 us
    all_to_all x2, waiting for transfers between devices, exchanged(): lax.all_to_all(copies, PLANE, split_axis=0, concat_axis=0, tiled=True)  16.4 us
    ppermute x14, waiting for transfers between devices, moved(): return lax.ppermute(value, EVERY, pairs)  11.8 us
    all_to_all x2, starting transfers between devices, exchanged(): lax.all_to_all(copies, PLANE, split_axis=0, concat_axis=0, tiled=True)  9.61 us
    pallas_call x4, Pallas kernels, multiply(): pl.pallas_call(kernel, out_shape=[PARTS] + extra, in_specs=[WHOLE] * len(...  8.12 us
    pallas_call x1, Pallas kernels, fetched(): pl.pallas_call(fetch_kernel, out_shape=jax.ShapeDtypeStruct(weights.shape...  3.44 us
  transfers between devices with their start and end apart: 16, of which 7 were waited for; matrix products, arithmetic and copies ran while one was open for 1% of the time, Pallas kernels for 13%

profile of v6, /device:TPU:1, one launch (start us, length us, event | category | flops | bytes accessed | tf_op | source)
XLA Modules:
  0.0 106.0 jit_solution(8867125649031514422)
XLA Ops:
  0.6 1.4 %collective-permute-start = (bf16[128,128]{1,0:T(8,128)(2,1)}, bf16[128,128]{1,0:T(8,128)(2,1)S(1)}, u32[]{:S(2)}, u32[]{:S(2)}) collective-permute-start(bf16[128,128]{1,0:T(8,128)(2,1)} %param.10), channel_id=1, source_target_pairs={{0,0},{1,1},{2,2},{3,3},{4,4},{5,5},{6,6},{7,7},{8,8},{9,9},{10,10... | collective-permute-start | bytes 98312 | tf_op jit(solution)/shard_map/ppermute | solution.py:39
  2.1 19.3 %all_to_all.15.mine = bf16[8,128,128]{2,1,0:T(8,128)(2,1)S(1)} all-to-all(bf16[8,128,128]{2,1,0:T(8,128)(2,1)S(1)} %broadcast_in_dim.21), channel_id=1, replica_groups=mesh['x'=4,'y'=4,'z'=8,'c'=2] {'z'}, dimensions={0} | all-to-all | bytes 524288 | tf_op jit(solution)/shard_map/all_to_all | solution.py:53
  21.4 8.3 %collective-permute-start.1 = (bf16[8,128,128]{2,1,0:T(8,128)(2,1)S(1)}, bf16[8,128,128]{2,1,0:T(8,128)(2,1)S(1)}, u32[]{:S(2)}, u32[]{:S(2)}) collective-permute-start(bf16[8,128,128]{2,1,0:T(8,128)(2,1)S(1)} %all_to_all.15.mine), channel_id=1, source_target_pairs={{0,16},{1,49},{2,18},{3,51},{4,20},{5,53},{6,22},{7,55},{8,24},{9,... | collective-permute-start | bytes 786440 | tf_op jit(solution)/shard_map/ppermute | solution.py:39
  29.7 3.8 %collective-permute-start.7 = (bf16[8,128,128]{2,1,0:T(8,128)(2,1)S(1)}, bf16[8,128,128]{2,1,0:T(8,128)(2,1)S(1)}, u32[]{:S(2)}, u32[]{:S(2)}) collective-permute-start(bf16[8,128,128]{2,1,0:T(8,128)(2,1)S(1)} %all_to_all.15.mine), channel_id=1, source_target_pairs={{0,1},{1,0},{2,3},{3,2},{4,5},{5,4},{6,7},{7,6},{8,9},{9,8},{10,11... | collective-permute-start | bytes 786440 | tf_op jit(solution)/shard_map/ppermute | solution.py:39
  33.5 6.1 %collective-permute-start.5 = (bf16[8,128,128]{2,1,0:T(8,128)(2,1)S(1)}, bf16[8,128,128]{2,1,0:T(8,128)(2,1)S(1)}, u32[]{:S(2)}, u32[]{:S(2)}) collective-permute-start(bf16[8,128,128]{2,1,0:T(8,128)(2,1)S(1)} %collective-permute-done.1.one), channel_id=1, source_target_pairs={{0,1},{1,0},{2,3},{3,2},{4,5},{5,4},{6,7},{7,6},{8,9},{9,8},{10,11... | collective-permute-start | bytes 786440 | tf_op jit(solution)/shard_map/ppermute | solution.py:39
  39.7 3.4 %fetched.1.weights = bf16[2004,2048]{1,0:T(8,128)(2,1)S(1)} custom-call(bf16[2004,2048]{1,0:T(8,128)(2,1)} %bitcast.24), custom_call_target="tpu_custom_call" | custom-call | flops 2101346304 | bytes 16416768 | tf_op jit(solution)/shard_map/fetched/pallas_call | solution.py:118
  43.2 2.4 %shard_map.121.given = f32[4,2016,128]{2,1,0:T(8,128)S(1)} custom-call(bf16[8,128,128]{2,1,0:T(8,128)(2,1)S(1)} %all_to_all.15.mine, bf16[8,128,128]{2,1,0:T(8,128)(2,1)S(1)} %collective-permute-done.7.other, bf16[2004,2048]{1,0:T(8,128)(2,1)S(1)} %fetched.1.weights), custom_call_target="tpu_custom_call" | custom-call | flops 2101346304 | bytes 8208384 | tf_op jit(solution)/shard_map/pallas_call | solution.py:229
  45.5 1.6 %collective-permute-start.3 = (bf16[8,128,128]{2,1,0:T(8,128)(2,1)S(1)}, bf16[8,128,128]{2,1,0:T(8,128)(2,1)S(1)}, u32[]{:S(2)}, u32[]{:S(2)}) collective-permute-start(bf16[8,128,128]{2,1,0:T(8,128)(2,1)S(1)} %collective-permute-done.2.mine), channel_id=1, source_target_pairs={{0,1},{1,0},{2,3},{3,2},{4,5},{5,4},{6,7},{7,6},{8,9},{9,8},{10,11... | collective-permute-start | bytes 786440 | tf_op jit(solution)/shard_map/ppermute | solution.py:39
  47.2 2.6 %shard_map.122.given = f32[4,2016,128]{2,1,0:T(8,128)S(1)} custom-call(bf16[8,128,128]{2,1,0:T(8,128)(2,1)S(1)} %collective-permute-done.1.one, bf16[8,128,128]{2,1,0:T(8,128)(2,1)S(1)} %collective-permute-done.4.two, bf16[8,128,128]{2,1,0:T(8,128)(2,1)S(1)} %collective-permute-done.5.other_one, ...), custom_call_target="tpu_custom_call", output_to_operand_aliasing={{}: (5, {})} | custom-call | flops 2101346304 | bytes 8208384 | tf_op jit(solution)/shard_map/pallas_call | solution.py:229
  49.8 1.3 %shard_map.123.given = f32[4,2016,128]{2,1,0:T(8,128)S(1)} custom-call(bf16[8,128,128]{2,1,0:T(8,128)(2,1)S(1)} %collective-permute-done.2.mine, bf16[2004,2048]{1,0:T(8,128)(2,1)S(1)} %fetched.1.weights, f32[4,2016,128]{2,1,0:T(8,128)S(1)} %shard_map.122.given), custom_call_target="tpu_custom_call", output_to_operand_aliasing={{}: (2, {})} | custom-call | flops 2101346304 | bytes 8208384 | tf_op jit(solution)/shard_map/pallas_call | solution.py:229
  51.1 1.8 %shard_map.124 = (f32[4,2016,128]{2,1,0:T(8,128)S(1)}, s32[512,128]{1,0:T(8,128)S(1)}, s32[512,128]{1,0:T(8,128)S(1)}) custom-call(bf16[8,128,128]{2,1,0:T(8,128)(2,1)S(1)} %collective-permute-done.3.other, bf16[2004,2048]{1,0:T(8,128)(2,1)S(1)} %fetched.1.weights, f32[4,2016,128]{2,1,0:T(8,128)S(1)} %shard_map.123.given), custom_call_target="tpu_custom_call", output_to_operand_aliasing={{0}: (2, {})} | custom-call | flops 2101346304 | bytes 8208384 | tf_op jit(solution)/shard_map/pallas_call | solution.py:229
  53.0 1.9 %collective-permute-start.10 = (s32[512,128]{1,0:T(8,128)S(1)}, s32[512,128]{1,0:T(8,128)S(1)}, u32[]{:S(2)}, u32[]{:S(2)}) collective-permute-start(s32[512,128]{1,0:T(8,128)S(1)} %get-tuple-element.29), channel_id=1, source_target_pairs={{0,64},{1,65},{2,66},{3,67},{4,68},{5,69},{6,70},{7,71},{8,72},{9,... | collective-permute-start | bytes 786440 | tf_op jit(solution)/shard_map/ppermute | solution.py:39
  56.3 1.5 %collective-permute-start.9 = (s32[512,128]{1,0:T(8,128)S(1)}, s32[512,128]{1,0:T(8,128)S(1)}, u32[]{:S(2)}, u32[]{:S(2)}) collective-permute-start(s32[512,128]{1,0:T(8,128)S(1)} %get-tuple-element.24), channel_id=1, source_target_pairs={{0,64},{1,65},{2,66},{3,67},{4,68},{5,69},{6,70},{7,71},{8,72},{9,... | collective-permute-start | bytes 786440 | tf_op jit(solution)/shard_map/ppermute | solution.py:39
  57.7 4.4 %collective-permute-done.10.far_a = s32[512,128]{1,0:T(8,128)S(1)} collective-permute-done((s32[512,128]{1,0:T(8,128)S(1)}, s32[512,128]{1,0:T(8,128)S(1)}, u32[]{:S(2)}, u32[]{:S(2)}) %collective-permute-start.10) | collective-permute-done | bytes 262176 | tf_op jit(solution)/shard_map/ppermute | solution.py:39
  63.6 2.1 %collective-permute-start.13 = (s32[512,128]{1,0:T(8,128)S(1)}, s32[512,128]{1,0:T(8,128)S(1)}, u32[]{:S(2)}, u32[]{:S(2)}) collective-permute-start(s32[512,128]{1,0:T(8,128)S(1)} %get-tuple-element.32), channel_id=1, source_target_pairs={{0,192},{1,193},{2,194},{3,195},{4,196},{5,197},{6,198},{7,199},{8... | collective-permute-start | bytes 786440 | tf_op jit(solution)/shard_map/ppermute | solution.py:39
  65.8 2.3 %collective-permute-done.8.a_one = s32[512,128]{1,0:T(8,128)S(1)} collective-permute-done((s32[512,128]{1,0:T(8,128)S(1)}, s32[512,128]{1,0:T(8,128)S(1)}, u32[]{:S(2)}, u32[]{:S(2)}) %collective-permute-start.8) | collective-permute-done | bytes 262176 | tf_op jit(solution)/shard_map/ppermute | solution.py:39
  68.7 3.9 %collective-permute-done.12.a_two = s32[512,128]{1,0:T(8,128)S(1)} collective-permute-done((s32[512,128]{1,0:T(8,128)S(1)}, s32[512,128]{1,0:T(8,128)S(1)}, u32[]{:S(2)}, u32[]{:S(2)}) %collective-permute-start.12) | collective-permute-done | bytes 262176 | tf_op jit(solution)/shard_map/ppermute | solution.py:39
  73.6 1.7 %scored.1 = (f32[2004,128]{1,0:T(8,128)S(1)}, f32[1,128]{1,0:T(1,128)S(1)}, f32[64,2,128]{2,1,0:T(2,128)}) custom-call(f32[2004,128]{1,0:T(8,128)S(1)} %get-tuple-element.25.sums, f32[2004,128]{1,0:T(8,128)S(1)} %get-tuple-element.26.rising, f32[2004,128]{1,0:T(8,128)S(1)} %get-tuple-element.27.falling, f32[2004,128]{1,0:T(8,128)S(1)} %get-tuple-element.28.fines, ...), custom_call_target="tpu_custom_call" | custom-call | flops 7695360 | bytes 6156288 | tf_op jit(solution)/shard_map/scored/pallas_call | solution.py:353
  75.3 5.2 %all-to-all-start.1 = ((f32[64,2,128]{2,1,0:T(2,128)}), f32[64,2,128]{2,1,0:T(2,128)S(1)}, u32[]{:S(2)}, u32[]{:S(2)}) async-start(f32[64,2,128]{2,1,0:T(2,128)} %get-tuple-element.36), calls=%async_computation.1 | async-start | bytes 131072 | tf_op jit(solution)/shard_map/all_to_all | solution.py:57
  80.5 1.9 %prefixes.1 = (f32[2004,128]{1,0:T(8,128)S(1)}, f32[1,128]{1,0:T(1,128)S(1)}, s32[2004,128]{1,0:T(8,128)}) custom-call(f32[2004,128]{1,0:T(8,128)S(1)} %get-tuple-element.33.scores, f32[1,128]{1,0:T(1,128)S(1)} %get-tuple-element.34.line, s32[2004,128]{1,0:T(8,128)S(1)} %bitcast.14, s32[1,128]{1,0:T(1,128)S(1)} %bitcast.17), custom_call_target="tpu_custom_call" | custom-call | flops 102604800 | bytes 2052096 | tf_op jit(solution)/shard_map/prefixes/pallas_call | solution.py:390
  82.4 8.0 %all-to-all-done.1.stats = f32[64,2,128]{2,1,0:T(2,128)S(1)} async-done(((f32[64,2,128]{2,1,0:T(2,128)}), f32[64,2,128]{2,1,0:T(2,128)S(1)}, u32[]{:S(2)}, u32[]{:S(2)}) %all-to-all-start.1) | async-done | bytes 65568 | tf_op jit(solution)/shard_map/all_to_all | solution.py:57
  90.4 1.1 %quantiles.1 = (f32[64,1,128]{2,1,0:T(1,128)}, f32[1,128]{1,0:T(1,128)S(1)}) custom-call(f32[64,2,128]{2,1,0:T(2,128)S(1)} %all-to-all-done.1.stats, f32[1,128]{1,0:T(1,128)S(1)} %get-tuple-element.34.line, f32[1,128]{1,0:T(1,128)S(1)} %bitcast.22, f32[2004,128]{1,0:T(8,128)S(1)} %get-tuple-element.37.before, f32[1,128]{1,0:T(1,128)S(1)} %get-tuple-element.38.end), custom_call_target="tpu_custom_call" | custom-call | flops 2565120 | bytes 2052096 | tf_op jit(solution)/shard_map/quantiles/pallas_call | solution.py:432
  91.5 4.4 %all-to-all-start.2 = ((f32[64,1,128]{2,1,0:T(1,128)}), f32[64,1,128]{2,1,0:T(1,128)S(1)}, u32[]{:S(2)}, u32[]{:S(2)}) async-start(f32[64,1,128]{2,1,0:T(1,128)} %get-tuple-element.40), calls=%async_computation.2 | async-start | bytes 65536 | tf_op jit(solution)/shard_map/all_to_all | solution.py:57
  97.0 8.4 %all-to-all-done.2 = f32[64,1,128]{2,1,0:T(1,128)S(1)} async-done(((f32[64,1,128]{2,1,0:T(1,128)}), f32[64,1,128]{2,1,0:T(1,128)S(1)}, u32[]{:S(2)}, u32[]{:S(2)}) %all-to-all-start.2) | async-done | bytes 32800 | tf_op jit(solution)/shard_map/all_to_all | solution.py:57
  (39 shorter events, 6.4 us)
Async XLA Ops:
  0.6 1.4 %collective-permute-start = (bf16[128,128]{1,0:T(8,128)(2,1)}, bf16[128,128]{1,0:T(8,128)(2,1)S(1)}, u32[]{:S(2)}, u32[]{:S(2)}) collective-permute-start(bf16[128,128]{1,0:T(8,128)(2,1)} %param.10), channel_id=1, source_target_pairs={{0,0},{1,1},{2,2},{3,3},{4,4},{5,5},{6,6},{7,7},{8,8},{9,9},{10,10... | collective-permute-start | bytes 98312 | tf_op jit(solution)/shard_map/ppermute | solution.py:39
  21.4 12.1 %collective-permute-start.1 = (bf16[8,128,128]{2,1,0:T(8,128)(2,1)S(1)}, bf16[8,128,128]{2,1,0:T(8,128)(2,1)S(1)}, u32[]{:S(2)}, u32[]{:S(2)}) collective-permute-start(bf16[8,128,128]{2,1,0:T(8,128)(2,1)S(1)} %all_to_all.15.mine), channel_id=1, source_target_pairs={{0,16},{1,49},{2,18},{3,51},{4,20},{5,53},{6,22},{7,55},{8,24},{9,... | collective-permute-start | bytes 786440 | tf_op jit(solution)/shard_map/ppermute | solution.py:39
  29.7 9.9 %collective-permute-start.4 = (bf16[8,128,128]{2,1,0:T(8,128)(2,1)S(1)}, bf16[8,128,128]{2,1,0:T(8,128)(2,1)S(1)}, u32[]{:S(2)}, u32[]{:S(2)}) collective-permute-start(bf16[8,128,128]{2,1,0:T(8,128)(2,1)S(1)} %all_to_all.15.mine), channel_id=1, source_target_pairs={{0,48},{1,17},{2,50},{3,19},{4,52},{5,21},{6,54},{7,23},{8,56},{9,... | collective-permute-start | bytes 786440 | tf_op jit(solution)/shard_map/ppermute | solution.py:39
  29.7 13.5 %collective-permute-start.7 = (bf16[8,128,128]{2,1,0:T(8,128)(2,1)S(1)}, bf16[8,128,128]{2,1,0:T(8,128)(2,1)S(1)}, u32[]{:S(2)}, u32[]{:S(2)}) collective-permute-start(bf16[8,128,128]{2,1,0:T(8,128)(2,1)S(1)} %all_to_all.15.mine), channel_id=1, source_target_pairs={{0,1},{1,0},{2,3},{3,2},{4,5},{5,4},{6,7},{7,6},{8,9},{9,8},{10,11... | collective-permute-start | bytes 786440 | tf_op jit(solution)/shard_map/ppermute | solution.py:39
  33.5 13.7 %collective-permute-start.5 = (bf16[8,128,128]{2,1,0:T(8,128)(2,1)S(1)}, bf16[8,128,128]{2,1,0:T(8,128)(2,1)S(1)}, u32[]{:S(2)}, u32[]{:S(2)}) collective-permute-start(bf16[8,128,128]{2,1,0:T(8,128)(2,1)S(1)} %collective-permute-done.1.one), channel_id=1, source_target_pairs={{0,1},{1,0},{2,3},{3,2},{4,5},{5,4},{6,7},{7,6},{8,9},{9,8},{10,11... | collective-permute-start | bytes 786440 | tf_op jit(solution)/shard_map/ppermute | solution.py:39
  39.6 5.9 %collective-permute-start.2 = (bf16[8,128,128]{2,1,0:T(8,128)(2,1)S(1)}, bf16[8,128,128]{2,1,0:T(8,128)(2,1)S(1)}, u32[]{:S(2)}, u32[]{:S(2)}) collective-permute-start(bf16[8,128,128]{2,1,0:T(8,128)(2,1)S(1)} %collective-permute-done.1.one), channel_id=1, source_target_pairs={{0,16},{1,49},{2,18},{3,51},{4,20},{5,53},{6,22},{7,55},{8,24},{9,... | collective-permute-start | bytes 786440 | tf_op jit(solution)/shard_map/ppermute | solution.py:39
  39.6 7.6 %collective-permute-start.6 = (bf16[8,128,128]{2,1,0:T(8,128)(2,1)S(1)}, bf16[8,128,128]{2,1,0:T(8,128)(2,1)S(1)}, u32[]{:S(2)}, u32[]{:S(2)}) collective-permute-start(bf16[8,128,128]{2,1,0:T(8,128)(2,1)S(1)} %collective-permute-done.4.two), channel_id=1, source_target_pairs={{0,1},{1,0},{2,3},{3,2},{4,5},{5,4},{6,7},{7,6},{8,9},{9,8},{10,11... | collective-permute-start | bytes 786440 | tf_op jit(solution)/shard_map/ppermute | solution.py:39
  45.5 5.6 %collective-permute-start.3 = (bf16[8,128,128]{2,1,0:T(8,128)(2,1)S(1)}, bf16[8,128,128]{2,1,0:T(8,128)(2,1)S(1)}, u32[]{:S(2)}, u32[]{:S(2)}) collective-permute-start(bf16[8,128,128]{2,1,0:T(8,128)(2,1)S(1)} %collective-permute-done.2.mine), channel_id=1, source_target_pairs={{0,1},{1,0},{2,3},{3,2},{4,5},{5,4},{6,7},{7,6},{8,9},{9,8},{10,11... | collective-permute-start | bytes 786440 | tf_op jit(solution)/shard_map/ppermute | solution.py:39
  53.0 9.1 %collective-permute-start.10 = (s32[512,128]{1,0:T(8,128)S(1)}, s32[512,128]{1,0:T(8,128)S(1)}, u32[]{:S(2)}, u32[]{:S(2)}) collective-permute-start(s32[512,128]{1,0:T(8,128)S(1)} %get-tuple-element.29), channel_id=1, source_target_pairs={{0,64},{1,65},{2,66},{3,67},{4,68},{5,69},{6,70},{7,71},{8,72},{9,... | collective-permute-start | bytes 786440 | tf_op jit(solution)/shard_map/ppermute | solution.py:39
  54.8 7.6 %collective-permute-start.11 = (s32[512,128]{1,0:T(8,128)S(1)}, s32[512,128]{1,0:T(8,128)S(1)}, u32[]{:S(2)}, u32[]{:S(2)}) collective-permute-start(s32[512,128]{1,0:T(8,128)S(1)} %get-tuple-element.30), channel_id=1, source_target_pairs={{0,192},{1,193},{2,194},{3,195},{4,196},{5,197},{6,198},{7,199},{8... | collective-permute-start | bytes 786440 | tf_op jit(solution)/shard_map/ppermute | solution.py:39
  55.7 12.3 %copy-start = (s32[128,2004]{0,1:T(8,128)S(1)}, s32[128,2004]{0,1:T(8,128)}, u32[]{:S(2)}) copy-start(s32[128,2004]{0,1:T(8,128)} %param.13) | copy-start | bytes 3078148
  55.7 12.3 %copy-start.1 = (s32[128,2004]{0,1:T(8,128)S(1)}, s32[128,2004]{0,1:T(8,128)}, u32[]{:S(2)}) copy-start(s32[128,2004]{0,1:T(8,128)} %param.12) | copy-start | bytes 3078148
  55.7 12.3 %copy-start.2 = (s32[128]{0:T(128)S(1)}, s32[128]{0:T(128)}, u32[]{:S(2)}) copy-start(s32[128]{0:T(128)} %param.14) | copy-start | bytes 1540
  55.7 12.3 %copy-start.3 = (f32[128]{0:T(128)S(1)}, f32[128]{0:T(128)}, u32[]{:S(2)}) copy-start(f32[128]{0:T(128)} %param.15) | copy-start | bytes 1540
  55.7 12.3 %copy-start.4 = (f32[128]{0:T(128)S(1)}, f32[128]{0:T(128)}, u32[]{:S(2)}) copy-start(f32[128]{0:T(128)} %param.16) | copy-start | bytes 1540
  55.8 12.3 %copy-start.5 = (f32[128]{0:T(128)S(1)}, f32[128]{0:T(128)}, u32[]{:S(2)}) copy-start(f32[128]{0:T(128)} %param.17) | copy-start | bytes 1540
  55.8 12.3 %copy-start.6 = (f32[128]{0:T(128)S(1)}, f32[128]{0:T(128)}, u32[]{:S(2)}) copy-start(f32[128]{0:T(128)} %param.18) | copy-start | bytes 1540
  56.2 11.8 %collective-permute-start.8 = (s32[512,128]{1,0:T(8,128)S(1)}, s32[512,128]{1,0:T(8,128)S(1)}, u32[]{:S(2)}, u32[]{:S(2)}) collective-permute-start(s32[512,128]{1,0:T(8,128)S(1)} %get-tuple-element.23), channel_id=1, source_target_pairs={{0,192},{1,193},{2,194},{3,195},{4,196},{5,197},{6,198},{7,199},{8... | collective-permute-start | bytes 786440 | tf_op jit(solution)/shard_map/ppermute | solution.py:39
  56.3 11.7 %collective-permute-start.9 = (s32[512,128]{1,0:T(8,128)S(1)}, s32[512,128]{1,0:T(8,128)S(1)}, u32[]{:S(2)}, u32[]{:S(2)}) collective-permute-start(s32[512,128]{1,0:T(8,128)S(1)} %get-tuple-element.24), channel_id=1, source_target_pairs={{0,64},{1,65},{2,66},{3,67},{4,68},{5,69},{6,70},{7,71},{8,72},{9,... | collective-permute-start | bytes 786440 | tf_op jit(solution)/shard_map/ppermute | solution.py:39
  63.0 9.6 %collective-permute-start.12 = (s32[512,128]{1,0:T(8,128)S(1)}, s32[512,128]{1,0:T(8,128)S(1)}, u32[]{:S(2)}, u32[]{:S(2)}) collective-permute-start(s32[512,128]{1,0:T(8,128)S(1)} %get-tuple-element.31), channel_id=1, source_target_pairs={{0,64},{1,65},{2,66},{3,67},{4,68},{5,69},{6,70},{7,71},{8,72},{9,... | collective-permute-start | bytes 786440 | tf_op jit(solution)/shard_map/ppermute | solution.py:39
  63.6 10.0 %collective-permute-start.13 = (s32[512,128]{1,0:T(8,128)S(1)}, s32[512,128]{1,0:T(8,128)S(1)}, u32[]{:S(2)}, u32[]{:S(2)}) collective-permute-start(s32[512,128]{1,0:T(8,128)S(1)} %get-tuple-element.32), channel_id=1, source_target_pairs={{0,192},{1,193},{2,194},{3,195},{4,196},{5,197},{6,198},{7,199},{8... | collective-permute-start | bytes 786440 | tf_op jit(solution)/shard_map/ppermute | solution.py:39
  68.7 21.7 %copy-start.7 = (f32[128]{0:T(128)S(1)}, f32[128]{0:T(128)}, u32[]{:S(2)}) copy-start(f32[128]{0:T(128)} %param.19) | copy-start | bytes 1540
  75.3 15.1 %all-to-all-start.1 = ((f32[64,2,128]{2,1,0:T(2,128)}), f32[64,2,128]{2,1,0:T(2,128)S(1)}, u32[]{:S(2)}, u32[]{:S(2)}) async-start(f32[64,2,128]{2,1,0:T(2,128)} %get-tuple-element.36), calls=%async_computation.1 | async-start | bytes 131072 | tf_op jit(solution)/shard_map/all_to_all | solution.py:57
  91.5 13.8 %all-to-all-start.2 = ((f32[64,1,128]{2,1,0:T(1,128)}), f32[64,1,128]{2,1,0:T(1,128)S(1)}, u32[]{:S(2)}, u32[]{:S(2)}) async-start(f32[64,1,128]{2,1,0:T(1,128)} %get-tuple-element.40), calls=%async_computation.2 | async-start | bytes 65536 | tf_op jit(solution)/shard_map/all_to_all | solution.py:57
